TPU v7x, 32 devices: a whole 2x2x4 slice. The times are simulated.
32 devices in a mesh: lat: 4 (over z), lon: 8 (over y, x, core).
Axes of the slice: x: 2, y: 2, z: 4, core: 2. Of those that a mesh axis runs over, the one named last changes fastest.
Arguments:
- poleward_flow: float32 [10, 4, 256, 1024], P(None, None, 'lat', 'lon'), may hold values from -16 to 16
- potential_warmth: float32 [10, 4, 256, 1024], P(None, None, 'lat', 'lon'), may hold values from -16 to 16
- water_profile_flag: int32 [256, 1024], P('lat', 'lon'), may hold values from 0 to 1
- floor_count: int32 [256, 1024], P('lat', 'lon'), may hold values from 0 to 4, as said below
- catchment_label_for_site: int32 [256, 1024], P('lat', 'lon'), may hold values from 0 to 9
Outputs:
- eddy_temp: float32 [4, 256, 1024], P(None, 'lat', 'lon')
- transport: float32 [4, 10, 4, 256], P(None, None, None, ('lat', 'lon'))
Inputs may be any that keep to these rules, and one draw needn't show every extreme that they name: `floor_count`: land rows of zeros occur at some latitudes; elsewhere columns have 1 to 4 wet levels.
All inputs are finite; a program needn't handle non-finite values.
Results may differ from a plain program's by a relative error of at most 0.0003.
Values sent between devices are 32-bit elements; how exact they have to be, the bound alone decides.
No kernel may reach another device: no remote copies, remote signals or barrier semaphores. Data moves between devices by JAX's collectives and lax.ppermute only.
A program may use at most 64 MiB of HBM per device.

v0:
```python
import math

import jax
import jax.numpy as jnp
from jax import lax
from jax.sharding import PartitionSpec as P

BASINS = 10


highest_accuracy = lax.Precision.HIGHEST


def shifted(block, axis, distance):
    devices = range(lax.axis_size(axis))
    route = [(i - distance, i) for i in devices if i - distance in devices]
    return lax.ppermute(block, axis, route)


def zonal_means(watered_total, along_latitude_totals):
    return along_latitude_totals / jnp.maximum(watered_total, 1.0)


def basin_cells(one_hot, per_basin):
    return jnp.einsum("bji,bkj->kji", one_hot, per_basin, precision=highest_accuracy)


def shards(
    poleward_flow, potential_warmth, water_profile_flag, floor_count, catchment_label_for_site
):
    snapshots, levels, lat_rows, lon_cols = poleward_flow.shape
    lon_devices = lax.axis_size("lon")
    share_rows = lat_rows // lon_devices
    row_start = lax.axis_index("lon") * share_rows
    scaling = 1.0 / math.sqrt(lon_cols * lon_devices)
    bottom_layer_limit = (water_profile_flag * floor_count).astype(jnp.float32)
    poleward_warmth, poleward_floor = shifted(
        (potential_warmth[:, :, 0, :], bottom_layer_limit[0]), "lat", -1
    )
    topmost_warmth = jnp.concatenate(
        [potential_warmth[:, :, 1:, :], poleward_warmth[:, :, None, :]], axis=2
    )
    warmth_entry = 0.5 * (potential_warmth + topmost_warmth)
    upper_depth = jnp.concatenate([bottom_layer_limit[1:], poleward_floor[None]], axis=0)
    level_values = jnp.arange(levels, dtype=jnp.float32)[:, None, None]
    wet_cells = (
        (level_values < bottom_layer_limit[None]) & (level_values < upper_depth[None])
    ).astype(jnp.float32)
    basin_ids = jnp.arange(BASINS, dtype=jnp.int32)
    one_hot = (catchment_label_for_site[None] == basin_ids[:, None, None]).astype(jnp.float32)
    scaling_factors = one_hot[:, None] * wet_cells[None]
    watered_total = jnp.sum(scaling_factors, axis=3)[None]
    along_latitude_flow = jnp.einsum(
        "yalq,falq->fyal", scaling_factors, poleward_flow, precision=highest_accuracy
    )
    along_latitude_warmth = jnp.einsum(
        "yalq,falq->fyal", scaling_factors, warmth_entry, precision=highest_accuracy
    )
    along_latitude_totals = jnp.concatenate([along_latitude_flow, along_latitude_warmth], axis=0)
    mean_velocity = jnp.mean(poleward_flow, axis=0)
    average_warmth = jnp.mean(warmth_entry, axis=0)
    cross_time = jnp.mean((poleward_flow - mean_velocity) * (warmth_entry - average_warmth), axis=0)
    product_sum = jnp.einsum(
        "bkji,kji->bkj", scaling_factors, mean_velocity * average_warmth, precision=highest_accuracy
    )
    cross_sum = jnp.einsum("bkji,kji->bkj", scaling_factors, cross_time, precision=highest_accuracy)
    stats = (watered_total, along_latitude_totals, jnp.stack([product_sum, cross_sum]))
    totals = lax.psum((stats[0], stats[1], stats[2]), "lon")
    own_stats = tuple(
        (lax.dynamic_slice_in_dim(member, row_start, share_rows, 3) for member in totals)
    )
    own_means = zonal_means(own_stats[0], own_stats[1])
    every_means = zonal_means(totals[0], totals[1])
    every_bar_temp = jnp.mean(every_means[snapshots:], axis=0)
    own_count = own_stats[0][0]
    own_bar_v = jnp.mean(own_means[:snapshots], axis=0)
    own_bar_t = jnp.mean(own_means[snapshots:], axis=0)
    mean_flow = scaling * own_count * own_bar_v * own_bar_t
    swing_product = jnp.mean(
        (own_means[:snapshots] - own_bar_v) * (own_means[snapshots:] - own_bar_t), axis=0
    )
    zonal_swing = scaling * own_count * swing_product
    averaged_warmth_grid = basin_cells(one_hot, every_bar_temp)
    temp_star = average_warmth - averaged_warmth_grid
    eddy_temp = wet_cells * temp_star
    steady_share = scaling * (own_stats[2][0] - own_count * own_bar_v * own_bar_t)
    transient = scaling * own_stats[2][1] - zonal_swing
    transport = jnp.stack([mean_flow, steady_share, zonal_swing, transient])
    return (eddy_temp, transport)


def solution(mesh):
    return jax.shard_map(
        shards,
        mesh=mesh,
        in_specs=(
            P(None, None, "lat", "lon"),
            P(None, None, "lat", "lon"),
            P("lat", "lon"),
            P("lat", "lon"),
            P("lat", "lon"),
        ),
        out_specs=(P(None, "lat", "lon"), P(None, None, None, ("lat", "lon"))),
        check_vma=False,
    )
```

profile of v0, /device:TPU:0, one launch (start us, length us, event | category | flops | bytes accessed | tf_op | source)
XLA Modules:
  0.0 108.0 jit_solution(1735994457637224425)
XLA Ops:
  7.2 0.0 copy-start.3
  7.2 0.0 copy-start
  7.2 0.0 all-reduce.3.cloned.1.call-start
  7.2 1.0 slice.32
  8.3 1.3 %collective-permute-start.1 = (f32[10,4,128]{2,1,0:T(4,128)S(1)}, f32[10,4,128]{2,1,0:T(4,128)S(1)}, u32[]{:S(2)}, u32[]{:S(2)}) collective-permute-start(f32[10,4,128]{2,1,0:T(4,128)S(1)} %bitcast.58), channel_id=1, source_target_pairs={{8,0},{16,8},{24,16},{9,1},{17,9},{25,17},{10,2},{18,10},{26,18},{... | collective-permute-start | bytes 61448 | tf_op jit(solution)/shard_map/ppermute | solution.py:17
  9.6 0.8 multiply_convert_fusion
  10.3 1.3 %collective-permute-start = (f32[128]{0:T(128)S(1)}, f32[128]{0:T(128)S(1)}, u32[]{:S(2)}, u32[]{:S(2)}) collective-permute-start(f32[128]{0:T(128)S(1)} %slice_bitcast_fusion), channel_id=1, source_target_pairs={{8,0},{16,8},{24,16},{9,1},{17,9},{25,17},{10,2},{18,10},{26,18},{... | collective-permute-start | bytes 1544 | tf_op jit(solution)/shard_map/ppermute | solution.py:17
  11.6 2.5 %slice.31 = f32[10,4,63,128]{3,2,1,0:T(8,128)} slice(f32[10,4,64,128]{3,2,1,0:T(8,128)} %param.6), slice={[0:10], [0:4], [1:64], [0:128]} | slice | bytes 2580480 | tf_op jit(solution)/shard_map/slice | solution.py:41
  14.2 0.0 copy-done
  14.2 0.7 reduce_sum.77
  15.0 2.5 %collective-permute-done = f32[128]{0:T(128)S(1)} collective-permute-done((f32[128]{0:T(128)S(1)}, f32[128]{0:T(128)S(1)}, u32[]{:S(2)}, u32[]{:S(2)}) %collective-permute-start) | collective-permute-done | bytes 544 | tf_op jit(solution)/shard_map/ppermute | solution.py:17
  17.5 5.4 %fusion.10 = f32[10,10,4,64]{0,1,3,2:T(8,128)} fusion(f32[10,4,64,128]{3,2,1,0:T(8,128)S(1)} %copy-done, f32[4,64,128]{2,1,0:T(8,128)S(1)} %copy.72, f32[10,64,128]{2,0,1:T(8,128)S(1)} %fusion.31), kind=kOutput, calls=%fused_computation.11 | convolution fusion | flops 39649280 | bytes 1871872 | tf_op jit(solution)/shard_map/yalq,falq->fyal/dot_general | solution.py:53
  22.9 1.3 %multiply_reduce_fusion = f32[10,4,64]{0,2,1:T(8,128)} fusion(f32[4,64,128]{2,1,0:T(8,128)S(1)} %copy.72, f32[10,64,128]{2,0,1:T(8,128)S(1)} %fusion.31), kind=kLoop, calls=%fused_computation.4 | loop fusion | flops 652800 | bytes 468992 | tf_op jit(solution)/shard_map/reduce_sum | solution.py:52
  24.2 2.2 %copy.75 = f32[10,10,4,64]{3,2,1,0:T(4,128)S(1)} copy(f32[10,10,4,64]{0,1,3,2:T(8,128)} %fusion.10) | data formatting | bytes 204800 | tf_op jit(solution)/shard_map/yalq,falq->fyal/transpose | solution.py:53
  26.4 0.0 collective-permute-done.1
  26.4 0.6 copy-done.5
  27.0 2.6 %fusion.40 = (f32[4,64,128]{2,1,0:T(8,128)}, f32[10,4,64,128]{3,2,1,0:T(8,128)S(1)}) fusion(f32[10,4,64,128]{3,2,1,0:T(8,128)} %param.6, f32[10,4,1,128]{3,2,1,0:T(1,128)} %bitcast.57, f32[10,4,63,128]{3,2,1,0:T(8,128)} %slice.31), kind=kLoop, calls=%fused_computation.67 | loop fusion | flops 1277952 | bytes 4063232 | tf_op jit(solution)/shard_map/reduce_sum | solution.py:61
  29.6 5.4 %fusion.15 = f32[10,10,4,64]{0,1,3,2:T(8,128)} fusion(f32[10,4,64,128]{3,2,1,0:T(8,128)S(1)} %get-tuple-element.19, f32[4,64,128]{2,1,0:T(8,128)S(1)} %copy.72, f32[10,64,128]{2,0,1:T(8,128)S(1)} %fusion.31), kind=kOutput, calls=%fused_computation.12 | convolution fusion | flops 39649280 | bytes 1871872 | tf_op jit(solution)/shard_map/yalq,falq->fyal/dot_general | solution.py:56
  35.0 2.9 %copy.76 = f32[10,10,4,64]{3,2,1,0:T(4,128)} copy(f32[10,10,4,64]{0,1,3,2:T(8,128)} %fusion.15) | data formatting | bytes 204800 | tf_op jit(solution)/shard_map/yalq,falq->fyal/transpose | solution.py:56
  37.9 1.8 %pad_maximum_fusion = f32[20,10,4,64]{3,2,1,0:T(4,128)} fusion(f32[10,10,4,64]{3,2,1,0:T(4,128)} %copy.76, f32[10,10,4,64]{3,2,1,0:T(4,128)S(1)} %copy.75), kind=kLoop, calls=%fused_computation.29 | loop fusion | flops 51200 | bytes 409600 | tf_op jit(solution)/shard_map/concatenate | solution.py:59
  39.7 0.0 all-reduce.3.cloned.1.call-update
  39.7 1.2 %multiply_bitcast_fusion = (f32[4,64,128,1]{2,0,1,3:T(4,128)S(1)}, f32[4,64,128]{2,0,1:T(4,128)S(1)}, f32[4,64,128]{2,0,1:T(4,128)S(1)}) fusion(f32[4,64,128]{2,1,0:T(8,128)} %reduce_sum.77, f32[4,64,128]{2,1,0:T(8,128)} %get-tuple-element.18), kind=kLoop, calls=%fused_computation.42 | loop fusion | flops 98304 | bytes 655360 | tf_op jit(solution)/shard_map/mul | solution.py:64
  40.9 0.3 multiply_reduce_fusion.1
  41.3 0.0 copy-start.1
  41.3 0.0 copy-start.4
  41.3 0.1 copy.121
  41.4 3.6 %fusion = f32[4,64,1,10]{3,2,1,0:T(1,128)S(1)} fusion(f32[4,64,128]{2,1,0:T(8,128)S(1)} %copy.72, f32[10,64,128]{2,0,1:T(8,128)S(1)} %fusion.31, f32[4,64,128,1]{2,0,1,3:T(4,128)S(1)} %bitcast.54), kind=kOutput, calls=%fused_computation | convolution fusion | flops 4259840 | bytes 600064 | tf_op jit(solution)/shard_map/bkji,kji->bkj/dot_general | solution.py:66
  45.0 0.1 copy.96
  45.1 3.4 %fusion.2 = f32[4,64,1,10]{3,2,1,0:T(1,128)S(1)} fusion(f32[4,64,128]{2,1,0:T(8,128)S(1)} %copy.72, f32[10,64,128]{2,0,1:T(8,128)S(1)} %fusion.31, f32[4,64,128,1]{2,0,1,3:T(4,128)S(1)} %get-tuple-element.22), kind=kOutput, calls=%fused_computation.2 | convolution fusion | flops 4259840 | bytes 600064 | tf_op jit(solution)/shard_map/bkji,kji->bkj/dot_general | solution.py:63
  48.5 0.1 copy.94
  48.6 0.1 copy.88
  48.7 28.2 %all-reduce = (f32[1,10,4,64]{1,3,2,0:T(8,128)S(1)}, f32[2,10,4,64]{1,3,2,0:T(8,128)S(1)}) all-reduce(f32[1,10,4,64]{1,3,2,0:T(8,128)S(1)} %bitcast.53, f32[2,10,4,64]{1,3,2,0:T(8,128)S(1)} %copy.88), channel_id=1, replica_groups=mesh['lat'=4,'lon'=8] {'lon'}, use_global_device_ids=true, to_apply=%region_3.0 | all-reduce | flops 7680 | bytes 61440 | tf_op jit(solution)/shard_map/psum | solution.py:68
  76.9 0.1 copy.77
  77.0 0.1 copy.81
  77.1 19.0 %all-reduce.3.cloned.1.call-done = f32[20,10,4,64]{3,2,1,0:T(4,128)} async-done(((f32[20,10,4,64]{3,2,1,0:T(4,128)}), f32[20,10,4,64]{3,2,1,0:T(4,128)}) %all-reduce.3.cloned.1.call-update) | async-done | bytes 204816 | tf_op jit(solution)/shard_map/psum | solution.py:68
  96.2 1.0 fusion.33
  97.2 0.1 copy.80
  97.3 0.5 fusion.22
  97.8 0.7 copy.92
  98.5 1.3 %dynamic-slice_divide_fusion = f32[20,10,4,8]{3,2,1,0:T(4,128)S(1)} fusion(f32[20,10,4,64]{3,2,1,0:T(4,128)} %all-reduce.3.cloned.1.call-done, s32[]{:T(128)S(6)} %select_n.2, f32[10,4,8]{2,1,0:T(4,128)S(1)} %copy.81), kind=kLoop, calls=%fused_computation.30 | loop fusion | flops 6400 | bytes 52484 | tf_op jit(solution)/shard_map/div | solution.py:21
  99.8 0.1 slice_reduce_fusion.1
  99.8 0.1 copy.83
  99.9 0.1 copy.90
  100.0 0.1 copy.82
  100.2 0.1 copy.89
  100.3 0.1 multiply_reduce_fusion.2
  100.4 0.1 copy.91
  100.5 0.6 pad_maximum_fusion.1
  (22 shorter events, 0.2 us)
Async XLA Ops:
  7.2 7.0 %copy-start.3 = (s32[64,128]{1,0:T(8,128)S(1)}, s32[64,128]{1,0:T(8,128)}, u32[]{:S(2)}) copy-start(s32[64,128]{1,0:T(8,128)} %param.9) | copy-start | bytes 98308
  7.2 7.1 %copy-start = (f32[10,4,64,128]{3,2,1,0:T(8,128)S(1)}, f32[10,4,64,128]{3,2,1,0:T(8,128)}, u32[]{:S(2)}) copy-start(f32[10,4,64,128]{3,2,1,0:T(8,128)} %param.5) | copy-start | bytes 3932164
  7.2 89.0 %all-reduce.3.cloned.1.call-start = ((), (), s32[]{:S(2)}) async-start(), calls=%async_computation | async-start | bytes 819200 | tf_op jit(solution)/shard_map/psum | solution.py:68
  8.3 18.2 %collective-permute-start.1 = (f32[10,4,128]{2,1,0:T(4,128)S(1)}, f32[10,4,128]{2,1,0:T(4,128)S(1)}, u32[]{:S(2)}, u32[]{:S(2)}) collective-permute-start(f32[10,4,128]{2,1,0:T(4,128)S(1)} %bitcast.58), channel_id=1, source_target_pairs={{8,0},{16,8},{24,16},{9,1},{17,9},{25,17},{10,2},{18,10},{26,18},{... | collective-permute-start | bytes 61448 | tf_op jit(solution)/shard_map/ppermute | solution.py:17
  10.3 7.1 %collective-permute-start = (f32[128]{0:T(128)S(1)}, f32[128]{0:T(128)S(1)}, u32[]{:S(2)}, u32[]{:S(2)}) collective-permute-start(f32[128]{0:T(128)S(1)} %slice_bitcast_fusion), channel_id=1, source_target_pairs={{8,0},{16,8},{24,16},{9,1},{17,9},{25,17},{10,2},{18,10},{26,18},{... | collective-permute-start | bytes 1544 | tf_op jit(solution)/shard_map/ppermute | solution.py:17
  26.4 0.6 copy-start.5
  41.2 7.5 %copy-start.2 = (f32[10,4,64]{0,2,1:T(8,128)S(1)}, f32[10,4,64]{0,2,1:T(8,128)}, u32[]{:S(2)}) copy-start(f32[10,4,64]{0,2,1:T(8,128)} %multiply_reduce_fusion) | copy-start | bytes 30724
  41.3 56.1 %copy-start.1 = (f32[4,64,128]{2,1,0:T(8,128)S(1)}, f32[4,64,128]{2,1,0:T(8,128)}, u32[]{:S(2)}) copy-start(f32[4,64,128]{2,1,0:T(8,128)} %get-tuple-element.18) | copy-start | bytes 393220
  41.3 56.1 %copy-start.4 = (s32[64,128]{1,0:T(8,128)S(1)}, s32[64,128]{1,0:T(8,128)}, u32[]{:S(2)}) copy-start(s32[64,128]{1,0:T(8,128)} %param.9) | copy-start | bytes 98308
Sparse Core Ops, SparseCore 0:
  39.8 56.3 all-reduce.2
where the time goes:
time: 108 us
  blocking collectives  28.2 us (26%)
  waiting for transfers between devices  21.5 us (20%)
  matrix products  18.2 us (17%)
  between operations  14.3 us (13%)
  other arithmetic  11.9 us (11%)
  local copies, waits for them, and re-layouts  11.3 us (10%)
  starting transfers between devices  2.62 us (2%)
    psum x1, blocking collectives, shards(): totals = lax.psum((stats[0], stats[1], stats[2]), 'lon')  28.2 us
    psum x1, waiting for transfers between devices, shards(): totals = lax.psum((stats[0], stats[1], stats[2]), 'lon')  19 us
    dot_general x1, matrix products, shards(): jnp.einsum('yalq,falq->fyal', scaling_factors, poleward_flow, precision=h...  5.38 us
    dot_general x1, matrix products, shards(): jnp.einsum('yalq,falq->fyal', scaling_factors, warmth_entry, precision=hi...  5.37 us
    dot_general x1, matrix products, shards(): jnp.einsum('bkji,kji->bkj', scaling_factors, cross_time, precision=highes...  3.56 us
    dot_general x1, matrix products, shards(): jnp.einsum('bkji,kji->bkj', scaling_factors, mean_velocity * average_warm...  3.4 us
    transpose x1, local copies, waits for them, and re-layouts, shards(): jnp.einsum('yalq,falq->fyal', scaling_factors, warmth_entry, precision=hi...  2.91 us
    reduce_sum x1, other arithmetic, shards(): average_warmth = jnp.mean(warmth_entry, axis=0)  2.58 us
  transfers between devices with their start and end apart: 3, of which 2 were waited for; matrix products, arithmetic and copies ran while one was open for 21% of the time, Pallas kernels for 0%

commit v1 on v0

v1 whole, which is shorter than its diff:
```python
import functools
import math

import jax
import jax.numpy as jnp
from jax import lax
from jax.experimental import pallas as pl
from jax.experimental.pallas import tpu as pltpu
from jax.sharding import PartitionSpec as P

BASINS = 10
SUB = 8
LANES = 128


def cover(total, unit):
    return -(-total // unit)


def iota(axis):
    return lax.broadcasted_iota(jnp.int32, (SUB, LANES), axis)


def pick_lanes(tiles, start, width):
    first, shift = divmod(start, LANES)
    if shift == 0:
        return tiles[first]
    left = pltpu.roll(tiles[first], LANES - shift, 1)
    if shift + width <= LANES:
        return left
    right = pltpu.roll(tiles[first + 1], LANES - shift, 1)
    return jnp.where(lax.broadcasted_iota(jnp.int32, left.shape, 1) < LANES - shift, left, right)


def place_lanes(blocks, width, count):
    tiles = [None] * count
    lane = lax.broadcasted_iota(jnp.int32, blocks[0].shape, 1)
    for k, block in enumerate(blocks):
        first, shift = divmod(k * width, LANES)
        moved = block if shift == 0 else pltpu.roll(block, shift, 1)
        if tiles[first] is None:
            tiles[first] = moved
        else:
            tiles[first] = jnp.where(lane < shift, tiles[first], moved)
        if shift + width > LANES:
            tiles[first + 1] = moved
    return tiles


def sums_kernel(
    dims, flow, warmth, flag, floor, basin, halo, out, mean_warmth, limit,
    flow_buf, warmth_buf, depth_buf, flow_sem, warmth_sem,
):
    snapshots, levels, rows, blocks, tiles, dests, per_dest = dims
    width = BASINS * SUB
    quantities = 2 * snapshots + 4
    own_rows = tiles * quantities

    def flow_copy(n):
        at = pl.ds(pl.multiple_of(n * SUB, SUB), SUB)
        return pltpu.make_async_copy(flow.at[:, :, at, :], flow_buf.at[:, :, at, :], flow_sem.at[n])

    def warmth_copy(n):
        at = pl.ds(pl.multiple_of(n * SUB, SUB), SUB)
        return pltpu.make_async_copy(
            warmth.at[:, :, at, :], warmth_buf.at[:, :, at, :], warmth_sem.at[n]
        )

    for n in range(blocks):
        warmth_copy(n).start()
        flow_copy(n).start()
    for t in range(snapshots):
        for k in range(levels):
            n = t * levels + k
            warmth_buf[t, k, rows : rows + 1, :] = halo[n : n + 1, :]
    depth_buf[0:rows, :] = (flag[...] * floor[...]).astype(jnp.float32)
    depth_buf[rows : rows + 1, :] = halo[snapshots * levels : snapshots * levels + 1, :]
    warmth_copy(0).wait()

    sub, lane = iota(0), iota(1)
    diagonal = lane % SUB

    def one_block(n, last):
        at = pl.multiple_of(n * SUB, SUB)
        if not last:
            warmth_copy(n + 1).wait()
        flow_copy(n).wait()
        shallow = jnp.minimum(depth_buf[pl.ds(at, SUB), :], depth_buf[pl.ds(at + 1, SUB), :])
        limit[pl.ds(at, SUB), :] = shallow
        label = basin[pl.ds(at, SUB), :]
        placed = []
        for k in range(levels):
            v = [flow_buf[t, k, pl.ds(at, SUB), :] for t in range(snapshots)]
            w = [
                0.5 * (warmth_buf[t, k, pl.ds(at, SUB), :] + warmth_buf[t, k, pl.ds(at + 1, SUB), :])
                for t in range(snapshots)
            ]
            mv = sum(v[1:], v[0]) * (1.0 / snapshots)
            mw = sum(w[1:], w[0]) * (1.0 / snapshots)
            cross = sum((a - mv) * (b - mw) for a, b in zip(v, w)) * (1.0 / snapshots)
            mean_warmth[k, pl.ds(at, SUB), :] = mw
            data = jnp.concatenate(v + w + [mv * mw, cross, mw, jnp.ones_like(mw)], axis=0)
            masked = jnp.where(shallow > float(k), label, -1)
            hot = jnp.concatenate(
                [jnp.where(masked == b, 1.0, 0.0) for b in range(BASINS)], axis=0
            ).astype(jnp.bfloat16)
            total = None
            rest = data
            for piece in range(3):
                part = rest.astype(jnp.bfloat16)
                if piece < 2:
                    rest = rest - part.astype(jnp.float32)
                dot = lax.dot_general(
                    part, hot, (((1,), (1,)), ((), ())), preferred_element_type=jnp.float32
                )
                total = dot if total is None else total + dot
            total = jnp.concatenate(
                [total, jnp.zeros((total.shape[0], LANES - width), jnp.float32)], axis=1
            )
            groups = []
            for g in range(quantities // SUB):
                acc = None
                for s in range(SUB):
                    q = g * SUB + s
                    row = jnp.take_along_axis(
                        total[q * SUB : (q + 1) * SUB], diagonal, axis=0, mode="promise_in_bounds"
                    )
                    acc = row if acc is None else jnp.where(sub == s, row, acc)
                groups.append(acc)
            placed.append(jnp.concatenate(groups, axis=0))
        done = place_lanes(placed, width, tiles)
        dest, inner = (n // per_dest, n % per_dest) if per_dest > 1 else (n, 0)
        for c in range(tiles):
            base = inner * own_rows + c * quantities
            out[dest, pl.ds(pl.multiple_of(base, SUB), quantities), :] = done[c]
            for q in range(2):
                row = per_dest * own_rows + (c * 2 + q) * blocks + n
                out[0, pl.ds(row, 1), :] = done[c][quantities - 2 + q : quantities - 1 + q]

    def body(n, carry):
        one_block(n, False)
        return carry

    lax.fori_loop(0, blocks - 1, body, 0)
    one_block(blocks - 1, True)
    for d in range(1, dests):
        out[d, per_dest * own_rows :, :] = out[0, per_dest * own_rows :, :]


def finish_kernel(dims, scaling, got, mean_warmth, limit, basin, eddy, transport):
    snapshots, levels, rows, blocks, tiles, dests, per_dest = dims
    width = BASINS * SUB
    quantities = 2 * snapshots + 4
    own_rows = tiles * quantities
    sub, lane = iota(0), iota(1)
    mine = got[0]
    for d in range(1, got.shape[0]):
        mine = mine + got[d]
    shared = mine[per_dest * own_rows :]
    bar = []
    for c in range(tiles):
        at = c * 2 * blocks
        bar.append(shared[at : at + blocks] / jnp.maximum(shared[at + blocks : at + 2 * blocks], 1.0))
    for k in range(levels):
        level = pick_lanes(bar, k * width, width)
        for n in range(blocks):
            where = basin[n * SUB : (n + 1) * SUB, :] * SUB + sub
            row = jnp.broadcast_to(level[n : n + 1], (SUB, LANES))
            cell = jnp.take_along_axis(row, where, axis=1, mode="promise_in_bounds")
            deep = limit[n * SUB : (n + 1) * SUB, :] > float(k)
            star = mean_warmth[k, n * SUB : (n + 1) * SUB, :] - cell
            eddy[k, n * SUB : (n + 1) * SUB, :] = jnp.where(deep, star, 0.0)
    spread = jnp.minimum(lane, BASINS - 1) * SUB + sub
    for i in range(per_dest):
        terms = []
        for c in range(tiles):
            own = mine[i * own_rows + c * quantities : i * own_rows + (c + 1) * quantities]
            count = own[quantities - 1 : quantities]
            floor = jnp.maximum(count, 1.0)
            v = own[:snapshots] / floor
            w = own[snapshots : 2 * snapshots] / floor
            bar_v = jnp.sum(v, axis=0, keepdims=True) * (1.0 / snapshots)
            bar_w = jnp.sum(w, axis=0, keepdims=True) * (1.0 / snapshots)
            swing = jnp.sum((v - bar_v) * (w - bar_w), axis=0, keepdims=True) * (1.0 / snapshots)
            mean_part = count * bar_v * bar_w
            swing = count * swing
            product = own[2 * snapshots : 2 * snapshots + 1]
            cross = own[2 * snapshots + 1 : 2 * snapshots + 2]
            four = [mean_part, product - mean_part, swing, cross - swing]
            terms.append(scaling * jnp.concatenate(four + four, axis=0))
        for k in range(levels):
            level = pick_lanes(terms, k * width, width)
            for term in range(4):
                row = jnp.broadcast_to(level[term : term + 1], (SUB, LANES))
                cell = jnp.take_along_axis(row, spread, axis=1, mode="promise_in_bounds")
                transport[term, k, i * SUB : (i + 1) * SUB, :] = cell[:, :BASINS]


def shards(flow, warmth, flag, floor, basin):
    snapshots, levels, rows, cols = flow.shape
    lon, lat = lax.axis_size("lon"), lax.axis_size("lat")
    scaling = 1.0 / math.sqrt(cols * lon)
    share = rows // lon
    blocks = rows // SUB
    per_dest = max(1, share // SUB)
    dests = blocks // per_dest
    width = BASINS * SUB
    tiles = cover(levels * width, LANES)
    quantities = 2 * snapshots + 4
    dims = (snapshots, levels, rows, blocks, tiles, dests, per_dest)
    chunk = per_dest * tiles * quantities + tiles * 2 * blocks

    edge = jnp.concatenate(
        [
            warmth[:, :, 0, :].reshape(snapshots * levels, cols),
            (flag[:1] * floor[:1]).astype(jnp.float32),
        ],
        axis=0,
    )
    halo = lax.ppermute(edge, "lat", [(i, i - 1) for i in range(1, lat)])

    vmem = pl.BlockSpec(memory_space=pltpu.VMEM)
    hbm = pl.BlockSpec(memory_space=pl.ANY)
    sent, mean_warmth, limit = pl.pallas_call(
        functools.partial(sums_kernel, dims),
        out_shape=(
            jax.ShapeDtypeStruct((dests, chunk, LANES), jnp.float32),
            jax.ShapeDtypeStruct((levels, rows, cols), jnp.float32),
            jax.ShapeDtypeStruct((rows, cols), jnp.float32),
        ),
        in_specs=[hbm, hbm, vmem, vmem, vmem, vmem],
        out_specs=(vmem, vmem, vmem),
        scratch_shapes=[
            pltpu.VMEM((snapshots, levels, rows, cols), jnp.float32),
            pltpu.VMEM((snapshots, levels, rows + SUB, cols), jnp.float32),
            pltpu.VMEM((rows + SUB, cols), jnp.float32),
            pltpu.SemaphoreType.DMA((blocks,)),
            pltpu.SemaphoreType.DMA((blocks,)),
        ],
        name="basin_sums",
    )(flow, warmth, flag, floor, basin, halo)

    if dests != lon:
        sent = jnp.repeat(sent, lon // dests, axis=0, total_repeat_length=lon)
    got = lax.all_to_all(sent, "lon", 0, 0)

    eddy, transport = pl.pallas_call(
        functools.partial(finish_kernel, dims, scaling),
        out_shape=(
            jax.ShapeDtypeStruct((levels, rows, cols), jnp.float32),
            jax.ShapeDtypeStruct((4, levels, per_dest * SUB, BASINS), jnp.float32),
        ),
        in_specs=[vmem, vmem, vmem, vmem],
        out_specs=(vmem, vmem),
        name="finish",
    )(got, mean_warmth, limit, basin)
    if dests != lon:
        first = lax.axis_index("lon") * share % SUB
        transport = lax.dynamic_slice_in_dim(transport, first, share, 2)
    return eddy, jnp.transpose(transport, (0, 3, 1, 2))


def solution(mesh):
    return jax.shard_map(
        shards,
        mesh=mesh,
        in_specs=(
            P(None, None, "lat", "lon"),
            P(None, None, "lat", "lon"),
            P("lat", "lon"),
            P("lat", "lon"),
            P("lat", "lon"),
        ),
        out_specs=(P(None, "lat", "lon"), P(None, None, None, ("lat", "lon"))),
        check_vma=False,
    )
```

time: 108 us -> 31.9 us (0.30)
  matrix products: 18.2 us -> 0 us
  waiting for transfers between devices: 21.5 us -> 5.46 us
  blocking collectives: 28.2 us -> 13.6 us
  between operations: 14.3 us -> 0.65 us
  other arithmetic: 11.9 us -> 0.72 us
  local copies, waits for them, and re-layouts: 11.3 us -> 1.54 us
  Pallas kernels: 0 us -> 8.19 us
  starting transfers between devices: 2.62 us -> 1.28 us
    psum x1 -> x0, blocking collectives: 28.2 us -> none  [shards(): totals = lax.psum((stats[0], stats[1], stats[2]), 'lon')]
    psum x1 -> x0, waiting for transfers between devices: 19 us -> none  [shards(): totals = lax.psum((stats[0], stats[1], stats[2]), 'lon')]
    dot_general x5 -> x0, matrix products: 18.2 us -> none  [the longest x1 5.38 us: shards(): jnp.einsum('yalq,falq->fyal', scaling_factors, poleward_flow, precision=h...]
    all_to_all x0 -> x1, blocking collectives: none -> 13.6 us  [shards(): got = lax.all_to_all(sent, 'lon', 0, 0)]
    pallas_call x0 -> x2, Pallas kernels: none -> 8.19 us  [the longest x1 6.2 us: shards(): pl.pallas_call(functools.partial(sums_kernel, dims), out_shape=(jax.Shape...]
    reduce_sum x7 -> x0, other arithmetic: 6.06 us -> none  [the longest x1 2.58 us: shards(): average_warmth = jnp.mean(warmth_entry, axis=0)]
    transpose x2 -> x0, local copies, waits for them, and re-layouts: 5.15 us -> none  [the longest x1 2.91 us: shards(): jnp.einsum('yalq,falq->fyal', scaling_factors, warmth_entry, precision=hi...]
    ppermute x2 -> x1, waiting for transfers between devices: 2.49 us -> 5.46 us  [shards(): halo = lax.ppermute(edge, 'lat', [(i, i - 1) for i in range(1, lat)])]
  transfers between devices with their start and end apart: 3 -> 1, of which waited for: 2 -> 1; matrix products, arithmetic and copies ran while one was open for 21% -> 0% of each run, Pallas kernels for 0% -> 0%
where the time goes in v1:
time: 31.9 us; the launch traced here: 31.5 us
  blocking collectives  13.6 us (43%)
  Pallas kernels  8.19 us (26%)
  waiting for transfers between devices  5.46 us (17%)
  local copies, waits for them, and re-layouts  1.54 us (5%)
  starting transfers between devices  1.28 us (4%)
  other arithmetic  0.72 us (2%)
  between operations  0.65 us (2%)
    all_to_all x1, blocking collectives, shards(): got = lax.all_to_all(sent, 'lon', 0, 0)  13.6 us
    pallas_call x1, Pallas kernels, shards(): pl.pallas_call(functools.partial(sums_kernel, dims), out_shape=(jax.Shape...  6.2 us
    ppermute x1, waiting for transfers between devices, shards(): halo = lax.ppermute(edge, 'lat', [(i, i - 1) for i in range(1, lat)])  5.46 us
    pallas_call x1, Pallas kernels, shards(): pl.pallas_call(functools.partial(finish_kernel, dims, scaling), out_shape...  2 us
    ppermute x1, starting transfers between devices, shards(): halo = lax.ppermute(edge, 'lat', [(i, i - 1) for i in range(1, lat)])  1.28 us
    slice x1, local copies, waits for them, and re-layouts, shards(): warmth[:, :, 0, :].reshape(snapshots * levels, cols)  0.93 us
    convert_element_type x1, other arithmetic, shards(): (flag[:1] * floor[:1]).astype(jnp.float32)  0.71 us
  transfers between devices with their start and end apart: 1, of which 1 were waited for; matrix products, arithmetic and copies ran while one was open for 0% of the time, Pallas kernels for 0%

profile of v1, /device:TPU:0, one launch (start us, length us, event | category | flops | bytes accessed | tf_op | source)
XLA Modules:
  0.0 31.5 jit_solution(4249815374889305142)
XLA Ops:
  0.6 0.9 %slice.9 = f32[10,4,1,128]{3,2,1,0:T(1,128)S(1)} slice(f32[10,4,64,128]{3,2,1,0:T(8,128)} %warmth.1), slice={[0:10], [0:4], [0:1], [0:128]} | slice | bytes 40960 | tf_op jit(solution)/shard_map/slice | solution.py:215
  1.6 0.7 %multiply_convert_fusion = f32[1,128]{1,0:T(1,128)S(1)} fusion(s32[64,128]{1,0:T(8,128)} %floor.1, s32[64,128]{1,0:T(8,128)} %flag.1), kind=kLoop, calls=%fused_computation.1 | loop fusion | flops 256 | bytes 1536 | tf_op jit(solution)/shard_map/convert_element_type | solution.py:216
  2.3 1.3 %collective-permute-start = (f32[41,128]{1,0:T(8,128)S(1)}, f32[41,128]{1,0:T(8,128)S(1)}, u32[]{:S(2)}, u32[]{:S(2)}) collective-permute-start(f32[41,128]{1,0:T(8,128)S(1)} %pad_maximum_fusion), channel_id=1, source_target_pairs={{8,0},{16,8},{24,16},{9,1},{17,9},{25,17},{10,2},{18,10},{26,18},{... | collective-permute-start | bytes 62984 | tf_op jit(solution)/shard_map/ppermute | solution.py:220
  3.6 5.5 %collective-permute-done.halo = f32[41,128]{1,0:T(8,128)S(1)} collective-permute-done((f32[41,128]{1,0:T(8,128)S(1)}, f32[41,128]{1,0:T(8,128)S(1)}, u32[]{:S(2)}, u32[]{:S(2)}) %collective-permute-start) | collective-permute-done | bytes 21024 | tf_op jit(solution)/shard_map/ppermute | solution.py:220
  9.0 0.0 copy-start
  9.0 0.6 %copy-done = f32[41,128]{1,0:T(8,128)} copy-done((f32[41,128]{1,0:T(8,128)}, f32[41,128]{1,0:T(8,128)S(1)}, u32[]{:S(2)}) %copy-start) | copy-done | bytes 21016
  9.6 6.2 %basin_sums.1 = (f32[8,120,128]{2,1,0:T(8,128)}, f32[4,64,128]{2,1,0:T(8,128)}, f32[64,128]{1,0:T(8,128)}) custom-call(f32[10,4,64,128]{3,2,1,0:T(8,128)} %flow.1, f32[10,4,64,128]{3,2,1,0:T(8,128)} %warmth.1, s32[64,128]{1,0:T(8,128)} %flag.1, s32[64,128]{1,0:T(8,128)} %floor.1, s32[64,128]{1,0:T(8,128)} %basin.3, f32[41,128]{1,0:T(8,128)} %copy-done), custom_call_target="tpu_custom_call" | custom-call | tf_op jit(solution)/shard_map/basin_sums/pallas_call | solution.py:224
  15.8 13.6 %all_to_all.5.got = f32[8,120,128]{2,1,0:T(8,128)} all-to-all(f32[8,120,128]{2,1,0:T(8,128)} %get-tuple-element.7), channel_id=1, replica_groups=mesh['lat'=4,'lon'=8] {'lon'}, dimensions={0} | all-to-all | bytes 983040 | tf_op jit(solution)/shard_map/all_to_all | solution.py:245
  29.5 2.0 %finish.1 = (f32[4,64,128]{2,1,0:T(8,128)}, f32[4,4,8,10]{3,2,1,0:T(8,128)}) custom-call(f32[8,120,128]{2,1,0:T(8,128)} %all_to_all.5.got, f32[4,64,128]{2,1,0:T(8,128)} %get-tuple-element.8.mean_warmth, f32[64,128]{1,0:T(8,128)} %get-tuple-element.9.limit, s32[64,128]{1,0:T(8,128)} %basin.3), custom_call_target="tpu_custom_call" | custom-call | tf_op jit(solution)/shard_map/finish/pallas_call | solution.py:247
  (1 shorter events, 0.0 us)
Async XLA Ops:
  2.3 6.7 %collective-permute-start = (f32[41,128]{1,0:T(8,128)S(1)}, f32[41,128]{1,0:T(8,128)S(1)}, u32[]{:S(2)}, u32[]{:S(2)}) collective-permute-start(f32[41,128]{1,0:T(8,128)S(1)} %pad_maximum_fusion), channel_id=1, source_target_pairs={{8,0},{16,8},{24,16},{9,1},{17,9},{25,17},{10,2},{18,10},{26,18},{... | collective-permute-start | bytes 62984 | tf_op jit(solution)/shard_map/ppermute | solution.py:220
  9.0 0.6 %copy-start = (f32[41,128]{1,0:T(8,128)}, f32[41,128]{1,0:T(8,128)S(1)}, u32[]{:S(2)}) copy-start(f32[41,128]{1,0:T(8,128)S(1)} %collective-permute-done.halo) | copy-start | bytes 62980

commit v2 on v1

v2 whole, which is shorter than its diff:
```python
import functools
import math

import jax
import jax.numpy as jnp
from jax import lax
from jax.experimental import pallas as pl
from jax.experimental.pallas import tpu as pltpu
from jax.sharding import PartitionSpec as P

BASINS = 10
SUB = 8
LANES = 128
GRANT = 16 * 1024 * 1024


def cover(total, unit):
    return -(-total // unit)


def iota(axis):
    return lax.broadcasted_iota(jnp.int32, (SUB, LANES), axis)


def pick_lanes(tiles, start, width):
    first, shift = divmod(start, LANES)
    if shift == 0:
        return tiles[first]
    left = pltpu.roll(tiles[first], LANES - shift, 1)
    if shift + width <= LANES:
        return left
    right = pltpu.roll(tiles[first + 1], LANES - shift, 1)
    return jnp.where(lax.broadcasted_iota(jnp.int32, left.shape, 1) < LANES - shift, left, right)


def place_lanes(blocks, width, count):
    tiles = [None] * count
    lane = lax.broadcasted_iota(jnp.int32, blocks[0].shape, 1)
    for k, block in enumerate(blocks):
        first, shift = divmod(k * width, LANES)
        moved = block if shift == 0 else pltpu.roll(block, shift, 1)
        if tiles[first] is None:
            tiles[first] = moved
        else:
            tiles[first] = jnp.where(lane < shift, tiles[first], moved)
        if shift + width > LANES:
            tiles[first + 1] = moved
    return tiles


def edge_kernel(dims, warmth, flag, floor, edge, rows_buf, flag_buf, floor_buf, sem):
    snapshots, levels = dims[:2]
    first = slice(0, SUB)
    copies = [
        pltpu.make_async_copy(flag.at[first, :], flag_buf, sem.at[snapshots]),
        pltpu.make_async_copy(floor.at[first, :], floor_buf, sem.at[snapshots + 1]),
    ] + [
        pltpu.make_async_copy(warmth.at[t, :, first, :], rows_buf.at[t], sem.at[t])
        for t in range(snapshots)
    ]
    for copy in copies:
        copy.start()
    for copy in copies:
        copy.wait()
    depth = (flag_buf[0:1, :] * floor_buf[0:1, :]).astype(jnp.float32)
    edge[snapshots * levels : snapshots * levels + 1, :] = depth
    for t in range(snapshots):
        for k in range(levels):
            edge[t * levels + k : t * levels + k + 1, :] = rows_buf[t, k, 0:1, :]


def block_sums(dims, n, get_v, get_w, shallow, label, put_own, put_shared, put_mean):
    snapshots, levels, rows, blocks, tiles, dests, per_dest = dims
    width = BASINS * SUB
    quantities = 2 * snapshots + 4
    own_rows = tiles * quantities
    sub, lane = iota(0), iota(1)
    diagonal = lane % SUB
    placed = []
    for k in range(levels):
        v = [get_v(t, k) for t in range(snapshots)]
        w = [get_w(t, k) for t in range(snapshots)]
        mv = sum(v[1:], v[0]) * (1.0 / snapshots)
        mw = sum(w[1:], w[0]) * (1.0 / snapshots)
        cross = sum((a - mv) * (b - mw) for a, b in zip(v, w)) * (1.0 / snapshots)
        put_mean(k, mw)
        data = jnp.concatenate(v + w + [mv * mw, cross, mw, jnp.ones_like(mw)], axis=0)
        masked = jnp.where(shallow > float(k), label, -1)
        hot = jnp.concatenate(
            [jnp.where(masked == b, 1.0, 0.0) for b in range(BASINS)], axis=0
        ).astype(jnp.bfloat16)
        total = None
        rest = data
        for piece in range(3):
            part = rest.astype(jnp.bfloat16)
            if piece < 2:
                rest = rest - part.astype(jnp.float32)
            dot = lax.dot_general(
                part, hot, (((1,), (1,)), ((), ())), preferred_element_type=jnp.float32
            )
            total = dot if total is None else total + dot
        total = jnp.concatenate(
            [total, jnp.zeros((total.shape[0], LANES - width), jnp.float32)], axis=1
        )
        groups = []
        for g in range(quantities // SUB):
            acc = None
            for s in range(SUB):
                q = g * SUB + s
                row = jnp.take_along_axis(
                    total[q * SUB : (q + 1) * SUB], diagonal, axis=0, mode="promise_in_bounds"
                )
                acc = row if acc is None else jnp.where(sub == s, row, acc)
            groups.append(acc)
        placed.append(jnp.concatenate(groups, axis=0))
    done = place_lanes(placed, width, tiles)
    for c in range(tiles):
        put_own(c, done[c])
        for q in range(2):
            put_shared(c * 2 + q, done[c][quantities - 2 + q : quantities - 1 + q])


def writers(dims, n, keep, give):
    snapshots, levels, rows, blocks, tiles, dests, per_dest = dims
    quantities = 2 * snapshots + 4
    own_rows = tiles * quantities
    dest, inner = (n // per_dest, n % per_dest) if per_dest > 1 else (n, 0)
    halves = (keep,) if give is None else (keep, give)
    half = dest if give is None else dest // 2
    shared_at = keep.shape[0] - 2 * tiles * blocks

    def put_own(c, value):
        base = (half * per_dest + inner) * own_rows + c * quantities
        if not isinstance(base, int):
            base = pl.multiple_of(base, SUB)
        at = pl.ds(base, quantities)
        if give is None:
            keep[at, :] = value
            return
        mine = lax.axis_index("lon") % 2 == dest % 2

        @pl.when(mine)
        def _():
            keep[at, :] = value

        @pl.when(jnp.logical_not(mine))
        def _():
            give[at, :] = value

    def put_shared(place, value):
        for ref in halves:
            ref[pl.ds(shared_at + place * blocks + n, 1), :] = value

    return put_own, put_shared


def inner_kernel(dims, pairs, flow, warmth, flag, floor, basin, *outs):
    rows, blocks = dims[2:4]
    keep, give = outs[:2] if pairs else (outs[0], None)
    mean_warmth, limit, depth_buf = outs[-3:]
    depth_buf[...] = (flag[...] * floor[...]).astype(jnp.float32)

    def body(n, carry):
        at = pl.multiple_of(n * SUB, SUB)
        here, north = pl.ds(at, SUB), pl.ds(at + 1, SUB)
        shallow = jnp.minimum(depth_buf[here, :], depth_buf[north, :])
        limit[here, :] = shallow

        def put_mean(k, value):
            mean_warmth[k, here, :] = value

        def get_v(t, k):
            return flow[t, k, here, :]

        def get_w(t, k):
            return 0.5 * (warmth[t, k, here, :] + warmth[t, k, north, :])

        put_own, put_shared = writers(dims, n, keep, give)
        block_sums(
            dims, n, get_v, get_w, shallow, basin[here, :], put_own, put_shared, put_mean
        )
        return carry

    lax.fori_loop(0, blocks - 1, body, 0)


def last_kernel(dims, pairs, halo, flow, warmth, flag, floor, basin, *refs):
    snapshots, levels, rows, blocks = dims[:4]
    outs = refs[len(refs) // 2 :]
    keep, give = outs[:2] if pairs else (outs[0], None)
    mean_warmth, limit = outs[-2:]
    here = slice(rows - SUB, rows)
    below = lax.broadcasted_iota(jnp.int32, (SUB, LANES), 0) < SUB - 1

    def north(block, edge_row):
        return jnp.where(below, pltpu.roll(block, SUB - 1, 0), edge_row)

    depth = (flag[here, :] * floor[here, :]).astype(jnp.float32)
    edge_at = snapshots * levels
    shallow = jnp.minimum(depth, north(depth, halo[edge_at : edge_at + 1, :]))
    limit[here, :] = shallow

    def put_mean(k, value):
        mean_warmth[k, here, :] = value

    def get_v(t, k):
        return flow[t, k, here, :]

    def get_w(t, k):
        block = warmth[t, k, here, :]
        n = t * levels + k
        return 0.5 * (block + north(block, halo[n : n + 1, :]))

    put_own, put_shared = writers(dims, blocks - 1, keep, give)
    block_sums(
        dims, blocks - 1, get_v, get_w, shallow, basin[here, :], put_own, put_shared, put_mean
    )


def pair_kernel(dims, keep, came, *outs):
    tiles, per_dest = dims[4], dims[6]
    own_rows = per_dest * tiles * (2 * dims[0] + 4)
    chips = len(outs)
    shared = chips * own_rows
    chip = lax.axis_index("lon") // 2
    for offset, out in enumerate(outs):
        at = pl.multiple_of((chip ^ offset) * own_rows, SUB)
        out[0:own_rows, :] = keep[pl.ds(at, own_rows), :] + came[pl.ds(at, own_rows), :]
        out[own_rows:, :] = keep[shared:, :] + came[shared:, :]


def finish_kernel(dims, scaling, *refs):
    mean_warmth, limit, basin, eddy, transport = refs[-5:]
    snapshots, levels, rows, blocks, tiles, dests, per_dest = dims
    width = BASINS * SUB
    quantities = 2 * snapshots + 4
    own_rows = tiles * quantities
    sub, lane = iota(0), iota(1)
    got = refs[:-5]
    if len(got) == 1:
        got = [got[0].at[d] for d in range(got[0].shape[0])]
    mine = got[0][...]
    for part in got[1:]:
        mine = mine + part[...]
    shared = mine[per_dest * own_rows :]
    bar = []
    for c in range(tiles):
        at = c * 2 * blocks
        bar.append(shared[at : at + blocks] / jnp.maximum(shared[at + blocks : at + 2 * blocks], 1.0))
    for k in range(levels):
        level = pick_lanes(bar, k * width, width)
        for n in range(blocks):
            where = basin[n * SUB : (n + 1) * SUB, :] * SUB + sub
            row = jnp.broadcast_to(level[n : n + 1], (SUB, LANES))
            cell = jnp.take_along_axis(row, where, axis=1, mode="promise_in_bounds")
            deep = limit[n * SUB : (n + 1) * SUB, :] > float(k)
            star = mean_warmth[k, n * SUB : (n + 1) * SUB, :] - cell
            eddy[k, n * SUB : (n + 1) * SUB, :] = jnp.where(deep, star, 0.0)
    spread = jnp.minimum(lane, BASINS - 1) * SUB + sub
    for i in range(per_dest):
        terms = []
        for c in range(tiles):
            own = mine[i * own_rows + c * quantities : i * own_rows + (c + 1) * quantities]
            count = own[quantities - 1 : quantities]
            floor = jnp.maximum(count, 1.0)
            v = own[:snapshots] / floor
            w = own[snapshots : 2 * snapshots] / floor
            bar_v = jnp.sum(v, axis=0, keepdims=True) * (1.0 / snapshots)
            bar_w = jnp.sum(w, axis=0, keepdims=True) * (1.0 / snapshots)
            swing = jnp.sum((v - bar_v) * (w - bar_w), axis=0, keepdims=True) * (1.0 / snapshots)
            mean_part = count * bar_v * bar_w
            swing = count * swing
            product = own[2 * snapshots : 2 * snapshots + 1]
            cross = own[2 * snapshots + 1 : 2 * snapshots + 2]
            four = [mean_part, product - mean_part, swing, cross - swing]
            terms.append(scaling * jnp.concatenate(four + four, axis=0))
        for k in range(levels):
            level = pick_lanes(terms, k * width, width)
            for term in range(4):
                row = jnp.broadcast_to(level[term : term + 1], (SUB, LANES))
                cell = jnp.take_along_axis(row, spread, axis=1, mode="promise_in_bounds")
                transport[term, k, i * SUB : (i + 1) * SUB, :] = cell[:, :BASINS]


def shards(flow, warmth, flag, floor, basin):
    snapshots, levels, rows, cols = flow.shape
    lon, lat = lax.axis_size("lon"), lax.axis_size("lat")
    scaling = 1.0 / math.sqrt(cols * lon)
    share = rows // lon
    blocks = rows // SUB
    per_dest = max(1, share // SUB)
    dests = blocks // per_dest
    width = BASINS * SUB
    tiles = cover(levels * width, LANES)
    quantities = 2 * snapshots + 4
    dims = (snapshots, levels, rows, blocks, tiles, dests, per_dest)
    own_rows, shared_rows = per_dest * tiles * quantities, tiles * 2 * blocks
    pairs = dests == lon and lon in (2, 4, 8)

    vmem = pl.BlockSpec(memory_space=pltpu.VMEM)
    hbm = pl.BlockSpec(memory_space=pl.ANY)
    params = pltpu.CompilerParams(vmem_limit_bytes=GRANT)

    def near(x):
        return pltpu.with_memory_space_constraint(x, pltpu.VMEM)

    def far(x):
        return pltpu.with_memory_space_constraint(x, pltpu.HBM)

    edge = pl.pallas_call(
        functools.partial(edge_kernel, dims),
        out_shape=pltpu.VMEM((snapshots * levels + 1, cols), jnp.float32),
        in_specs=[hbm] * 3,
        out_specs=vmem,
        scratch_shapes=[
            pltpu.VMEM((snapshots, levels, SUB, cols), jnp.float32),
            pltpu.VMEM((SUB, cols), jnp.int32),
            pltpu.VMEM((SUB, cols), jnp.int32),
            pltpu.SemaphoreType.DMA((snapshots + 2,)),
        ],
        compiler_params=params,
        cost_estimate=pl.CostEstimate(flops=10000000000, bytes_accessed=8 << 20, transcendentals=0),
        name="edge",
    )(far(warmth), far(flag), far(floor))
    halo = lax.ppermute(edge, "lat", [(i, i - 1) for i in range(1, lat)])

    flow, warmth, flag, floor, basin = (near(x) for x in (flow, warmth, flag, floor, basin))
    half = pltpu.VMEM((dests // 2 * own_rows + shared_rows, LANES), jnp.float32)
    full = pltpu.VMEM((dests * own_rows + shared_rows, LANES), jnp.float32)
    results = ((half, half) if pairs else (full,)) + (
        pltpu.VMEM((levels, rows, cols), jnp.float32),
        pltpu.VMEM((rows, cols), jnp.float32),
    )
    sums = pl.pallas_call(
        functools.partial(inner_kernel, dims, pairs),
        out_shape=results,
        in_specs=[vmem] * 5,
        out_specs=(vmem,) * len(results),
        scratch_shapes=[pltpu.VMEM((rows, cols), jnp.float32)],
        compiler_params=params,
        name="inner_rows",
    )(flow, warmth, flag, floor, basin)
    sums = pl.pallas_call(
        functools.partial(last_kernel, dims, pairs),
        out_shape=results,
        in_specs=[vmem] * (6 + len(results)),
        out_specs=(vmem,) * len(results),
        input_output_aliases={6 + i: i for i in range(len(results))},
        compiler_params=params,
        name="last_rows",
    )(halo, flow, warmth, flag, floor, basin, *sums)
    mean_warmth, limit = sums[-2:]

    if pairs:
        keep, give = sums[:2]
        came = lax.ppermute(give, "lon", [(i, i ^ 1) for i in range(lon)])
        message = pltpu.VMEM((own_rows + shared_rows, LANES), jnp.float32)
        chips = lon // 2
        messages = pl.pallas_call(
            functools.partial(pair_kernel, dims),
            out_shape=(message,) * chips,
            in_specs=[vmem, vmem],
            out_specs=(vmem,) * chips,
            compiler_params=params,
            name="pair_sums",
        )(keep, came)
        got = messages[:1] + tuple(
            lax.ppermute(messages[m], "lon", [(i, i ^ (2 * m)) for i in range(lon)])
            for m in range(1, chips)
        )
    else:
        own, shared = sums[0][: dests * own_rows], sums[0][dests * own_rows :]
        sent = jnp.concatenate(
            [own.reshape(dests, own_rows, LANES), jnp.broadcast_to(shared, (dests, shared_rows, LANES))],
            axis=1,
        )
        if dests != lon:
            sent = jnp.repeat(sent, lon // dests, axis=0, total_repeat_length=lon)
        got = (lax.all_to_all(sent, "lon", 0, 0),)

    eddy, transport = pl.pallas_call(
        functools.partial(finish_kernel, dims, scaling),
        out_shape=(
            jax.ShapeDtypeStruct((levels, rows, cols), jnp.float32),
            jax.ShapeDtypeStruct((4, levels, per_dest * SUB, BASINS), jnp.float32),
        ),
        in_specs=[vmem] * (len(got) + 3),
        out_specs=(vmem, vmem),
        compiler_params=params,
        name="finish",
    )(*got, mean_warmth, limit, basin)
    if dests != lon:
        first = lax.axis_index("lon") * share % SUB
        transport = lax.dynamic_slice_in_dim(transport, first, share, 2)
    return eddy, jnp.transpose(transport, (0, 3, 1, 2))


def solution(mesh):
    return jax.shard_map(
        shards,
        mesh=mesh,
        in_specs=(
            P(None, None, "lat", "lon"),
            P(None, None, "lat", "lon"),
            P("lat", "lon"),
            P("lat", "lon"),
            P("lat", "lon"),
        ),
        out_specs=(P(None, "lat", "lon"), P(None, None, None, ("lat", "lon"))),
        check_vma=False,
    )
```

time: 31.9 us -> 20.2 us (0.63)
  blocking collectives: 13.6 us -> 0 us
  starting transfers between devices: 1.28 us -> 4.91 us
  waiting for transfers between devices: 5.46 us -> 8.88 us
  Pallas kernels: 8.19 us -> 5.45 us
  local copies, waits for them, and re-layouts: 1.54 us -> 0.02 us
  other arithmetic: 0.72 us -> 0 us
    all_to_all x1 -> x0, blocking collectives: 13.6 us -> none  [shards(): got = lax.all_to_all(sent, 'lon', 0, 0)]
    ppermute x0 -> x4, waiting for transfers between devices: none -> 6.47 us  [the longest x3 5.08 us: shards(): lax.ppermute(messages[m], 'lon', [(i, i ^ 2 * m) for i in range(lon)])]
    ppermute x0 -> x4, starting transfers between devices: none -> 3.62 us  [the longest x3 3.55 us: shards(): lax.ppermute(messages[m], 'lon', [(i, i ^ 2 * m) for i in range(lon)])]
    ppermute x1, waiting for transfers between devices: 5.46 us -> 2.41 us  [shards(): halo = lax.ppermute(edge, 'lat', [(i, i - 1) for i in range(1, lat)])]
    pallas_call x1 -> x4, Pallas kernels: 6.2 us -> 4.56 us  [the longest x1 2.99 us: shards(): pl.pallas_call(functools.partial(inner_kernel, dims, pairs), out_shape=re...]
    pallas_call x1, Pallas kernels: 2 us -> 0.89 us  [shards(): pl.pallas_call(functools.partial(finish_kernel, dims, scaling), out_shape...]
    slice x1 -> x0, local copies, waits for them, and re-layouts: 0.93 us -> none  [shards(): warmth[:, :, 0, :].reshape(snapshots * levels, cols)]
    convert_element_type x1 -> x0, other arithmetic: 0.71 us -> none  [shards(): (flag[:1] * floor[:1]).astype(jnp.float32)]
  transfers between devices with their start and end apart: 1 -> 5, of which waited for: 1 -> 5; matrix products, arithmetic and copies ran while one was open for 0% -> 0% of each run, Pallas kernels for 0% -> 15%
where the time goes in v2:
time: 20.2 us; the launch traced here: 20 us
  waiting for transfers between devices  8.88 us (44%)
  Pallas kernels  5.45 us (27%)
  starting transfers between devices  4.91 us (24%)
  between operations  0.75 us (4%)
    ppermute x3, waiting for transfers between devices, shards(): lax.ppermute(messages[m], 'lon', [(i, i ^ 2 * m) for i in range(lon)])  5.08 us
    ppermute x3, starting transfers between devices, shards(): lax.ppermute(messages[m], 'lon', [(i, i ^ 2 * m) for i in range(lon)])  3.55 us
    pallas_call x1, Pallas kernels, shards(): pl.pallas_call(functools.partial(inner_kernel, dims, pairs), out_shape=re...  2.99 us
    ppermute x1, waiting for transfers between devices, shards(): halo = lax.ppermute(edge, 'lat', [(i, i - 1) for i in range(1, lat)])  2.41 us
    ppermute x1, waiting for transfers between devices, shards(): came = lax.ppermute(give, 'lon', [(i, i ^ 1) for i in range(lon)])  1.39 us
    ppermute x1, starting transfers between devices, shards(): halo = lax.ppermute(edge, 'lat', [(i, i - 1) for i in range(1, lat)])  1.29 us
    pallas_call x1, Pallas kernels, shards(): pl.pallas_call(functools.partial(edge_kernel, dims), out_shape=pltpu.VMEM...  1.1 us
    pallas_call x1, Pallas kernels, shards(): pl.pallas_call(functools.partial(finish_kernel, dims, scaling), out_shape...  0.89 us
  transfers between devices with their start and end apart: 5, of which 5 were waited for; matrix products, arithmetic and copies ran while one was open for 0% of the time, Pallas kernels for 15%

profile of v2, /device:TPU:0, one launch (start us, length us, event | category | flops | bytes accessed | tf_op | source)
XLA Modules:
  0.0 20.0 jit_solution(3451075440911004671)
XLA Ops:
  0.6 0.0 copy-start.4
  0.6 0.0 copy-start.3
  0.7 0.0 copy-start
  0.7 0.0 copy-start.2
  0.7 0.0 copy-start.1
  0.7 1.1 %edge.1 = f32[41,128]{1,0:T(8,128)S(1)} custom-call(f32[10,4,64,128]{3,2,1,0:T(8,128)} %warmth.5, s32[64,128]{1,0:T(8,128)} %flag.5, s32[64,128]{1,0:T(8,128)} %floor.5), custom_call_target="tpu_custom_call" | custom-call | flops 10000000000 | bytes 8388608 | tf_op jit(solution)/shard_map/edge/pallas_call | solution.py:310
  1.8 1.3 %collective-permute-start = (f32[41,128]{1,0:T(8,128)S(1)}, f32[41,128]{1,0:T(8,128)S(1)}, u32[]{:S(2)}, u32[]{:S(2)}) collective-permute-start(f32[41,128]{1,0:T(8,128)S(1)} %edge.1), channel_id=1, source_target_pairs={{8,0},{16,8},{24,16},{9,1},{17,9},{25,17},{10,2},{18,10},{26,18},{... | collective-permute-start | bytes 62984 | tf_op jit(solution)/shard_map/ppermute | solution.py:325
  3.1 0.0 copy-done.4
  3.1 0.0 copy-done.3
  3.1 0.0 copy-done
  3.1 0.0 copy-done.2
  3.1 0.0 copy-done.1
  3.1 3.0 %inner_rows.1 = (f32[336,128]{1,0:T(8,128)S(1)}, f32[336,128]{1,0:T(8,128)S(1)}, f32[4,64,128]{2,1,0:T(8,128)S(1)}, f32[64,128]{1,0:T(8,128)S(1)}) custom-call(f32[10,4,64,128]{3,2,1,0:T(8,128)S(1)} %copy-done.1, f32[10,4,64,128]{3,2,1,0:T(8,128)S(1)} %copy-done, s32[64,128]{1,0:T(8,128)S(1)} %copy-done.3, s32[64,128]{1,0:T(8,128)S(1)} %copy-done.4, ...), custom_call_target="tpu_custom_call" | custom-call | tf_op jit(solution)/shard_map/inner_rows/pallas_call | solution.py:334
  6.1 2.4 %collective-permute-done.halo = f32[41,128]{1,0:T(8,128)S(1)} collective-permute-done((f32[41,128]{1,0:T(8,128)S(1)}, f32[41,128]{1,0:T(8,128)S(1)}, u32[]{:S(2)}, u32[]{:S(2)}) %collective-permute-start) | collective-permute-done | bytes 21024 | tf_op jit(solution)/shard_map/ppermute | solution.py:325
  8.5 0.4 %last_rows.1 = (f32[336,128]{1,0:T(8,128)S(1)}, f32[336,128]{1,0:T(8,128)S(1)}, f32[4,64,128]{2,1,0:T(8,128)S(1)}, f32[64,128]{1,0:T(8,128)S(1)}) custom-call(f32[41,128]{1,0:T(8,128)S(1)} %collective-permute-done.halo, f32[10,4,64,128]{3,2,1,0:T(8,128)S(1)} %copy-done.1, ...), custom_call_target="tpu_custom_call", output_to_operand_aliasing={{0}: (6, {}), {1}: (7, {}), {2}: (8, {}), {3}: (9, {})} | custom-call | tf_op jit(solution)/shard_map/last_rows/pallas_call | solution.py:343
  9.0 0.1 collective-permute-start.1
  9.1 1.4 %collective-permute-done.1.came = f32[336,128]{1,0:T(8,128)S(1)} collective-permute-done((f32[336,128]{1,0:T(8,128)S(1)}, f32[336,128]{1,0:T(8,128)S(1)}, u32[]{:S(2)}, u32[]{:S(2)}) %collective-permute-start.1) | collective-permute-done | bytes 172064 | tf_op jit(solution)/shard_map/ppermute | solution.py:356
  10.5 2.0 %collective-permute-start.2 = (f32[120,128]{1,0:T(8,128)S(1)}, f32[120,128]{1,0:T(8,128)S(1)}, u32[]{:S(2)}, u32[]{:S(2)}) collective-permute-start(f32[120,128]{1,0:T(8,128)S(1)} %get-tuple-element.23), channel_id=1, source_target_pairs={{0,2},{1,3},{2,0},{3,1},{4,6},{5,7},{6,4},{7,5},{8,10},{9,11},{10,... | collective-permute-start | bytes 184328 | tf_op jit(solution)/shard_map/ppermute | solution.py:368
  12.5 1.5 %collective-permute-start.3 = (f32[120,128]{1,0:T(8,128)S(1)}, f32[120,128]{1,0:T(8,128)S(1)}, u32[]{:S(2)}, u32[]{:S(2)}) collective-permute-start(f32[120,128]{1,0:T(8,128)S(1)} %get-tuple-element.24), channel_id=1, source_target_pairs={{0,4},{1,5},{2,6},{3,7},{4,0},{5,1},{6,2},{7,3},{8,12},{9,13},{10,... | collective-permute-start | bytes 184328 | tf_op jit(solution)/shard_map/ppermute | solution.py:368
  14.0 0.0 collective-permute-start.4
  14.0 0.8 %collective-permute-done.2.refs_1_ = f32[120,128]{1,0:T(8,128)S(1)} collective-permute-done((f32[120,128]{1,0:T(8,128)S(1)}, f32[120,128]{1,0:T(8,128)S(1)}, u32[]{:S(2)}, u32[]{:S(2)}) %collective-permute-start.2) | collective-permute-done | bytes 61472 | tf_op jit(solution)/shard_map/ppermute | solution.py:368
  14.8 1.9 %collective-permute-done.3.refs_2_ = f32[120,128]{1,0:T(8,128)S(1)} collective-permute-done((f32[120,128]{1,0:T(8,128)S(1)}, f32[120,128]{1,0:T(8,128)S(1)}, u32[]{:S(2)}, u32[]{:S(2)}) %collective-permute-start.3) | collective-permute-done | bytes 61472 | tf_op jit(solution)/shard_map/ppermute | solution.py:368
  16.7 2.4 %collective-permute-done.4.refs_3_ = f32[120,128]{1,0:T(8,128)S(1)} collective-permute-done((f32[120,128]{1,0:T(8,128)S(1)}, f32[120,128]{1,0:T(8,128)S(1)}, u32[]{:S(2)}, u32[]{:S(2)}) %collective-permute-start.4) | collective-permute-done | bytes 61472 | tf_op jit(solution)/shard_map/ppermute | solution.py:368
  19.1 0.9 %finish.1 = (f32[4,64,128]{2,1,0:T(8,128)}, f32[4,4,8,10]{3,2,1,0:T(8,128)}) custom-call(f32[120,128]{1,0:T(8,128)S(1)} %get-tuple-element.22.refs_0_, f32[120,128]{1,0:T(8,128)S(1)} %collective-permute-done.2.refs_1_, f32[120,128]{1,0:T(8,128)S(1)} %collective-permute-done.3.refs_2_, f32[120,128]{1,0:T(8,128)S(1)} %collective-permute-done.4.refs_3_, ...), custom_call_target="tpu_custom_call" | custom-call | tf_op jit(solution)/shard_map/finish/pallas_call | solution.py:381
  (1 shorter events, 0.0 us)
Async XLA Ops:
  0.6 2.5 %copy-start.4 = (s32[64,128]{1,0:T(8,128)S(1)}, s32[64,128]{1,0:T(8,128)}, u32[]{:S(2)}) copy-start(s32[64,128]{1,0:T(8,128)} %floor.5) | copy-start | bytes 98308
  0.6 2.5 %copy-start.3 = (s32[64,128]{1,0:T(8,128)S(1)}, s32[64,128]{1,0:T(8,128)}, u32[]{:S(2)}) copy-start(s32[64,128]{1,0:T(8,128)} %flag.5) | copy-start | bytes 98308
  0.7 2.5 %copy-start = (f32[10,4,64,128]{3,2,1,0:T(8,128)S(1)}, f32[10,4,64,128]{3,2,1,0:T(8,128)}, u32[]{:S(2)}) copy-start(f32[10,4,64,128]{3,2,1,0:T(8,128)} %warmth.5) | copy-start | bytes 3932164
  0.7 2.5 %copy-start.2 = (s32[64,128]{1,0:T(8,128)S(1)}, s32[64,128]{1,0:T(8,128)}, u32[]{:S(2)}) copy-start(s32[64,128]{1,0:T(8,128)} %refs_6_.1) | copy-start | bytes 98308
  0.7 2.5 %copy-start.1 = (f32[10,4,64,128]{3,2,1,0:T(8,128)S(1)}, f32[10,4,64,128]{3,2,1,0:T(8,128)}, u32[]{:S(2)}) copy-start(f32[10,4,64,128]{3,2,1,0:T(8,128)} %flow.3) | copy-start | bytes 3932164
  1.8 6.8 %collective-permute-start = (f32[41,128]{1,0:T(8,128)S(1)}, f32[41,128]{1,0:T(8,128)S(1)}, u32[]{:S(2)}, u32[]{:S(2)}) collective-permute-start(f32[41,128]{1,0:T(8,128)S(1)} %edge.1), channel_id=1, source_target_pairs={{8,0},{16,8},{24,16},{9,1},{17,9},{25,17},{10,2},{18,10},{26,18},{... | collective-permute-start | bytes 62984 | tf_op jit(solution)/shard_map/ppermute | solution.py:325
  9.0 1.5 %collective-permute-start.1 = (f32[336,128]{1,0:T(8,128)S(1)}, f32[336,128]{1,0:T(8,128)S(1)}, u32[]{:S(2)}, u32[]{:S(2)}) collective-permute-start(f32[336,128]{1,0:T(8,128)S(1)} %get-tuple-element.21), channel_id=1, source_target_pairs={{0,1},{1,0},{2,3},{3,2},{4,5},{5,4},{6,7},{7,6},{8,9},{9,8},{10,11... | collective-permute-start | bytes 516104 | tf_op jit(solution)/shard_map/ppermute | solution.py:356
  10.5 4.3 %collective-permute-start.2 = (f32[120,128]{1,0:T(8,128)S(1)}, f32[120,128]{1,0:T(8,128)S(1)}, u32[]{:S(2)}, u32[]{:S(2)}) collective-permute-start(f32[120,128]{1,0:T(8,128)S(1)} %get-tuple-element.23), channel_id=1, source_target_pairs={{0,2},{1,3},{2,0},{3,1},{4,6},{5,7},{6,4},{7,5},{8,10},{9,11},{10,... | collective-permute-start | bytes 184328 | tf_op jit(solution)/shard_map/ppermute | solution.py:368
  12.5 4.2 %collective-permute-start.3 = (f32[120,128]{1,0:T(8,128)S(1)}, f32[120,128]{1,0:T(8,128)S(1)}, u32[]{:S(2)}, u32[]{:S(2)}) collective-permute-start(f32[120,128]{1,0:T(8,128)S(1)} %get-tuple-element.24), channel_id=1, source_target_pairs={{0,4},{1,5},{2,6},{3,7},{4,0},{5,1},{6,2},{7,3},{8,12},{9,13},{10,... | collective-permute-start | bytes 184328 | tf_op jit(solution)/shard_map/ppermute | solution.py:368
  14.0 5.1 %collective-permute-start.4 = (f32[120,128]{1,0:T(8,128)S(1)}, f32[120,128]{1,0:T(8,128)S(1)}, u32[]{:S(2)}, u32[]{:S(2)}) collective-permute-start(f32[120,128]{1,0:T(8,128)S(1)} %get-tuple-element.25), channel_id=1, source_target_pairs={{0,6},{1,7},{2,4},{3,5},{4,2},{5,3},{6,0},{7,1},{8,14},{9,15},{10,... | collective-permute-start | bytes 184328 | tf_op jit(solution)/shard_map/ppermute | solution.py:368

commit v3 on v2

--- a/solution.py
+++ b/solution.py
@@ -31,21 +31,6 @@
         return left
     right = pltpu.roll(tiles[first + 1], LANES - shift, 1)
     return jnp.where(lax.broadcasted_iota(jnp.int32, left.shape, 1) < LANES - shift, left, right)
-
-
-def place_lanes(blocks, width, count):
-    tiles = [None] * count
-    lane = lax.broadcasted_iota(jnp.int32, blocks[0].shape, 1)
-    for k, block in enumerate(blocks):
-        first, shift = divmod(k * width, LANES)
-        moved = block if shift == 0 else pltpu.roll(block, shift, 1)
-        if tiles[first] is None:
-            tiles[first] = moved
-        else:
-            tiles[first] = jnp.where(lane < shift, tiles[first], moved)
-        if shift + width > LANES:
-            tiles[first + 1] = moved
-    return tiles
 
 
 def edge_kernel(dims, warmth, flag, floor, edge, rows_buf, flag_buf, floor_buf, sem):
@@ -76,44 +61,75 @@
     own_rows = tiles * quantities
     sub, lane = iota(0), iota(1)
     diagonal = lane % SUB
-    placed = []
-    for k in range(levels):
+
+    def level_data(k):
         v = [get_v(t, k) for t in range(snapshots)]
         w = [get_w(t, k) for t in range(snapshots)]
         mv = sum(v[1:], v[0]) * (1.0 / snapshots)
         mw = sum(w[1:], w[0]) * (1.0 / snapshots)
         cross = sum((a - mv) * (b - mw) for a, b in zip(v, w)) * (1.0 / snapshots)
         put_mean(k, mw)
-        data = jnp.concatenate(v + w + [mv * mw, cross, mw, jnp.ones_like(mw)], axis=0)
+        return jnp.concatenate(v + w + [mv * mw, cross, mw, jnp.ones_like(mw)], axis=0)
+
+    def level_hot(k):
         masked = jnp.where(shallow > float(k), label, -1)
-        hot = jnp.concatenate(
-            [jnp.where(masked == b, 1.0, 0.0) for b in range(BASINS)], axis=0
-        ).astype(jnp.bfloat16)
-        total = None
-        rest = data
-        for piece in range(3):
-            part = rest.astype(jnp.bfloat16)
-            if piece < 2:
-                rest = rest - part.astype(jnp.float32)
-            dot = lax.dot_general(
-                part, hot, (((1,), (1,)), ((), ())), preferred_element_type=jnp.float32
+        return [jnp.where(masked == b, 1.0, 0.0) for b in range(BASINS)]
+
+    done = [None] * tiles
+    nothing = jnp.zeros((SUB, LANES), jnp.float32)
+    for first in range(0, levels, 2):
+        pair = range(first, min(first + 2, levels))
+        tile, shift = divmod(first * width, LANES)
+        data = jnp.concatenate([level_data(k) for k in pair], axis=1)
+        pad = [nothing] * (shift // SUB)
+        columns = []
+        for k in pair:
+            column = list(pad)
+            for other in pair:
+                column += level_hot(k) if other == k else [nothing] * BASINS
+            columns.append(jnp.concatenate(column, axis=0))
+        hot = jnp.concatenate(columns, axis=1).astype(jnp.bfloat16)
+        height = quantities * SUB
+        parts = []
+        for at in range(0, height, 64):
+            rest = data[at : at + 64]
+            for piece in range(3):
+                parts.append(rest.astype(jnp.bfloat16))
+                if piece < 2:
+                    rest = rest - parts[-1].astype(jnp.float32)
+        dots = lax.dot_general(
+            jnp.concatenate(parts, axis=0),
+            hot,
+            (((1,), (1,)), ((), ())),
+            preferred_element_type=jnp.float32,
+        )
+        sums = []
+        for at in range(0, height, 64):
+            x = [dots[3 * at + p * 64 : 3 * at + (p + 1) * 64] for p in range(3)]
+            sums.append(x[0] + x[1] + x[2])
+        total = jnp.concatenate(sums, axis=0)
+        spare = -total.shape[1] % LANES
+        if spare:
+            total = jnp.concatenate(
+                [total, jnp.zeros((total.shape[0], spare), jnp.float32)], axis=1
             )
-            total = dot if total is None else total + dot
-        total = jnp.concatenate(
-            [total, jnp.zeros((total.shape[0], LANES - width), jnp.float32)], axis=1
-        )
-        groups = []
-        for g in range(quantities // SUB):
-            acc = None
-            for s in range(SUB):
-                q = g * SUB + s
-                row = jnp.take_along_axis(
-                    total[q * SUB : (q + 1) * SUB], diagonal, axis=0, mode="promise_in_bounds"
-                )
-                acc = row if acc is None else jnp.where(sub == s, row, acc)
-            groups.append(acc)
-        placed.append(jnp.concatenate(groups, axis=0))
-    done = place_lanes(placed, width, tiles)
+        for c in range(total.shape[1] // LANES):
+            groups = []
+            for g in range(quantities // SUB):
+                acc = None
+                for s in range(SUB):
+                    q = g * SUB + s
+                    row = jnp.take_along_axis(
+                        total[q * SUB : (q + 1) * SUB, c * LANES : (c + 1) * LANES],
+                        diagonal,
+                        axis=0,
+                        mode="promise_in_bounds",
+                    )
+                    acc = row if acc is None else jnp.where(sub == s, row, acc)
+                if done[tile + c] is not None:
+                    acc = jnp.where(lane < shift, done[tile + c][g * SUB : (g + 1) * SUB], acc)
+                groups.append(acc)
+            done[tile + c] = jnp.concatenate(groups, axis=0)
     for c in range(tiles):
         put_own(c, done[c])
         for q in range(2):
@@ -184,7 +200,7 @@
     lax.fori_loop(0, blocks - 1, body, 0)
 
 
-def last_kernel(dims, pairs, halo, flow, warmth, flag, floor, basin, *refs):
+def last_kernel(dims, pairs, odd_halo, even_halo, flow, warmth, flag, floor, basin, *refs):
     snapshots, levels, rows, blocks = dims[:4]
     outs = refs[len(refs) // 2 :]
     keep, give = outs[:2] if pairs else (outs[0], None)
@@ -192,12 +208,17 @@
     here = slice(rows - SUB, rows)
     below = lax.broadcasted_iota(jnp.int32, (SUB, LANES), 0) < SUB - 1
 
-    def north(block, edge_row):
-        return jnp.where(below, pltpu.roll(block, SUB - 1, 0), edge_row)
+    lat = lax.axis_index("lat")
+    even = lat % 2 == 0
+    inside = jnp.where(lat < lax.axis_size("lat") - 1, 1.0, 0.0)
+
+    def north(block, n):
+        row = jnp.where(even, even_halo[n : n + 1, :], odd_halo[n : n + 1, :]) * inside
+        return jnp.where(below, pltpu.roll(block, SUB - 1, 0), row)
 
     depth = (flag[here, :] * floor[here, :]).astype(jnp.float32)
     edge_at = snapshots * levels
-    shallow = jnp.minimum(depth, north(depth, halo[edge_at : edge_at + 1, :]))
+    shallow = jnp.minimum(depth, north(depth, edge_at))
     limit[here, :] = shallow
 
     def put_mean(k, value):
@@ -208,8 +229,7 @@
 
     def get_w(t, k):
         block = warmth[t, k, here, :]
-        n = t * levels + k
-        return 0.5 * (block + north(block, halo[n : n + 1, :]))
+        return 0.5 * (block + north(block, t * levels + k))
 
     put_own, put_shared = writers(dims, blocks - 1, keep, give)
     block_sums(
@@ -282,6 +302,19 @@
                 transport[term, k, i * SUB : (i + 1) * SUB, :] = cell[:, :BASINS]
 
 
+def neighbours(lat, lon, first):
+    route = []
+    for i in range(lat):
+        other = i + 1 if (i - first) % 2 == 0 else i - 1
+        for j in range(lon):
+            if 0 <= other < lat:
+                target = other * lon + j
+            else:
+                target = i * lon + (j ^ 1 if lon % 2 == 0 else j)
+            route.append((i * lon + j, target))
+    return route
+
+
 def shards(flow, warmth, flag, floor, basin):
     snapshots, levels, rows, cols = flow.shape
     lon, lat = lax.axis_size("lon"), lax.axis_size("lat")
@@ -322,7 +355,9 @@
         cost_estimate=pl.CostEstimate(flops=10000000000, bytes_accessed=8 << 20, transcendentals=0),
         name="edge",
     )(far(warmth), far(flag), far(floor))
-    halo = lax.ppermute(edge, "lat", [(i, i - 1) for i in range(1, lat)])
+    halos = tuple(
+        lax.ppermute(edge, ("lat", "lon"), neighbours(lat, lon, first)) for first in range(2)
+    )
 
     flow, warmth, flag, floor, basin = (near(x) for x in (flow, warmth, flag, floor, basin))
     half = pltpu.VMEM((dests // 2 * own_rows + shared_rows, LANES), jnp.float32)
@@ -343,12 +378,12 @@
     sums = pl.pallas_call(
         functools.partial(last_kernel, dims, pairs),
         out_shape=results,
-        in_specs=[vmem] * (6 + len(results)),
+        in_specs=[vmem] * (7 + len(results)),
         out_specs=(vmem,) * len(results),
-        input_output_aliases={6 + i: i for i in range(len(results))},
+        input_output_aliases={7 + i: i for i in range(len(results))},
         compiler_params=params,
         name="last_rows",
-    )(halo, flow, warmth, flag, floor, basin, *sums)
+    )(*halos[::-1], flow, warmth, flag, floor, basin, *sums)
     mean_warmth, limit = sums[-2:]
 
     if pairs:
@@ -366,7 +401,7 @@
         )(keep, came)
         got = messages[:1] + tuple(
             lax.ppermute(messages[m], "lon", [(i, i ^ (2 * m)) for i in range(lon)])
-            for m in range(1, chips)
+            for m in reversed(range(1, chips))
         )
     else:
         own, shared = sums[0][: dests * own_rows], sums[0][dests * own_rows :]

time: 20.2 us -> 18.1 us (0.90)
  waiting for transfers between devices: 8.88 us -> 4.73 us
  starting transfers between devices: 4.91 us -> 7.23 us
    ppermute x1 -> x2, waiting for transfers between devices: 2.41 us -> 0.01 us  [shards(): lax.ppermute(edge, ('lat', 'lon'), neighbours(lat, lon, first))]
    ppermute x1 -> x2, starting transfers between devices: 1.29 us -> 3.12 us  [shards(): lax.ppermute(edge, ('lat', 'lon'), neighbours(lat, lon, first))]
    ppermute x3, waiting for transfers between devices: 5.08 us -> 3.69 us  [shards(): lax.ppermute(messages[m], 'lon', [(i, i ^ 2 * m) for i in range(lon)])]
    ppermute x1, starting transfers between devices: 0.07 us -> 0.56 us  [shards(): came = lax.ppermute(give, 'lon', [(i, i ^ 1) for i in range(lon)])]
    ppermute x1, waiting for transfers between devices: 1.39 us -> 1.04 us  [shards(): came = lax.ppermute(give, 'lon', [(i, i ^ 1) for i in range(lon)])]
  transfers between devices with their start and end apart: 5 -> 6, of which waited for: 5 -> 4; matrix products, arithmetic and copies ran while one was open for 0% -> 0% of each run, Pallas kernels for 15% -> 16%
where the time goes in v3:
time: 18.1 us; the launch traced here: 18 us
  starting transfers between devices  7.23 us (40%)
  Pallas kernels  5.25 us (29%)
  waiting for transfers between devices  4.73 us (26%)
  between operations  0.75 us (4%)
    ppermute x3, waiting for transfers between devices, shards(): lax.ppermute(messages[m], 'lon', [(i, i ^ 2 * m) for i in range(lon)])  3.69 us
    ppermute x3, starting transfers between devices, shards(): lax.ppermute(messages[m], 'lon', [(i, i ^ 2 * m) for i in range(lon)])  3.55 us
    ppermute x2, starting transfers between devices, shards(): lax.ppermute(edge, ('lat', 'lon'), neighbours(lat, lon, first))  3.12 us
    pallas_call x1, Pallas kernels, shards(): pl.pallas_call(functools.partial(inner_kernel, dims, pairs), out_shape=re...  2.83 us
    pallas_call x1, Pallas kernels, shards(): pl.pallas_call(functools.partial(edge_kernel, dims), out_shape=pltpu.VMEM...  1.1 us
    ppermute x1, waiting for transfers between devices, shards(): came = lax.ppermute(give, 'lon', [(i, i ^ 1) for i in range(lon)])  1.04 us
    pallas_call x1, Pallas kernels, shards(): pl.pallas_call(functools.partial(finish_kernel, dims, scaling), out_shape...  0.89 us
    ppermute x1, starting transfers between devices, shards(): came = lax.ppermute(give, 'lon', [(i, i ^ 1) for i in range(lon)])  0.56 us
  transfers between devices with their start and end apart: 6, of which 4 were waited for; matrix products, arithmetic and copies ran while one was open for 0% of the time, Pallas kernels for 16%

profile of v3, /device:TPU:0, one launch (start us, length us, event | category | flops | bytes accessed | tf_op | source)
XLA Modules:
  0.0 18.0 jit_solution(1049149336893893672)
XLA Ops:
  0.6 0.0 copy-start.4
  0.6 0.0 copy-start.3
  0.7 0.0 copy-start
  0.7 0.0 copy-start.2
  0.7 0.0 copy-start.1
  0.7 1.1 %edge.1 = f32[41,128]{1,0:T(8,128)S(1)} custom-call(f32[10,4,64,128]{3,2,1,0:T(8,128)} %warmth.5, s32[64,128]{1,0:T(8,128)} %flag.5, s32[64,128]{1,0:T(8,128)} %floor.5), custom_call_target="tpu_custom_call" | custom-call | flops 10000000000 | bytes 8388608 | tf_op jit(solution)/shard_map/edge/pallas_call | solution.py:343
  1.8 3.1 %collective-permute-start.1 = (f32[41,128]{1,0:T(8,128)S(1)}, f32[41,128]{1,0:T(8,128)S(1)}, u32[]{:S(2)}, u32[]{:S(2)}) collective-permute-start(f32[41,128]{1,0:T(8,128)S(1)} %edge.1), channel_id=1, source_target_pairs={{0,8},{1,9},{2,10},{3,11},{4,12},{5,13},{6,14},{7,15},{8,0},{9,1},... | collective-permute-start | bytes 62984 | tf_op jit(solution)/shard_map/ppermute | solution.py:359
  4.9 0.0 collective-permute-start
  4.9 0.0 copy-done.4
  4.9 0.0 copy-done.3
  4.9 0.0 copy-done
  4.9 0.0 copy-done.2
  4.9 0.0 copy-done.1
  4.9 2.8 %inner_rows.1 = (f32[336,128]{1,0:T(8,128)S(1)}, f32[336,128]{1,0:T(8,128)S(1)}, f32[4,64,128]{2,1,0:T(8,128)S(1)}, f32[64,128]{1,0:T(8,128)S(1)}) custom-call(f32[10,4,64,128]{3,2,1,0:T(8,128)S(1)} %copy-done.1, f32[10,4,64,128]{3,2,1,0:T(8,128)S(1)} %copy-done, s32[64,128]{1,0:T(8,128)S(1)} %copy-done.3, s32[64,128]{1,0:T(8,128)S(1)} %copy-done.4, ...), custom_call_target="tpu_custom_call" | custom-call | tf_op jit(solution)/shard_map/inner_rows/pallas_call | solution.py:369
  7.8 0.0 collective-permute-done.1.even_halo
  7.8 0.0 collective-permute-done.odd_halo
  7.8 0.4 %last_rows.1 = (f32[336,128]{1,0:T(8,128)S(1)}, f32[336,128]{1,0:T(8,128)S(1)}, f32[4,64,128]{2,1,0:T(8,128)S(1)}, f32[64,128]{1,0:T(8,128)S(1)}) custom-call(f32[41,128]{1,0:T(8,128)S(1)} %collective-permute-done.odd_halo, f32[41,128]{1,0:T(8,128)S(1)} %collective-permute-done.1.even_halo, ...), custom_call_target="tpu_custom_call", output_to_operand_aliasing={{0}: (7, {}), {1}: (8, {}), {2}: (9, {}), {3}: (10, {})} | custom-call | tf_op jit(solution)/shard_map/last_rows/pallas_call | solution.py:378
  8.2 0.6 %collective-permute-start.2 = (f32[336,128]{1,0:T(8,128)S(1)}, f32[336,128]{1,0:T(8,128)S(1)}, u32[]{:S(2)}, u32[]{:S(2)}) collective-permute-start(f32[336,128]{1,0:T(8,128)S(1)} %get-tuple-element.21), channel_id=1, source_target_pairs={{0,1},{1,0},{2,3},{3,2},{4,5},{5,4},{6,7},{7,6},{8,9},{9,8},{10,11... | collective-permute-start | bytes 516104 | tf_op jit(solution)/shard_map/ppermute | solution.py:391
  8.8 1.0 %collective-permute-done.2.came = f32[336,128]{1,0:T(8,128)S(1)} collective-permute-done((f32[336,128]{1,0:T(8,128)S(1)}, f32[336,128]{1,0:T(8,128)S(1)}, u32[]{:S(2)}, u32[]{:S(2)}) %collective-permute-start.2) | collective-permute-done | bytes 172064 | tf_op jit(solution)/shard_map/ppermute | solution.py:391
  9.8 2.5 %collective-permute-start.3 = (f32[120,128]{1,0:T(8,128)S(1)}, f32[120,128]{1,0:T(8,128)S(1)}, u32[]{:S(2)}, u32[]{:S(2)}) collective-permute-start(f32[120,128]{1,0:T(8,128)S(1)} %get-tuple-element.23), channel_id=1, source_target_pairs={{0,6},{1,7},{2,4},{3,5},{4,2},{5,3},{6,0},{7,1},{8,14},{9,15},{10,... | collective-permute-start | bytes 184328 | tf_op jit(solution)/shard_map/ppermute | solution.py:403
  12.4 0.5 %collective-permute-start.4 = (f32[120,128]{1,0:T(8,128)S(1)}, f32[120,128]{1,0:T(8,128)S(1)}, u32[]{:S(2)}, u32[]{:S(2)}) collective-permute-start(f32[120,128]{1,0:T(8,128)S(1)} %get-tuple-element.24), channel_id=1, source_target_pairs={{0,4},{1,5},{2,6},{3,7},{4,0},{5,1},{6,2},{7,3},{8,12},{9,13},{10,... | collective-permute-start | bytes 184328 | tf_op jit(solution)/shard_map/ppermute | solution.py:403
  12.9 0.5 %collective-permute-start.5 = (f32[120,128]{1,0:T(8,128)S(1)}, f32[120,128]{1,0:T(8,128)S(1)}, u32[]{:S(2)}, u32[]{:S(2)}) collective-permute-start(f32[120,128]{1,0:T(8,128)S(1)} %get-tuple-element.25), channel_id=1, source_target_pairs={{0,2},{1,3},{2,0},{3,1},{4,6},{5,7},{6,4},{7,5},{8,10},{9,11},{10,... | collective-permute-start | bytes 184328 | tf_op jit(solution)/shard_map/ppermute | solution.py:403
  13.4 1.7 %collective-permute-done.3.refs_1_ = f32[120,128]{1,0:T(8,128)S(1)} collective-permute-done((f32[120,128]{1,0:T(8,128)S(1)}, f32[120,128]{1,0:T(8,128)S(1)}, u32[]{:S(2)}, u32[]{:S(2)}) %collective-permute-start.3) | collective-permute-done | bytes 61472 | tf_op jit(solution)/shard_map/ppermute | solution.py:403
  15.1 1.5 %collective-permute-done.4.refs_2_ = f32[120,128]{1,0:T(8,128)S(1)} collective-permute-done((f32[120,128]{1,0:T(8,128)S(1)}, f32[120,128]{1,0:T(8,128)S(1)}, u32[]{:S(2)}, u32[]{:S(2)}) %collective-permute-start.4) | collective-permute-done | bytes 61472 | tf_op jit(solution)/shard_map/ppermute | solution.py:403
  16.6 0.5 %collective-permute-done.5.refs_3_ = f32[120,128]{1,0:T(8,128)S(1)} collective-permute-done((f32[120,128]{1,0:T(8,128)S(1)}, f32[120,128]{1,0:T(8,128)S(1)}, u32[]{:S(2)}, u32[]{:S(2)}) %collective-permute-start.5) | collective-permute-done | bytes 61472 | tf_op jit(solution)/shard_map/ppermute | solution.py:403
  17.1 0.9 %finish.1 = (f32[4,64,128]{2,1,0:T(8,128)}, f32[4,4,8,10]{3,2,1,0:T(8,128)}) custom-call(f32[120,128]{1,0:T(8,128)S(1)} %get-tuple-element.22.refs_0_, f32[120,128]{1,0:T(8,128)S(1)} %collective-permute-done.3.refs_1_, f32[120,128]{1,0:T(8,128)S(1)} %collective-permute-done.4.refs_2_, f32[120,128]{1,0:T(8,128)S(1)} %collective-permute-done.5.refs_3_, ...), custom_call_target="tpu_custom_call" | custom-call | tf_op jit(solution)/shard_map/finish/pallas_call | solution.py:416
  (1 shorter events, 0.0 us)
Async XLA Ops:
  0.6 4.3 %copy-start.4 = (s32[64,128]{1,0:T(8,128)S(1)}, s32[64,128]{1,0:T(8,128)}, u32[]{:S(2)}) copy-start(s32[64,128]{1,0:T(8,128)} %floor.5) | copy-start | bytes 98308
  0.6 4.3 %copy-start.3 = (s32[64,128]{1,0:T(8,128)S(1)}, s32[64,128]{1,0:T(8,128)}, u32[]{:S(2)}) copy-start(s32[64,128]{1,0:T(8,128)} %flag.5) | copy-start | bytes 98308
  0.7 4.3 %copy-start = (f32[10,4,64,128]{3,2,1,0:T(8,128)S(1)}, f32[10,4,64,128]{3,2,1,0:T(8,128)}, u32[]{:S(2)}) copy-start(f32[10,4,64,128]{3,2,1,0:T(8,128)} %warmth.5) | copy-start | bytes 3932164
  0.7 4.3 %copy-start.2 = (s32[64,128]{1,0:T(8,128)S(1)}, s32[64,128]{1,0:T(8,128)}, u32[]{:S(2)}) copy-start(s32[64,128]{1,0:T(8,128)} %refs_6_.1) | copy-start | bytes 98308
  0.7 4.3 %copy-start.1 = (f32[10,4,64,128]{3,2,1,0:T(8,128)S(1)}, f32[10,4,64,128]{3,2,1,0:T(8,128)}, u32[]{:S(2)}) copy-start(f32[10,4,64,128]{3,2,1,0:T(8,128)} %flow.3) | copy-start | bytes 3932164
  1.8 6.0 %collective-permute-start.1 = (f32[41,128]{1,0:T(8,128)S(1)}, f32[41,128]{1,0:T(8,128)S(1)}, u32[]{:S(2)}, u32[]{:S(2)}) collective-permute-start(f32[41,128]{1,0:T(8,128)S(1)} %edge.1), channel_id=1, source_target_pairs={{0,8},{1,9},{2,10},{3,11},{4,12},{5,13},{6,14},{7,15},{8,0},{9,1},... | collective-permute-start | bytes 62984 | tf_op jit(solution)/shard_map/ppermute | solution.py:359
  4.9 2.9 %collective-permute-start = (f32[41,128]{1,0:T(8,128)S(1)}, f32[41,128]{1,0:T(8,128)S(1)}, u32[]{:S(2)}, u32[]{:S(2)}) collective-permute-start(f32[41,128]{1,0:T(8,128)S(1)} %edge.1), channel_id=1, source_target_pairs={{0,1},{1,0},{2,3},{3,2},{4,5},{5,4},{6,7},{7,6},{8,16},{9,17},{10,... | collective-permute-start | bytes 62984 | tf_op jit(solution)/shard_map/ppermute | solution.py:359
  8.2 1.6 %collective-permute-start.2 = (f32[336,128]{1,0:T(8,128)S(1)}, f32[336,128]{1,0:T(8,128)S(1)}, u32[]{:S(2)}, u32[]{:S(2)}) collective-permute-start(f32[336,128]{1,0:T(8,128)S(1)} %get-tuple-element.21), channel_id=1, source_target_pairs={{0,1},{1,0},{2,3},{3,2},{4,5},{5,4},{6,7},{7,6},{8,9},{9,8},{10,11... | collective-permute-start | bytes 516104 | tf_op jit(solution)/shard_map/ppermute | solution.py:391
  9.8 5.2 %collective-permute-start.3 = (f32[120,128]{1,0:T(8,128)S(1)}, f32[120,128]{1,0:T(8,128)S(1)}, u32[]{:S(2)}, u32[]{:S(2)}) collective-permute-start(f32[120,128]{1,0:T(8,128)S(1)} %get-tuple-element.23), channel_id=1, source_target_pairs={{0,6},{1,7},{2,4},{3,5},{4,2},{5,3},{6,0},{7,1},{8,14},{9,15},{10,... | collective-permute-start | bytes 184328 | tf_op jit(solution)/shard_map/ppermute | solution.py:403
  12.4 4.2 %collective-permute-start.4 = (f32[120,128]{1,0:T(8,128)S(1)}, f32[120,128]{1,0:T(8,128)S(1)}, u32[]{:S(2)}, u32[]{:S(2)}) collective-permute-start(f32[120,128]{1,0:T(8,128)S(1)} %get-tuple-element.24), channel_id=1, source_target_pairs={{0,4},{1,5},{2,6},{3,7},{4,0},{5,1},{6,2},{7,3},{8,12},{9,13},{10,... | collective-permute-start | bytes 184328 | tf_op jit(solution)/shard_map/ppermute | solution.py:403
  12.9 4.2 %collective-permute-start.5 = (f32[120,128]{1,0:T(8,128)S(1)}, f32[120,128]{1,0:T(8,128)S(1)}, u32[]{:S(2)}, u32[]{:S(2)}) collective-permute-start(f32[120,128]{1,0:T(8,128)S(1)} %get-tuple-element.25), channel_id=1, source_target_pairs={{0,2},{1,3},{2,0},{3,1},{4,6},{5,7},{6,4},{7,5},{8,10},{9,11},{10,... | collective-permute-start | bytes 184328 | tf_op jit(solution)/shard_map/ppermute | solution.py:403

commit v4 on v3

--- a/solution.py
+++ b/solution.py
@@ -90,23 +90,30 @@
             columns.append(jnp.concatenate(column, axis=0))
         hot = jnp.concatenate(columns, axis=1).astype(jnp.bfloat16)
         height = quantities * SUB
-        parts = []
-        for at in range(0, height, 64):
-            rest = data[at : at + 64]
-            for piece in range(3):
+        exact = 2 * snapshots * SUB
+        cuts = [c for c in range(0, exact, 80)] + [exact, height]
+        parts, spans = [], []
+        for at, end in zip(cuts, cuts[1:]):
+            rest = data[at:end]
+            count = 2 if at < exact else 3
+            for piece in range(count):
                 parts.append(rest.astype(jnp.bfloat16))
-                if piece < 2:
+                if piece < count - 1:
                     rest = rest - parts[-1].astype(jnp.float32)
+            spans.append((end - at, count))
         dots = lax.dot_general(
             jnp.concatenate(parts, axis=0),
             hot,
             (((1,), (1,)), ((), ())),
             preferred_element_type=jnp.float32,
         )
-        sums = []
-        for at in range(0, height, 64):
-            x = [dots[3 * at + p * 64 : 3 * at + (p + 1) * 64] for p in range(3)]
-            sums.append(x[0] + x[1] + x[2])
+        sums, at = [], 0
+        for size, count in spans:
+            x = dots[at : at + size]
+            for piece in range(1, count):
+                x = x + dots[at + piece * size : at + (piece + 1) * size]
+            sums.append(x)
+            at += size * count
         total = jnp.concatenate(sums, axis=0)
         spare = -total.shape[1] % LANES
         if spare:

time: 18.1 us -> 17.7 us (0.978)
  Pallas kernels: 5.25 us -> 4.87 us
    pallas_call x1, Pallas kernels: 2.83 us -> 2.48 us  [shards(): pl.pallas_call(functools.partial(inner_kernel, dims, pairs), out_shape=re...]
  transfers between devices with their start and end apart: 6 -> 6, of which waited for: 4 -> 4; matrix products, arithmetic and copies ran while one was open for 0% -> 0% of each run, Pallas kernels for 16% -> 14%
where the time goes in v4:
time: 17.7 us; the launch traced here: 17.6 us
  starting transfers between devices  7.23 us (41%)
  Pallas kernels  4.87 us (28%)
  waiting for transfers between devices  4.73 us (27%)
  between operations  0.75 us (4%)
    ppermute x3, waiting for transfers between devices, shards(): lax.ppermute(messages[m], 'lon', [(i, i ^ 2 * m) for i in range(lon)])  3.69 us
    ppermute x3, starting transfers between devices, shards(): lax.ppermute(messages[m], 'lon', [(i, i ^ 2 * m) for i in range(lon)])  3.55 us
    ppermute x2, starting transfers between devices, shards(): lax.ppermute(edge, ('lat', 'lon'), neighbours(lat, lon, first))  3.12 us
    pallas_call x1, Pallas kernels, shards(): pl.pallas_call(functools.partial(inner_kernel, dims, pairs), out_shape=re...  2.48 us
    pallas_call x1, Pallas kernels, shards(): pl.pallas_call(functools.partial(edge_kernel, dims), out_shape=pltpu.VMEM...  1.1 us
    ppermute x1, waiting for transfers between devices, shards(): came = lax.ppermute(give, 'lon', [(i, i ^ 1) for i in range(lon)])  1.04 us
    pallas_call x1, Pallas kernels, shards(): pl.pallas_call(functools.partial(finish_kernel, dims, scaling), out_shape...  0.89 us
    ppermute x1, starting transfers between devices, shards(): came = lax.ppermute(give, 'lon', [(i, i ^ 1) for i in range(lon)])  0.55 us
  transfers between devices with their start and end apart: 6, of which 4 were waited for; matrix products, arithmetic and copies ran while one was open for 0% of the time, Pallas kernels for 14%

profile of v4, /device:TPU:0, one launch (start us, length us, event | category | flops | bytes accessed | tf_op | source)
XLA Modules:
  0.0 17.6 jit_solution(3679623348616683196)
XLA Ops:
  0.6 0.0 copy-start.4
  0.6 0.0 copy-start.3
  0.7 0.0 copy-start
  0.7 0.0 copy-start.2
  0.7 0.0 copy-start.1
  0.7 1.1 %edge.1 = f32[41,128]{1,0:T(8,128)S(1)} custom-call(f32[10,4,64,128]{3,2,1,0:T(8,128)} %warmth.5, s32[64,128]{1,0:T(8,128)} %flag.5, s32[64,128]{1,0:T(8,128)} %floor.5), custom_call_target="tpu_custom_call" | custom-call | flops 10000000000 | bytes 8388608 | tf_op jit(solution)/shard_map/edge/pallas_call | solution.py:350
  1.8 3.1 %collective-permute-start.1 = (f32[41,128]{1,0:T(8,128)S(1)}, f32[41,128]{1,0:T(8,128)S(1)}, u32[]{:S(2)}, u32[]{:S(2)}) collective-permute-start(f32[41,128]{1,0:T(8,128)S(1)} %edge.1), channel_id=1, source_target_pairs={{0,8},{1,9},{2,10},{3,11},{4,12},{5,13},{6,14},{7,15},{8,0},{9,1},... | collective-permute-start | bytes 62984 | tf_op jit(solution)/shard_map/ppermute | solution.py:366
  4.9 0.0 collective-permute-start
  4.9 0.0 copy-done.4
  4.9 0.0 copy-done.3
  4.9 0.0 copy-done
  4.9 0.0 copy-done.2
  4.9 0.0 copy-done.1
  4.9 2.5 %inner_rows.1 = (f32[336,128]{1,0:T(8,128)S(1)}, f32[336,128]{1,0:T(8,128)S(1)}, f32[4,64,128]{2,1,0:T(8,128)S(1)}, f32[64,128]{1,0:T(8,128)S(1)}) custom-call(f32[10,4,64,128]{3,2,1,0:T(8,128)S(1)} %copy-done.1, f32[10,4,64,128]{3,2,1,0:T(8,128)S(1)} %copy-done, s32[64,128]{1,0:T(8,128)S(1)} %copy-done.3, s32[64,128]{1,0:T(8,128)S(1)} %copy-done.4, ...), custom_call_target="tpu_custom_call" | custom-call | tf_op jit(solution)/shard_map/inner_rows/pallas_call | solution.py:376
  7.4 0.0 collective-permute-done.1.even_halo
  7.4 0.0 collective-permute-done.odd_halo
  7.5 0.4 %last_rows.1 = (f32[336,128]{1,0:T(8,128)S(1)}, f32[336,128]{1,0:T(8,128)S(1)}, f32[4,64,128]{2,1,0:T(8,128)S(1)}, f32[64,128]{1,0:T(8,128)S(1)}) custom-call(f32[41,128]{1,0:T(8,128)S(1)} %collective-permute-done.odd_halo, f32[41,128]{1,0:T(8,128)S(1)} %collective-permute-done.1.even_halo, ...), custom_call_target="tpu_custom_call", output_to_operand_aliasing={{0}: (7, {}), {1}: (8, {}), {2}: (9, {}), {3}: (10, {})} | custom-call | tf_op jit(solution)/shard_map/last_rows/pallas_call | solution.py:385
  7.8 0.6 %collective-permute-start.2 = (f32[336,128]{1,0:T(8,128)S(1)}, f32[336,128]{1,0:T(8,128)S(1)}, u32[]{:S(2)}, u32[]{:S(2)}) collective-permute-start(f32[336,128]{1,0:T(8,128)S(1)} %get-tuple-element.21), channel_id=1, source_target_pairs={{0,1},{1,0},{2,3},{3,2},{4,5},{5,4},{6,7},{7,6},{8,9},{9,8},{10,11... | collective-permute-start | bytes 516104 | tf_op jit(solution)/shard_map/ppermute | solution.py:398
  8.4 1.0 %collective-permute-done.2.came = f32[336,128]{1,0:T(8,128)S(1)} collective-permute-done((f32[336,128]{1,0:T(8,128)S(1)}, f32[336,128]{1,0:T(8,128)S(1)}, u32[]{:S(2)}, u32[]{:S(2)}) %collective-permute-start.2) | collective-permute-done | bytes 172064 | tf_op jit(solution)/shard_map/ppermute | solution.py:398
  9.5 2.5 %collective-permute-start.3 = (f32[120,128]{1,0:T(8,128)S(1)}, f32[120,128]{1,0:T(8,128)S(1)}, u32[]{:S(2)}, u32[]{:S(2)}) collective-permute-start(f32[120,128]{1,0:T(8,128)S(1)} %get-tuple-element.23), channel_id=1, source_target_pairs={{0,6},{1,7},{2,4},{3,5},{4,2},{5,3},{6,0},{7,1},{8,14},{9,15},{10,... | collective-permute-start | bytes 184328 | tf_op jit(solution)/shard_map/ppermute | solution.py:410
  12.0 0.5 %collective-permute-start.4 = (f32[120,128]{1,0:T(8,128)S(1)}, f32[120,128]{1,0:T(8,128)S(1)}, u32[]{:S(2)}, u32[]{:S(2)}) collective-permute-start(f32[120,128]{1,0:T(8,128)S(1)} %get-tuple-element.24), channel_id=1, source_target_pairs={{0,4},{1,5},{2,6},{3,7},{4,0},{5,1},{6,2},{7,3},{8,12},{9,13},{10,... | collective-permute-start | bytes 184328 | tf_op jit(solution)/shard_map/ppermute | solution.py:410
  12.5 0.5 %collective-permute-start.5 = (f32[120,128]{1,0:T(8,128)S(1)}, f32[120,128]{1,0:T(8,128)S(1)}, u32[]{:S(2)}, u32[]{:S(2)}) collective-permute-start(f32[120,128]{1,0:T(8,128)S(1)} %get-tuple-element.25), channel_id=1, source_target_pairs={{0,2},{1,3},{2,0},{3,1},{4,6},{5,7},{6,4},{7,5},{8,10},{9,11},{10,... | collective-permute-start | bytes 184328 | tf_op jit(solution)/shard_map/ppermute | solution.py:410
  13.0 1.7 %collective-permute-done.3.refs_1_ = f32[120,128]{1,0:T(8,128)S(1)} collective-permute-done((f32[120,128]{1,0:T(8,128)S(1)}, f32[120,128]{1,0:T(8,128)S(1)}, u32[]{:S(2)}, u32[]{:S(2)}) %collective-permute-start.3) | collective-permute-done | bytes 61472 | tf_op jit(solution)/shard_map/ppermute | solution.py:410
  14.7 1.5 %collective-permute-done.4.refs_2_ = f32[120,128]{1,0:T(8,128)S(1)} collective-permute-done((f32[120,128]{1,0:T(8,128)S(1)}, f32[120,128]{1,0:T(8,128)S(1)}, u32[]{:S(2)}, u32[]{:S(2)}) %collective-permute-start.4) | collective-permute-done | bytes 61472 | tf_op jit(solution)/shard_map/ppermute | solution.py:410
  16.2 0.5 %collective-permute-done.5.refs_3_ = f32[120,128]{1,0:T(8,128)S(1)} collective-permute-done((f32[120,128]{1,0:T(8,128)S(1)}, f32[120,128]{1,0:T(8,128)S(1)}, u32[]{:S(2)}, u32[]{:S(2)}) %collective-permute-start.5) | collective-permute-done | bytes 61472 | tf_op jit(solution)/shard_map/ppermute | solution.py:410
  16.7 0.9 %finish.1 = (f32[4,64,128]{2,1,0:T(8,128)}, f32[4,4,8,10]{3,2,1,0:T(8,128)}) custom-call(f32[120,128]{1,0:T(8,128)S(1)} %get-tuple-element.22.refs_0_, f32[120,128]{1,0:T(8,128)S(1)} %collective-permute-done.3.refs_1_, f32[120,128]{1,0:T(8,128)S(1)} %collective-permute-done.4.refs_2_, f32[120,128]{1,0:T(8,128)S(1)} %collective-permute-done.5.refs_3_, ...), custom_call_target="tpu_custom_call" | custom-call | tf_op jit(solution)/shard_map/finish/pallas_call | solution.py:423
  (1 shorter events, 0.0 us)
Async XLA Ops:
  0.6 4.3 %copy-start.4 = (s32[64,128]{1,0:T(8,128)S(1)}, s32[64,128]{1,0:T(8,128)}, u32[]{:S(2)}) copy-start(s32[64,128]{1,0:T(8,128)} %floor.5) | copy-start | bytes 98308
  0.6 4.3 %copy-start.3 = (s32[64,128]{1,0:T(8,128)S(1)}, s32[64,128]{1,0:T(8,128)}, u32[]{:S(2)}) copy-start(s32[64,128]{1,0:T(8,128)} %flag.5) | copy-start | bytes 98308
  0.7 4.3 %copy-start = (f32[10,4,64,128]{3,2,1,0:T(8,128)S(1)}, f32[10,4,64,128]{3,2,1,0:T(8,128)}, u32[]{:S(2)}) copy-start(f32[10,4,64,128]{3,2,1,0:T(8,128)} %warmth.5) | copy-start | bytes 3932164
  0.7 4.3 %copy-start.2 = (s32[64,128]{1,0:T(8,128)S(1)}, s32[64,128]{1,0:T(8,128)}, u32[]{:S(2)}) copy-start(s32[64,128]{1,0:T(8,128)} %refs_6_.1) | copy-start | bytes 98308
  0.7 4.3 %copy-start.1 = (f32[10,4,64,128]{3,2,1,0:T(8,128)S(1)}, f32[10,4,64,128]{3,2,1,0:T(8,128)}, u32[]{:S(2)}) copy-start(f32[10,4,64,128]{3,2,1,0:T(8,128)} %flow.3) | copy-start | bytes 3932164
  1.8 5.6 %collective-permute-start.1 = (f32[41,128]{1,0:T(8,128)S(1)}, f32[41,128]{1,0:T(8,128)S(1)}, u32[]{:S(2)}, u32[]{:S(2)}) collective-permute-start(f32[41,128]{1,0:T(8,128)S(1)} %edge.1), channel_id=1, source_target_pairs={{0,8},{1,9},{2,10},{3,11},{4,12},{5,13},{6,14},{7,15},{8,0},{9,1},... | collective-permute-start | bytes 62984 | tf_op jit(solution)/shard_map/ppermute | solution.py:366
  4.9 2.5 %collective-permute-start = (f32[41,128]{1,0:T(8,128)S(1)}, f32[41,128]{1,0:T(8,128)S(1)}, u32[]{:S(2)}, u32[]{:S(2)}) collective-permute-start(f32[41,128]{1,0:T(8,128)S(1)} %edge.1), channel_id=1, source_target_pairs={{0,1},{1,0},{2,3},{3,2},{4,5},{5,4},{6,7},{7,6},{8,16},{9,17},{10,... | collective-permute-start | bytes 62984 | tf_op jit(solution)/shard_map/ppermute | solution.py:366
  7.8 1.6 %collective-permute-start.2 = (f32[336,128]{1,0:T(8,128)S(1)}, f32[336,128]{1,0:T(8,128)S(1)}, u32[]{:S(2)}, u32[]{:S(2)}) collective-permute-start(f32[336,128]{1,0:T(8,128)S(1)} %get-tuple-element.21), channel_id=1, source_target_pairs={{0,1},{1,0},{2,3},{3,2},{4,5},{5,4},{6,7},{7,6},{8,9},{9,8},{10,11... | collective-permute-start | bytes 516104 | tf_op jit(solution)/shard_map/ppermute | solution.py:398
  9.5 5.2 %collective-permute-start.3 = (f32[120,128]{1,0:T(8,128)S(1)}, f32[120,128]{1,0:T(8,128)S(1)}, u32[]{:S(2)}, u32[]{:S(2)}) collective-permute-start(f32[120,128]{1,0:T(8,128)S(1)} %get-tuple-element.23), channel_id=1, source_target_pairs={{0,6},{1,7},{2,4},{3,5},{4,2},{5,3},{6,0},{7,1},{8,14},{9,15},{10,... | collective-permute-start | bytes 184328 | tf_op jit(solution)/shard_map/ppermute | solution.py:410
  12.0 4.2 %collective-permute-start.4 = (f32[120,128]{1,0:T(8,128)S(1)}, f32[120,128]{1,0:T(8,128)S(1)}, u32[]{:S(2)}, u32[]{:S(2)}) collective-permute-start(f32[120,128]{1,0:T(8,128)S(1)} %get-tuple-element.24), channel_id=1, source_target_pairs={{0,4},{1,5},{2,6},{3,7},{4,0},{5,1},{6,2},{7,3},{8,12},{9,13},{10,... | collective-permute-start | bytes 184328 | tf_op jit(solution)/shard_map/ppermute | solution.py:410
  12.5 4.2 %collective-permute-start.5 = (f32[120,128]{1,0:T(8,128)S(1)}, f32[120,128]{1,0:T(8,128)S(1)}, u32[]{:S(2)}, u32[]{:S(2)}) collective-permute-start(f32[120,128]{1,0:T(8,128)S(1)} %get-tuple-element.25), channel_id=1, source_target_pairs={{0,2},{1,3},{2,0},{3,1},{4,6},{5,7},{6,4},{7,5},{8,10},{9,11},{10,... | collective-permute-start | bytes 184328 | tf_op jit(solution)/shard_map/ppermute | solution.py:410

commit v5 on v3

--- a/solution.py
+++ b/solution.py
@@ -11,6 +11,7 @@
 BASINS = 10
 SUB = 8
 LANES = 128
+CUT = 80
 GRANT = 16 * 1024 * 1024
 
 
@@ -54,83 +55,105 @@
             edge[t * levels + k : t * levels + k + 1, :] = rows_buf[t, k, 0:1, :]
 
 
-def block_sums(dims, n, get_v, get_w, shallow, label, put_own, put_shared, put_mean):
-    snapshots, levels, rows, blocks, tiles, dests, per_dest = dims
-    width = BASINS * SUB
-    quantities = 2 * snapshots + 4
-    own_rows = tiles * quantities
-    sub, lane = iota(0), iota(1)
-    diagonal = lane % SUB
-
-    def level_data(k):
+def prepare(dims, rows_of, room):
+    snapshots, levels = dims[:2]
+    get_v, get_w, put_mean = rows_of
+    for k in range(levels):
         v = [get_v(t, k) for t in range(snapshots)]
         w = [get_w(t, k) for t in range(snapshots)]
         mv = sum(v[1:], v[0]) * (1.0 / snapshots)
         mw = sum(w[1:], w[0]) * (1.0 / snapshots)
         cross = sum((a - mv) * (b - mw) for a, b in zip(v, w)) * (1.0 / snapshots)
         put_mean(k, mw)
-        return jnp.concatenate(v + w + [mv * mw, cross, mw, jnp.ones_like(mw)], axis=0)
+        for at, value in enumerate(w + [mv * mw, cross, mw]):
+            room[k, at] = value
+
+
+def multiply(dims, group, get_v, room, shallow, label):
+    snapshots = dims[0]
+    width = BASINS * SUB
+    nothing = jnp.zeros((SUB, LANES), jnp.float32)
+
+    def level_data(k):
+        v = [get_v(t, k) for t in range(snapshots)]
+        rest = [room[k, at] for at in range(snapshots + 3)]
+        return jnp.concatenate(v + rest + [jnp.ones((SUB, LANES), jnp.float32)], axis=0)
 
     def level_hot(k):
         masked = jnp.where(shallow > float(k), label, -1)
         return [jnp.where(masked == b, 1.0, 0.0) for b in range(BASINS)]
 
-    done = [None] * tiles
-    nothing = jnp.zeros((SUB, LANES), jnp.float32)
-    for first in range(0, levels, 2):
-        pair = range(first, min(first + 2, levels))
-        tile, shift = divmod(first * width, LANES)
-        data = jnp.concatenate([level_data(k) for k in pair], axis=1)
-        pad = [nothing] * (shift // SUB)
-        columns = []
-        for k in pair:
-            column = list(pad)
-            for other in pair:
-                column += level_hot(k) if other == k else [nothing] * BASINS
-            columns.append(jnp.concatenate(column, axis=0))
-        hot = jnp.concatenate(columns, axis=1).astype(jnp.bfloat16)
-        height = quantities * SUB
-        parts = []
-        for at in range(0, height, 64):
-            rest = data[at : at + 64]
-            for piece in range(3):
-                parts.append(rest.astype(jnp.bfloat16))
-                if piece < 2:
-                    rest = rest - parts[-1].astype(jnp.float32)
-        dots = lax.dot_general(
-            jnp.concatenate(parts, axis=0),
-            hot,
-            (((1,), (1,)), ((), ())),
-            preferred_element_type=jnp.float32,
-        )
-        sums = []
-        for at in range(0, height, 64):
-            x = [dots[3 * at + p * 64 : 3 * at + (p + 1) * 64] for p in range(3)]
-            sums.append(x[0] + x[1] + x[2])
-        total = jnp.concatenate(sums, axis=0)
-        spare = -total.shape[1] % LANES
-        if spare:
-            total = jnp.concatenate(
-                [total, jnp.zeros((total.shape[0], spare), jnp.float32)], axis=1
-            )
-        for c in range(total.shape[1] // LANES):
-            groups = []
-            for g in range(quantities // SUB):
-                acc = None
-                for s in range(SUB):
-                    q = g * SUB + s
-                    row = jnp.take_along_axis(
-                        total[q * SUB : (q + 1) * SUB, c * LANES : (c + 1) * LANES],
-                        diagonal,
-                        axis=0,
-                        mode="promise_in_bounds",
-                    )
-                    acc = row if acc is None else jnp.where(sub == s, row, acc)
-                if done[tile + c] is not None:
-                    acc = jnp.where(lane < shift, done[tile + c][g * SUB : (g + 1) * SUB], acc)
-                groups.append(acc)
-            done[tile + c] = jnp.concatenate(groups, axis=0)
-    for c in range(tiles):
+    data = jnp.concatenate([level_data(k) for k in group], axis=1)
+    columns = []
+    for k in group:
+        column = [nothing] * (group[0] * width % LANES // SUB)
+        for other in group:
+            column += level_hot(k) if other == k else [nothing] * BASINS
+        columns.append(jnp.concatenate(column, axis=0))
+    hot = jnp.concatenate(columns, axis=1).astype(jnp.bfloat16)
+    exact, height = 2 * snapshots * SUB, data.shape[0]
+    cuts = list(range(0, exact, CUT)) + [exact, height]
+    parts, spans = [], []
+    for at, end in zip(cuts, cuts[1:]):
+        rest = data[at:end]
+        count = 2 if at < exact else 3
+        for piece in range(count):
+            parts.append(rest.astype(jnp.bfloat16))
+            if piece < count - 1:
+                rest = rest - parts[-1].astype(jnp.float32)
+        spans.append((end - at, count))
+    dots = lax.dot_general(
+        jnp.concatenate(parts, axis=0),
+        hot,
+        (((1,), (1,)), ((), ())),
+        preferred_element_type=jnp.float32,
+    )
+    sums, at = [], 0
+    for size, count in spans:
+        x = dots[at : at + size]
+        for piece in range(1, count):
+            x = x + dots[at + piece * size : at + (piece + 1) * size]
+        sums.append(x)
+        at += size * count
+    total = jnp.concatenate(sums, axis=0)
+    spare = -total.shape[1] % LANES
+    if spare:
+        total = jnp.concatenate([total, jnp.zeros((total.shape[0], spare), jnp.float32)], axis=1)
+    return total
+
+
+def extract(dims, group, total, done):
+    quantities = 2 * dims[0] + 4
+    sub, lane = iota(0), iota(1)
+    diagonal = lane % SUB
+    tile, shift = divmod(group[0] * BASINS * SUB, LANES)
+    for c in range(total.shape[1] // LANES):
+        groups = []
+        for g in range(quantities // SUB):
+            acc = None
+            for s in range(SUB):
+                q = g * SUB + s
+                row = jnp.take_along_axis(
+                    total[q * SUB : (q + 1) * SUB, c * LANES : (c + 1) * LANES],
+                    diagonal,
+                    axis=0,
+                    mode="promise_in_bounds",
+                )
+                acc = row if acc is None else jnp.where(sub == s, row, acc)
+            if done[tile + c] is not None:
+                acc = jnp.where(lane < shift, done[tile + c][g * SUB : (g + 1) * SUB], acc)
+            groups.append(acc)
+        done[tile + c] = jnp.concatenate(groups, axis=0)
+
+
+def level_groups(dims):
+    return [tuple(range(k, min(k + 2, dims[1]))) for k in range(0, dims[1], 2)]
+
+
+def store_block(dims, n, done, keep, give):
+    quantities = 2 * dims[0] + 4
+    put_own, put_shared = writers(dims, n, keep, give)
+    for c in range(dims[4]):
         put_own(c, done[c])
         for q in range(2):
             put_shared(c * 2 + q, done[c][quantities - 2 + q : quantities - 1 + q])
@@ -170,17 +193,18 @@
     return put_own, put_shared
 
 
-def inner_kernel(dims, pairs, flow, warmth, flag, floor, basin, *outs):
-    rows, blocks = dims[2:4]
+def inner_kernel(dims, pairs, flow, warmth, flag, floor, basin, *refs):
+    blocks, tiles = dims[3:5]
+    outs, room = refs[:-1], refs[-1]
     keep, give = outs[:2] if pairs else (outs[0], None)
-    mean_warmth, limit, depth_buf = outs[-3:]
-    depth_buf[...] = (flag[...] * floor[...]).astype(jnp.float32)
-
-    def body(n, carry):
-        at = pl.multiple_of(n * SUB, SUB)
-        here, north = pl.ds(at, SUB), pl.ds(at + 1, SUB)
-        shallow = jnp.minimum(depth_buf[here, :], depth_buf[north, :])
-        limit[here, :] = shallow
+    mean_warmth, limit = outs[-2:]
+
+    def span(n):
+        at = n * SUB if isinstance(n, int) else pl.multiple_of(n * SUB, SUB)
+        return pl.ds(at, SUB), pl.ds(at + 1, SUB)
+
+    def rows_of(n):
+        here, north = span(n)
 
         def put_mean(k, value):
             mean_warmth[k, here, :] = value
@@ -191,17 +215,42 @@
         def get_w(t, k):
             return 0.5 * (warmth[t, k, here, :] + warmth[t, k, north, :])
 
-        put_own, put_shared = writers(dims, n, keep, give)
-        block_sums(
-            dims, n, get_v, get_w, shallow, basin[here, :], put_own, put_shared, put_mean
-        )
+        return get_v, get_w, put_mean
+
+    def several(ns):
+        work = []
+        for n in ns:
+            here, north = span(n)
+            depth = (flag[here, :] * floor[here, :]).astype(jnp.float32)
+            upper = (flag[north, :] * floor[north, :]).astype(jnp.float32)
+            shallow = jnp.minimum(depth, upper)
+            limit[here, :] = shallow
+            work.append((n, rows_of(n), shallow, basin[here, :], [None] * tiles))
+        totals = []
+        rooms = [room.at[i] for i in range(7)]
+        for (n, rows, shallow, label, done), r in zip(work, rooms):
+            prepare(dims, rows, r)
+            for group in level_groups(dims):
+                totals.append((group, done, multiply(dims, group, rows[0], r, shallow, label)))
+        for group, done, total in totals:
+            extract(dims, group, total, done)
+
+        for n, _, _, _, done in work:
+            store_block(dims, n, done, keep, give)
+
+    def body(i, carry):
+        several([i * 7 + j for j in range(7)])
         return carry
 
-    lax.fori_loop(0, blocks - 1, body, 0)
+    lax.fori_loop(0, (blocks - 1) // 7, body, 0)
+    rest = (blocks - 1) % 7
+    if rest:
+        several(list(range(blocks - 1 - rest, blocks - 1)))
 
 
 def last_kernel(dims, pairs, odd_halo, even_halo, flow, warmth, flag, floor, basin, *refs):
     snapshots, levels, rows, blocks = dims[:4]
+    refs, room = refs[:-1], refs[-1]
     outs = refs[len(refs) // 2 :]
     keep, give = outs[:2] if pairs else (outs[0], None)
     mean_warmth, limit = outs[-2:]
@@ -231,10 +280,13 @@
         block = warmth[t, k, here, :]
         return 0.5 * (block + north(block, t * levels + k))
 
-    put_own, put_shared = writers(dims, blocks - 1, keep, give)
-    block_sums(
-        dims, blocks - 1, get_v, get_w, shallow, basin[here, :], put_own, put_shared, put_mean
-    )
+    room = room.at[0]
+    prepare(dims, (get_v, get_w, put_mean), room)
+    done = [None] * dims[4]
+    for group in level_groups(dims):
+        total = multiply(dims, group, get_v, room, shallow, basin[here, :])
+        extract(dims, group, total, done)
+    store_block(dims, blocks - 1, done, keep, give)
 
 
 def pair_kernel(dims, keep, came, *outs):
@@ -366,12 +418,13 @@
         pltpu.VMEM((levels, rows, cols), jnp.float32),
         pltpu.VMEM((rows, cols), jnp.float32),
     )
+    room = pltpu.VMEM((7, levels, snapshots + 3, SUB, cols), jnp.float32)
     sums = pl.pallas_call(
         functools.partial(inner_kernel, dims, pairs),
         out_shape=results,
         in_specs=[vmem] * 5,
         out_specs=(vmem,) * len(results),
-        scratch_shapes=[pltpu.VMEM((rows, cols), jnp.float32)],
+        scratch_shapes=[room],
         compiler_params=params,
         name="inner_rows",
     )(flow, warmth, flag, floor, basin)
@@ -381,6 +434,7 @@
         in_specs=[vmem] * (7 + len(results)),
         out_specs=(vmem,) * len(results),
         input_output_aliases={7 + i: i for i in range(len(results))},
+        scratch_shapes=[room],
         compiler_params=params,
         name="last_rows",
     )(*halos[::-1], flow, warmth, flag, floor, basin, *sums)

time: 18.1 us -> 17.4 us (0.961)
  Pallas kernels: 5.25 us -> 3.92 us
  waiting for transfers between devices: 4.73 us -> 5.41 us
    pallas_call x1, Pallas kernels: 2.83 us -> 1.54 us  [shards(): pl.pallas_call(functools.partial(inner_kernel, dims, pairs), out_shape=re...]
    ppermute x3, waiting for transfers between devices: 3.69 us -> 4.08 us  [shards(): lax.ppermute(messages[m], 'lon', [(i, i ^ 2 * m) for i in range(lon)])]
    ppermute x2, waiting for transfers between devices: 0.01 us -> 0.22 us  [shards(): lax.ppermute(edge, ('lat', 'lon'), neighbours(lat, lon, first))]
    ppermute x1, starting transfers between devices: 0.56 us -> 0.36 us  [shards(): came = lax.ppermute(give, 'lon', [(i, i ^ 1) for i in range(lon)])]
  transfers between devices with their start and end apart: 6 -> 6, of which waited for: 4 -> 5; matrix products, arithmetic and copies ran while one was open for 0% -> 0% of each run, Pallas kernels for 16% -> 9%
where the time goes in v5:
time: 17.4 us; the launch traced here: 17.2 us
  starting transfers between devices  7.08 us (41%)
  waiting for transfers between devices  5.41 us (31%)
  Pallas kernels  3.92 us (23%)
  between operations  0.73 us (4%)
    ppermute x3, waiting for transfers between devices, shards(): lax.ppermute(messages[m], 'lon', [(i, i ^ 2 * m) for i in range(lon)])  4.08 us
    ppermute x3, starting transfers between devices, shards(): lax.ppermute(messages[m], 'lon', [(i, i ^ 2 * m) for i in range(lon)])  3.6 us
    ppermute x2, starting transfers between devices, shards(): lax.ppermute(edge, ('lat', 'lon'), neighbours(lat, lon, first))  3.12 us
    pallas_call x1, Pallas kernels, shards(): pl.pallas_call(functools.partial(inner_kernel, dims, pairs), out_shape=re...  1.54 us
    ppermute x1, waiting for transfers between devices, shards(): came = lax.ppermute(give, 'lon', [(i, i ^ 1) for i in range(lon)])  1.11 us
    pallas_call x1, Pallas kernels, shards(): pl.pallas_call(functools.partial(edge_kernel, dims), out_shape=pltpu.VMEM...  1.1 us
    pallas_call x1, Pallas kernels, shards(): pl.pallas_call(functools.partial(finish_kernel, dims, scaling), out_shape...  0.89 us
    ppermute x1, starting transfers between devices, shards(): came = lax.ppermute(give, 'lon', [(i, i ^ 1) for i in range(lon)])  0.36 us
  transfers between devices with their start and end apart: 6, of which 5 were waited for; matrix products, arithmetic and copies ran while one was open for 0% of the time, Pallas kernels for 9%

profile of v5, /device:TPU:0, one launch (start us, length us, event | category | flops | bytes accessed | tf_op | source)
XLA Modules:
  0.0 17.2 jit_solution(11346537623848656660)
XLA Ops:
  0.6 0.0 copy-start.4
  0.6 0.0 copy-start.3
  0.7 0.0 copy-start
  0.7 0.0 copy-start.2
  0.7 0.0 copy-start.1
  0.7 1.1 %edge.1 = f32[41,128]{1,0:T(8,128)S(1)} custom-call(f32[10,4,64,128]{3,2,1,0:T(8,128)} %warmth.5, s32[64,128]{1,0:T(8,128)} %flag.5, s32[64,128]{1,0:T(8,128)} %floor.5), custom_call_target="tpu_custom_call" | custom-call | flops 10000000000 | bytes 8388608 | tf_op jit(solution)/shard_map/edge/pallas_call | solution.py:395
  1.8 3.1 %collective-permute-start.1 = (f32[41,128]{1,0:T(8,128)S(1)}, f32[41,128]{1,0:T(8,128)S(1)}, u32[]{:S(2)}, u32[]{:S(2)}) collective-permute-start(f32[41,128]{1,0:T(8,128)S(1)} %edge.1), channel_id=1, source_target_pairs={{0,8},{1,9},{2,10},{3,11},{4,12},{5,13},{6,14},{7,15},{8,0},{9,1},... | collective-permute-start | bytes 62984 | tf_op jit(solution)/shard_map/ppermute | solution.py:411
  4.9 0.0 collective-permute-start
  4.9 0.0 copy-done.4
  4.9 0.0 copy-done.3
  4.9 0.0 copy-done
  4.9 0.0 copy-done.2
  4.9 0.0 copy-done.1
  4.9 1.5 %inner_rows.1 = (f32[336,128]{1,0:T(8,128)S(1)}, f32[336,128]{1,0:T(8,128)S(1)}, f32[4,64,128]{2,1,0:T(8,128)S(1)}, f32[64,128]{1,0:T(8,128)S(1)}) custom-call(f32[10,4,64,128]{3,2,1,0:T(8,128)S(1)} %copy-done.1, f32[10,4,64,128]{3,2,1,0:T(8,128)S(1)} %copy-done, s32[64,128]{1,0:T(8,128)S(1)} %copy-done.3, s32[64,128]{1,0:T(8,128)S(1)} %copy-done.4, ...), custom_call_target="tpu_custom_call" | custom-call | tf_op jit(solution)/shard_map/inner_rows/pallas_call | solution.py:422
  6.5 0.2 %collective-permute-done.1.even_halo = f32[41,128]{1,0:T(8,128)S(1)} collective-permute-done((f32[41,128]{1,0:T(8,128)S(1)}, f32[41,128]{1,0:T(8,128)S(1)}, u32[]{:S(2)}, u32[]{:S(2)}) %collective-permute-start.1) | collective-permute-done | bytes 21024 | tf_op jit(solution)/shard_map/ppermute | solution.py:411
  6.7 0.0 collective-permute-done.odd_halo
  6.7 0.4 %last_rows.1 = (f32[336,128]{1,0:T(8,128)S(1)}, f32[336,128]{1,0:T(8,128)S(1)}, f32[4,64,128]{2,1,0:T(8,128)S(1)}, f32[64,128]{1,0:T(8,128)S(1)}) custom-call(f32[41,128]{1,0:T(8,128)S(1)} %collective-permute-done.odd_halo, f32[41,128]{1,0:T(8,128)S(1)} %collective-permute-done.1.even_halo, ...), custom_call_target="tpu_custom_call", output_to_operand_aliasing={{0}: (7, {}), {1}: (8, {}), {2}: (9, {}), {3}: (10, {})} | custom-call | tf_op jit(solution)/shard_map/last_rows/pallas_call | solution.py:431
  7.1 0.4 %collective-permute-start.2 = (f32[336,128]{1,0:T(8,128)S(1)}, f32[336,128]{1,0:T(8,128)S(1)}, u32[]{:S(2)}, u32[]{:S(2)}) collective-permute-start(f32[336,128]{1,0:T(8,128)S(1)} %get-tuple-element.21), channel_id=1, source_target_pairs={{0,1},{1,0},{2,3},{3,2},{4,5},{5,4},{6,7},{7,6},{8,9},{9,8},{10,11... | collective-permute-start | bytes 516104 | tf_op jit(solution)/shard_map/ppermute | solution.py:445
  7.4 1.1 %collective-permute-done.2.came = f32[336,128]{1,0:T(8,128)S(1)} collective-permute-done((f32[336,128]{1,0:T(8,128)S(1)}, f32[336,128]{1,0:T(8,128)S(1)}, u32[]{:S(2)}, u32[]{:S(2)}) %collective-permute-start.2) | collective-permute-done | bytes 172064 | tf_op jit(solution)/shard_map/ppermute | solution.py:445
  8.6 3.0 %collective-permute-start.3 = (f32[120,128]{1,0:T(8,128)S(1)}, f32[120,128]{1,0:T(8,128)S(1)}, u32[]{:S(2)}, u32[]{:S(2)}) collective-permute-start(f32[120,128]{1,0:T(8,128)S(1)} %get-tuple-element.23), channel_id=1, source_target_pairs={{0,6},{1,7},{2,4},{3,5},{4,2},{5,3},{6,0},{7,1},{8,14},{9,15},{10,... | collective-permute-start | bytes 184328 | tf_op jit(solution)/shard_map/ppermute | solution.py:457
  11.5 0.5 %collective-permute-start.4 = (f32[120,128]{1,0:T(8,128)S(1)}, f32[120,128]{1,0:T(8,128)S(1)}, u32[]{:S(2)}, u32[]{:S(2)}) collective-permute-start(f32[120,128]{1,0:T(8,128)S(1)} %get-tuple-element.24), channel_id=1, source_target_pairs={{0,4},{1,5},{2,6},{3,7},{4,0},{5,1},{6,2},{7,3},{8,12},{9,13},{10,... | collective-permute-start | bytes 184328 | tf_op jit(solution)/shard_map/ppermute | solution.py:457
  12.0 0.1 collective-permute-start.5
  12.2 1.7 %collective-permute-done.3.refs_1_ = f32[120,128]{1,0:T(8,128)S(1)} collective-permute-done((f32[120,128]{1,0:T(8,128)S(1)}, f32[120,128]{1,0:T(8,128)S(1)}, u32[]{:S(2)}, u32[]{:S(2)}) %collective-permute-start.3) | collective-permute-done | bytes 61472 | tf_op jit(solution)/shard_map/ppermute | solution.py:457
  13.9 1.9 %collective-permute-done.4.refs_2_ = f32[120,128]{1,0:T(8,128)S(1)} collective-permute-done((f32[120,128]{1,0:T(8,128)S(1)}, f32[120,128]{1,0:T(8,128)S(1)}, u32[]{:S(2)}, u32[]{:S(2)}) %collective-permute-start.4) | collective-permute-done | bytes 61472 | tf_op jit(solution)/shard_map/ppermute | solution.py:457
  15.8 0.5 %collective-permute-done.5.refs_3_ = f32[120,128]{1,0:T(8,128)S(1)} collective-permute-done((f32[120,128]{1,0:T(8,128)S(1)}, f32[120,128]{1,0:T(8,128)S(1)}, u32[]{:S(2)}, u32[]{:S(2)}) %collective-permute-start.5) | collective-permute-done | bytes 61472 | tf_op jit(solution)/shard_map/ppermute | solution.py:457
  16.3 0.9 %finish.1 = (f32[4,64,128]{2,1,0:T(8,128)}, f32[4,4,8,10]{3,2,1,0:T(8,128)}) custom-call(f32[120,128]{1,0:T(8,128)S(1)} %get-tuple-element.22.refs_0_, f32[120,128]{1,0:T(8,128)S(1)} %collective-permute-done.3.refs_1_, f32[120,128]{1,0:T(8,128)S(1)} %collective-permute-done.4.refs_2_, f32[120,128]{1,0:T(8,128)S(1)} %collective-permute-done.5.refs_3_, ...), custom_call_target="tpu_custom_call" | custom-call | tf_op jit(solution)/shard_map/finish/pallas_call | solution.py:470
  (1 shorter events, 0.0 us)
Async XLA Ops:
  0.6 4.3 %copy-start.4 = (s32[64,128]{1,0:T(8,128)S(1)}, s32[64,128]{1,0:T(8,128)}, u32[]{:S(2)}) copy-start(s32[64,128]{1,0:T(8,128)} %floor.5) | copy-start | bytes 98308
  0.6 4.3 %copy-start.3 = (s32[64,128]{1,0:T(8,128)S(1)}, s32[64,128]{1,0:T(8,128)}, u32[]{:S(2)}) copy-start(s32[64,128]{1,0:T(8,128)} %flag.5) | copy-start | bytes 98308
  0.7 4.3 %copy-start = (f32[10,4,64,128]{3,2,1,0:T(8,128)S(1)}, f32[10,4,64,128]{3,2,1,0:T(8,128)}, u32[]{:S(2)}) copy-start(f32[10,4,64,128]{3,2,1,0:T(8,128)} %warmth.5) | copy-start | bytes 3932164
  0.7 4.3 %copy-start.2 = (s32[64,128]{1,0:T(8,128)S(1)}, s32[64,128]{1,0:T(8,128)}, u32[]{:S(2)}) copy-start(s32[64,128]{1,0:T(8,128)} %refs_6_.1) | copy-start | bytes 98308
  0.7 4.3 %copy-start.1 = (f32[10,4,64,128]{3,2,1,0:T(8,128)S(1)}, f32[10,4,64,128]{3,2,1,0:T(8,128)}, u32[]{:S(2)}) copy-start(f32[10,4,64,128]{3,2,1,0:T(8,128)} %flow.3) | copy-start | bytes 3932164
  1.8 4.9 %collective-permute-start.1 = (f32[41,128]{1,0:T(8,128)S(1)}, f32[41,128]{1,0:T(8,128)S(1)}, u32[]{:S(2)}, u32[]{:S(2)}) collective-permute-start(f32[41,128]{1,0:T(8,128)S(1)} %edge.1), channel_id=1, source_target_pairs={{0,8},{1,9},{2,10},{3,11},{4,12},{5,13},{6,14},{7,15},{8,0},{9,1},... | collective-permute-start | bytes 62984 | tf_op jit(solution)/shard_map/ppermute | solution.py:411
  4.9 1.8 %collective-permute-start = (f32[41,128]{1,0:T(8,128)S(1)}, f32[41,128]{1,0:T(8,128)S(1)}, u32[]{:S(2)}, u32[]{:S(2)}) collective-permute-start(f32[41,128]{1,0:T(8,128)S(1)} %edge.1), channel_id=1, source_target_pairs={{0,1},{1,0},{2,3},{3,2},{4,5},{5,4},{6,7},{7,6},{8,16},{9,17},{10,... | collective-permute-start | bytes 62984 | tf_op jit(solution)/shard_map/ppermute | solution.py:411
  7.1 1.5 %collective-permute-start.2 = (f32[336,128]{1,0:T(8,128)S(1)}, f32[336,128]{1,0:T(8,128)S(1)}, u32[]{:S(2)}, u32[]{:S(2)}) collective-permute-start(f32[336,128]{1,0:T(8,128)S(1)} %get-tuple-element.21), channel_id=1, source_target_pairs={{0,1},{1,0},{2,3},{3,2},{4,5},{5,4},{6,7},{7,6},{8,9},{9,8},{10,11... | collective-permute-start | bytes 516104 | tf_op jit(solution)/shard_map/ppermute | solution.py:445
  8.6 5.3 %collective-permute-start.3 = (f32[120,128]{1,0:T(8,128)S(1)}, f32[120,128]{1,0:T(8,128)S(1)}, u32[]{:S(2)}, u32[]{:S(2)}) collective-permute-start(f32[120,128]{1,0:T(8,128)S(1)} %get-tuple-element.23), channel_id=1, source_target_pairs={{0,6},{1,7},{2,4},{3,5},{4,2},{5,3},{6,0},{7,1},{8,14},{9,15},{10,... | collective-permute-start | bytes 184328 | tf_op jit(solution)/shard_map/ppermute | solution.py:457
  11.5 4.2 %collective-permute-start.4 = (f32[120,128]{1,0:T(8,128)S(1)}, f32[120,128]{1,0:T(8,128)S(1)}, u32[]{:S(2)}, u32[]{:S(2)}) collective-permute-start(f32[120,128]{1,0:T(8,128)S(1)} %get-tuple-element.24), channel_id=1, source_target_pairs={{0,4},{1,5},{2,6},{3,7},{4,0},{5,1},{6,2},{7,3},{8,12},{9,13},{10,... | collective-permute-start | bytes 184328 | tf_op jit(solution)/shard_map/ppermute | solution.py:457
  12.0 4.2 %collective-permute-start.5 = (f32[120,128]{1,0:T(8,128)S(1)}, f32[120,128]{1,0:T(8,128)S(1)}, u32[]{:S(2)}, u32[]{:S(2)}) collective-permute-start(f32[120,128]{1,0:T(8,128)S(1)} %get-tuple-element.25), channel_id=1, source_target_pairs={{0,2},{1,3},{2,0},{3,1},{4,6},{5,7},{6,4},{7,5},{8,10},{9,11},{10,... | collective-permute-start | bytes 184328 | tf_op jit(solution)/shard_map/ppermute | solution.py:457

commit v6 on v5

--- a/solution.py
+++ b/solution.py
@@ -176,7 +176,8 @@
         if give is None:
             keep[at, :] = value
             return
-        mine = lax.axis_index("lon") % 2 == dest % 2
+        me = lax.axis_index("lon")
+        mine = (me % 2 == dest % 2) == (me // 2 == dest // 2)
 
         @pl.when(mine)
         def _():
@@ -230,7 +231,8 @@
         rooms = [room.at[i] for i in range(7)]
         for (n, rows, shallow, label, done), r in zip(work, rooms):
             prepare(dims, rows, r)
-            for group in level_groups(dims):
+        for group in level_groups(dims):
+            for (n, rows, shallow, label, done), r in zip(work, rooms):
                 totals.append((group, done, multiply(dims, group, rows[0], r, shallow, label)))
         for group, done, total in totals:
             extract(dims, group, total, done)
@@ -359,10 +361,13 @@
     for i in range(lat):
         other = i + 1 if (i - first) % 2 == 0 else i - 1
         for j in range(lon):
-            if 0 <= other < lat:
+            across = j ^ 1 if lon % 2 == 0 else j
+            if not 0 <= other < lat:
+                target = i * lon + across
+            elif other < i:
                 target = other * lon + j
             else:
-                target = i * lon + (j ^ 1 if lon % 2 == 0 else j)
+                target = other * lon + across
             route.append((i * lon + j, target))
     return route
 
@@ -454,7 +459,7 @@
             name="pair_sums",
         )(keep, came)
         got = messages[:1] + tuple(
-            lax.ppermute(messages[m], "lon", [(i, i ^ (2 * m)) for i in range(lon)])
+            lax.ppermute(messages[m], "lon", [(i, i ^ (2 * m + 1)) for i in range(lon)])
             for m in reversed(range(1, chips))
         )
     else:

time: 17.4 us -> 16.8 us (0.966)
  starting transfers between devices: 7.08 us -> 6.61 us
    ppermute x1, starting transfers between devices: 0.36 us -> 0.07 us  [shards(): came = lax.ppermute(give, 'lon', [(i, i ^ 1) for i in range(lon)])]
    ppermute x1, waiting for transfers between devices: 1.11 us -> 1.39 us  [shards(): came = lax.ppermute(give, 'lon', [(i, i ^ 1) for i in range(lon)])]
    ppermute x3, starting transfers between devices: 3.6 us -> 3.32 us  [shards(): lax.ppermute(messages[m], 'lon', [(i, i ^ 2 * m + 1) for i in range(lon)])]
    ppermute x3, waiting for transfers between devices: 4.08 us -> 3.84 us  [shards(): lax.ppermute(messages[m], 'lon', [(i, i ^ 2 * m + 1) for i in range(lon)])]
  transfers between devices with their start and end apart: 6 -> 6, of which waited for: 5 -> 5; matrix products, arithmetic and copies ran while one was open for 0% -> 0% of each run, Pallas kernels for 9% -> 8%
where the time goes in v6:
time: 16.8 us; the launch traced here: 16.6 us
  starting transfers between devices  6.61 us (39%)
  waiting for transfers between devices  5.49 us (33%)
  Pallas kernels  3.78 us (22%)
  between operations  0.72 us (4%)
    ppermute x3, waiting for transfers between devices, shards(): lax.ppermute(messages[m], 'lon', [(i, i ^ 2 * m + 1) for i in range(lon)])  3.84 us
    ppermute x3, starting transfers between devices, shards(): lax.ppermute(messages[m], 'lon', [(i, i ^ 2 * m + 1) for i in range(lon)])  3.32 us
    ppermute x2, starting transfers between devices, shards(): lax.ppermute(edge, ('lat', 'lon'), neighbours(lat, lon, first))  3.22 us
    pallas_call x1, Pallas kernels, shards(): pl.pallas_call(functools.partial(inner_kernel, dims, pairs), out_shape=re...  1.41 us
    ppermute x1, waiting for transfers between devices, shards(): came = lax.ppermute(give, 'lon', [(i, i ^ 1) for i in range(lon)])  1.39 us
    pallas_call x1, Pallas kernels, shards(): pl.pallas_call(functools.partial(edge_kernel, dims), out_shape=pltpu.VMEM...  1.1 us
    pallas_call x1, Pallas kernels, shards(): pl.pallas_call(functools.partial(finish_kernel, dims, scaling), out_shape...  0.89 us
    pallas_call x1, Pallas kernels, shards(): pl.pallas_call(functools.partial(last_kernel, dims, pairs), out_shape=res...  0.35 us
  transfers between devices with their start and end apart: 6, of which 5 were waited for; matrix products, arithmetic and copies ran while one was open for 0% of the time, Pallas kernels for 8%

profile of v6, /device:TPU:0, one launch (start us, length us, event | category | flops | bytes accessed | tf_op | source)
XLA Modules:
  0.0 16.6 jit_solution(7914819641877480806)
XLA Ops:
  0.6 0.0 copy-start.4
  0.6 0.0 copy-start.3
  0.7 0.0 copy-start
  0.7 0.0 copy-start.2
  0.7 0.0 copy-start.1
  0.7 1.1 %edge.1 = f32[41,128]{1,0:T(8,128)S(1)} custom-call(f32[10,4,64,128]{3,2,1,0:T(8,128)} %warmth.5, s32[64,128]{1,0:T(8,128)} %flag.5, s32[64,128]{1,0:T(8,128)} %floor.5), custom_call_target="tpu_custom_call" | custom-call | flops 10000000000 | bytes 8388608 | tf_op jit(solution)/shard_map/edge/pallas_call | solution.py:400
  1.8 2.5 %collective-permute-start.1 = (f32[41,128]{1,0:T(8,128)S(1)}, f32[41,128]{1,0:T(8,128)S(1)}, u32[]{:S(2)}, u32[]{:S(2)}) collective-permute-start(f32[41,128]{1,0:T(8,128)S(1)} %edge.1), channel_id=1, source_target_pairs={{0,9},{1,8},{2,11},{3,10},{4,13},{5,12},{6,15},{7,14},{8,0},{9,1},... | collective-permute-start | bytes 62984 | tf_op jit(solution)/shard_map/ppermute | solution.py:416
  4.3 0.7 %collective-permute-start = (f32[41,128]{1,0:T(8,128)S(1)}, f32[41,128]{1,0:T(8,128)S(1)}, u32[]{:S(2)}, u32[]{:S(2)}) collective-permute-start(f32[41,128]{1,0:T(8,128)S(1)} %edge.1), channel_id=1, source_target_pairs={{0,1},{1,0},{2,3},{3,2},{4,5},{5,4},{6,7},{7,6},{8,17},{9,16},{10,... | collective-permute-start | bytes 62984 | tf_op jit(solution)/shard_map/ppermute | solution.py:416
  5.0 0.0 copy-done.4
  5.0 0.0 copy-done.3
  5.0 0.0 copy-done
  5.0 0.0 copy-done.2
  5.0 0.0 copy-done.1
  5.0 1.4 %inner_rows.1 = (f32[336,128]{1,0:T(8,128)S(1)}, f32[336,128]{1,0:T(8,128)S(1)}, f32[4,64,128]{2,1,0:T(8,128)S(1)}, f32[64,128]{1,0:T(8,128)S(1)}) custom-call(f32[10,4,64,128]{3,2,1,0:T(8,128)S(1)} %copy-done.1, f32[10,4,64,128]{3,2,1,0:T(8,128)S(1)} %copy-done, s32[64,128]{1,0:T(8,128)S(1)} %copy-done.3, s32[64,128]{1,0:T(8,128)S(1)} %copy-done.4, ...), custom_call_target="tpu_custom_call" | custom-call | tf_op jit(solution)/shard_map/inner_rows/pallas_call | solution.py:427
  6.5 0.2 %collective-permute-done.1.even_halo = f32[41,128]{1,0:T(8,128)S(1)} collective-permute-done((f32[41,128]{1,0:T(8,128)S(1)}, f32[41,128]{1,0:T(8,128)S(1)}, u32[]{:S(2)}, u32[]{:S(2)}) %collective-permute-start.1) | collective-permute-done | bytes 21024 | tf_op jit(solution)/shard_map/ppermute | solution.py:416
  6.7 0.0 collective-permute-done.odd_halo
  6.7 0.4 %last_rows.1 = (f32[336,128]{1,0:T(8,128)S(1)}, f32[336,128]{1,0:T(8,128)S(1)}, f32[4,64,128]{2,1,0:T(8,128)S(1)}, f32[64,128]{1,0:T(8,128)S(1)}) custom-call(f32[41,128]{1,0:T(8,128)S(1)} %collective-permute-done.odd_halo, f32[41,128]{1,0:T(8,128)S(1)} %collective-permute-done.1.even_halo, ...), custom_call_target="tpu_custom_call", output_to_operand_aliasing={{0}: (7, {}), {1}: (8, {}), {2}: (9, {}), {3}: (10, {})} | custom-call | tf_op jit(solution)/shard_map/last_rows/pallas_call | solution.py:436
  7.1 0.1 collective-permute-start.2
  7.1 1.4 %collective-permute-done.2.came = f32[336,128]{1,0:T(8,128)S(1)} collective-permute-done((f32[336,128]{1,0:T(8,128)S(1)}, f32[336,128]{1,0:T(8,128)S(1)}, u32[]{:S(2)}, u32[]{:S(2)}) %collective-permute-start.2) | collective-permute-done | bytes 172064 | tf_op jit(solution)/shard_map/ppermute | solution.py:450
  8.6 2.7 %collective-permute-start.3 = (f32[120,128]{1,0:T(8,128)S(1)}, f32[120,128]{1,0:T(8,128)S(1)}, u32[]{:S(2)}, u32[]{:S(2)}) collective-permute-start(f32[120,128]{1,0:T(8,128)S(1)} %get-tuple-element.23), channel_id=1, source_target_pairs={{0,7},{1,6},{2,5},{3,4},{4,3},{5,2},{6,1},{7,0},{8,15},{9,14},{10,... | collective-permute-start | bytes 184328 | tf_op jit(solution)/shard_map/ppermute | solution.py:462
  11.3 0.5 %collective-permute-start.4 = (f32[120,128]{1,0:T(8,128)S(1)}, f32[120,128]{1,0:T(8,128)S(1)}, u32[]{:S(2)}, u32[]{:S(2)}) collective-permute-start(f32[120,128]{1,0:T(8,128)S(1)} %get-tuple-element.24), channel_id=1, source_target_pairs={{0,5},{1,4},{2,7},{3,6},{4,1},{5,0},{6,3},{7,2},{8,13},{9,12},{10,... | collective-permute-start | bytes 184328 | tf_op jit(solution)/shard_map/ppermute | solution.py:462
  11.8 0.1 collective-permute-start.5
  11.9 1.8 %collective-permute-done.3.refs_1_ = f32[120,128]{1,0:T(8,128)S(1)} collective-permute-done((f32[120,128]{1,0:T(8,128)S(1)}, f32[120,128]{1,0:T(8,128)S(1)}, u32[]{:S(2)}, u32[]{:S(2)}) %collective-permute-start.3) | collective-permute-done | bytes 61472 | tf_op jit(solution)/shard_map/ppermute | solution.py:462
  13.7 1.3 %collective-permute-done.4.refs_2_ = f32[120,128]{1,0:T(8,128)S(1)} collective-permute-done((f32[120,128]{1,0:T(8,128)S(1)}, f32[120,128]{1,0:T(8,128)S(1)}, u32[]{:S(2)}, u32[]{:S(2)}) %collective-permute-start.4) | collective-permute-done | bytes 61472 | tf_op jit(solution)/shard_map/ppermute | solution.py:462
  15.0 0.7 %collective-permute-done.5.refs_3_ = f32[120,128]{1,0:T(8,128)S(1)} collective-permute-done((f32[120,128]{1,0:T(8,128)S(1)}, f32[120,128]{1,0:T(8,128)S(1)}, u32[]{:S(2)}, u32[]{:S(2)}) %collective-permute-start.5) | collective-permute-done | bytes 61472 | tf_op jit(solution)/shard_map/ppermute | solution.py:462
  15.7 0.9 %finish.1 = (f32[4,64,128]{2,1,0:T(8,128)}, f32[4,4,8,10]{3,2,1,0:T(8,128)}) custom-call(f32[120,128]{1,0:T(8,128)S(1)} %get-tuple-element.22.refs_0_, f32[120,128]{1,0:T(8,128)S(1)} %collective-permute-done.3.refs_1_, f32[120,128]{1,0:T(8,128)S(1)} %collective-permute-done.4.refs_2_, f32[120,128]{1,0:T(8,128)S(1)} %collective-permute-done.5.refs_3_, ...), custom_call_target="tpu_custom_call" | custom-call | tf_op jit(solution)/shard_map/finish/pallas_call | solution.py:475
  (1 shorter events, 0.0 us)
Async XLA Ops:
  0.6 4.4 %copy-start.4 = (s32[64,128]{1,0:T(8,128)S(1)}, s32[64,128]{1,0:T(8,128)}, u32[]{:S(2)}) copy-start(s32[64,128]{1,0:T(8,128)} %floor.5) | copy-start | bytes 98308
  0.6 4.4 %copy-start.3 = (s32[64,128]{1,0:T(8,128)S(1)}, s32[64,128]{1,0:T(8,128)}, u32[]{:S(2)}) copy-start(s32[64,128]{1,0:T(8,128)} %flag.5) | copy-start | bytes 98308
  0.7 4.4 %copy-start = (f32[10,4,64,128]{3,2,1,0:T(8,128)S(1)}, f32[10,4,64,128]{3,2,1,0:T(8,128)}, u32[]{:S(2)}) copy-start(f32[10,4,64,128]{3,2,1,0:T(8,128)} %warmth.5) | copy-start | bytes 3932164
  0.7 4.4 %copy-start.2 = (s32[64,128]{1,0:T(8,128)S(1)}, s32[64,128]{1,0:T(8,128)}, u32[]{:S(2)}) copy-start(s32[64,128]{1,0:T(8,128)} %refs_6_.1) | copy-start | bytes 98308
  0.7 4.4 %copy-start.1 = (f32[10,4,64,128]{3,2,1,0:T(8,128)S(1)}, f32[10,4,64,128]{3,2,1,0:T(8,128)}, u32[]{:S(2)}) copy-start(f32[10,4,64,128]{3,2,1,0:T(8,128)} %flow.3) | copy-start | bytes 3932164
  1.8 4.9 %collective-permute-start.1 = (f32[41,128]{1,0:T(8,128)S(1)}, f32[41,128]{1,0:T(8,128)S(1)}, u32[]{:S(2)}, u32[]{:S(2)}) collective-permute-start(f32[41,128]{1,0:T(8,128)S(1)} %edge.1), channel_id=1, source_target_pairs={{0,9},{1,8},{2,11},{3,10},{4,13},{5,12},{6,15},{7,14},{8,0},{9,1},... | collective-permute-start | bytes 62984 | tf_op jit(solution)/shard_map/ppermute | solution.py:416
  4.3 2.4 %collective-permute-start = (f32[41,128]{1,0:T(8,128)S(1)}, f32[41,128]{1,0:T(8,128)S(1)}, u32[]{:S(2)}, u32[]{:S(2)}) collective-permute-start(f32[41,128]{1,0:T(8,128)S(1)} %edge.1), channel_id=1, source_target_pairs={{0,1},{1,0},{2,3},{3,2},{4,5},{5,4},{6,7},{7,6},{8,17},{9,16},{10,... | collective-permute-start | bytes 62984 | tf_op jit(solution)/shard_map/ppermute | solution.py:416
  7.1 1.5 %collective-permute-start.2 = (f32[336,128]{1,0:T(8,128)S(1)}, f32[336,128]{1,0:T(8,128)S(1)}, u32[]{:S(2)}, u32[]{:S(2)}) collective-permute-start(f32[336,128]{1,0:T(8,128)S(1)} %get-tuple-element.21), channel_id=1, source_target_pairs={{0,1},{1,0},{2,3},{3,2},{4,5},{5,4},{6,7},{7,6},{8,9},{9,8},{10,11... | collective-permute-start | bytes 516104 | tf_op jit(solution)/shard_map/ppermute | solution.py:450
  8.6 5.1 %collective-permute-start.3 = (f32[120,128]{1,0:T(8,128)S(1)}, f32[120,128]{1,0:T(8,128)S(1)}, u32[]{:S(2)}, u32[]{:S(2)}) collective-permute-start(f32[120,128]{1,0:T(8,128)S(1)} %get-tuple-element.23), channel_id=1, source_target_pairs={{0,7},{1,6},{2,5},{3,4},{4,3},{5,2},{6,1},{7,0},{8,15},{9,14},{10,... | collective-permute-start | bytes 184328 | tf_op jit(solution)/shard_map/ppermute | solution.py:462
  11.3 3.8 %collective-permute-start.4 = (f32[120,128]{1,0:T(8,128)S(1)}, f32[120,128]{1,0:T(8,128)S(1)}, u32[]{:S(2)}, u32[]{:S(2)}) collective-permute-start(f32[120,128]{1,0:T(8,128)S(1)} %get-tuple-element.24), channel_id=1, source_target_pairs={{0,5},{1,4},{2,7},{3,6},{4,1},{5,0},{6,3},{7,2},{8,13},{9,12},{10,... | collective-permute-start | bytes 184328 | tf_op jit(solution)/shard_map/ppermute | solution.py:462
  11.8 4.0 %collective-permute-start.5 = (f32[120,128]{1,0:T(8,128)S(1)}, f32[120,128]{1,0:T(8,128)S(1)}, u32[]{:S(2)}, u32[]{:S(2)}) collective-permute-start(f32[120,128]{1,0:T(8,128)S(1)} %get-tuple-element.25), channel_id=1, source_target_pairs={{0,3},{1,2},{2,1},{3,0},{4,7},{5,6},{6,5},{7,4},{8,11},{9,10},{10,... | collective-permute-start | bytes 184328 | tf_op jit(solution)/shard_map/ppermute | solution.py:462

commit v7 on v6

--- a/solution.py
+++ b/solution.py
@@ -291,19 +291,38 @@
     store_block(dims, blocks - 1, done, keep, give)
 
 
+def spare_lanes(dims):
+    snapshots, levels, rows, blocks, tiles, dests, per_dest = dims
+    quantities = 2 * snapshots + 4
+    used = levels * BASINS * SUB - (tiles - 1) * LANES
+    fits = 2 * used <= LANES and 2 * blocks <= quantities - 4 and blocks % SUB == 0
+    return fits, used, (tiles - 1) * quantities
+
+
 def pair_kernel(dims, keep, came, *outs):
     tiles, per_dest = dims[4], dims[6]
     own_rows = per_dest * tiles * (2 * dims[0] + 4)
     chips = len(outs)
     shared = chips * own_rows
     chip = lax.axis_index("lon") // 2
+    common = keep[shared:, :] + came[shared:, :]
+    fits, used, start = spare_lanes(dims)
     for offset, out in enumerate(outs):
         at = pl.multiple_of((chip ^ offset) * own_rows, SUB)
-        out[0:own_rows, :] = keep[pl.ds(at, own_rows), :] + came[pl.ds(at, own_rows), :]
-        out[own_rows:, :] = keep[shared:, :] + came[shared:, :]
-
-
-def finish_kernel(dims, scaling, *refs):
+        own = keep[pl.ds(at, own_rows), :] + came[pl.ds(at, own_rows), :]
+        out[0:own_rows, :] = own
+        if fits:
+            rest = out.shape[0] - own_rows
+            size = common.shape[0] - rest
+            moved = pltpu.roll(common[rest:], used, 1)
+            lane = lax.broadcasted_iota(jnp.int32, moved.shape, 1)
+            out[start : start + size, :] = jnp.where(lane < used, own[start : start + size], moved)
+            out[own_rows:, :] = common[:rest]
+        else:
+            out[own_rows:, :] = common
+
+
+def finish_kernel(dims, scaling, packed, *refs):
     mean_warmth, limit, basin, eddy, transport = refs[-5:]
     snapshots, levels, rows, blocks, tiles, dests, per_dest = dims
     width = BASINS * SUB
@@ -311,12 +330,16 @@
     own_rows = tiles * quantities
     sub, lane = iota(0), iota(1)
     got = refs[:-5]
-    if len(got) == 1:
+    if len(got[0].shape) == 3:
         got = [got[0].at[d] for d in range(got[0].shape[0])]
     mine = got[0][...]
     for part in got[1:]:
         mine = mine + part[...]
     shared = mine[per_dest * own_rows :]
+    if packed:
+        _, used, start = spare_lanes(dims)
+        beside = mine[start : start + 2 * blocks]
+        shared = jnp.concatenate([shared, pltpu.roll(beside, LANES - used, 1)], axis=0)
     bar = []
     for c in range(tiles):
         at = c * 2 * blocks
@@ -448,7 +471,8 @@
     if pairs:
         keep, give = sums[:2]
         came = lax.ppermute(give, "lon", [(i, i ^ 1) for i in range(lon)])
-        message = pltpu.VMEM((own_rows + shared_rows, LANES), jnp.float32)
+        beside = 2 * blocks if spare_lanes(dims)[0] else 0
+        message = pltpu.VMEM((own_rows + shared_rows - beside, LANES), jnp.float32)
         chips = lon // 2
         messages = pl.pallas_call(
             functools.partial(pair_kernel, dims),
@@ -473,7 +497,7 @@
         got = (lax.all_to_all(sent, "lon", 0, 0),)
 
     eddy, transport = pl.pallas_call(
-        functools.partial(finish_kernel, dims, scaling),
+        functools.partial(finish_kernel, dims, scaling, pairs and spare_lanes(dims)[0]),
         out_shape=(
             jax.ShapeDtypeStruct((levels, rows, cols), jnp.float32),
             jax.ShapeDtypeStruct((4, levels, per_dest * SUB, BASINS), jnp.float32),

time: 16.8 us -> 16.6 us (0.988)
  waiting for transfers between devices: 5.49 us -> 5.31 us
    ppermute x3, waiting for transfers between devices: 3.84 us -> 3.67 us  [shards(): lax.ppermute(messages[m], 'lon', [(i, i ^ 2 * m + 1) for i in range(lon)])]
  transfers between devices with their start and end apart: 6 -> 6, of which waited for: 5 -> 5; matrix products, arithmetic and copies ran while one was open for 0% -> 0% of each run, Pallas kernels for 8% -> 9%
where the time goes in v7:
time: 16.6 us; the launch traced here: 16.5 us
  starting transfers between devices  6.57 us (40%)
  waiting for transfers between devices  5.31 us (32%)
  Pallas kernels  3.87 us (23%)
  between operations  0.72 us (4%)
    ppermute x3, waiting for transfers between devices, shards(): lax.ppermute(messages[m], 'lon', [(i, i ^ 2 * m + 1) for i in range(lon)])  3.67 us
    ppermute x3, starting transfers between devices, shards(): lax.ppermute(messages[m], 'lon', [(i, i ^ 2 * m + 1) for i in range(lon)])  3.28 us
    ppermute x2, starting transfers between devices, shards(): lax.ppermute(edge, ('lat', 'lon'), neighbours(lat, lon, first))  3.22 us
    pallas_call x1, Pallas kernels, shards(): pl.pallas_call(functools.partial(inner_kernel, dims, pairs), out_shape=re...  1.41 us
    ppermute x1, waiting for transfers between devices, shards(): came = lax.ppermute(give, 'lon', [(i, i ^ 1) for i in range(lon)])  1.39 us
    pallas_call x1, Pallas kernels, shards(): pl.pallas_call(functools.partial(edge_kernel, dims), out_shape=pltpu.VMEM...  1.1 us
    pallas_call x1, Pallas kernels, shards(): pl.pallas_call(functools.partial(finish_kernel, dims, scaling, pairs and...  0.93 us
    pallas_call x1, Pallas kernels, shards(): pl.pallas_call(functools.partial(last_kernel, dims, pairs), out_shape=res...  0.35 us
  transfers between devices with their start and end apart: 6, of which 5 were waited for; matrix products, arithmetic and copies ran while one was open for 0% of the time, Pallas kernels for 9%

profile of v7, /device:TPU:0, one launch (start us, length us, event | category | flops | bytes accessed | tf_op | source)
XLA Modules:
  0.0 16.5 jit_solution(3786180185879940647)
XLA Ops:
  0.6 0.0 copy-start.4
  0.6 0.0 copy-start.3
  0.7 0.0 copy-start
  0.7 0.0 copy-start.2
  0.7 0.0 copy-start.1
  0.7 1.1 %edge.1 = f32[41,128]{1,0:T(8,128)S(1)} custom-call(f32[10,4,64,128]{3,2,1,0:T(8,128)} %warmth.5, s32[64,128]{1,0:T(8,128)} %flag.5, s32[64,128]{1,0:T(8,128)} %floor.5), custom_call_target="tpu_custom_call" | custom-call | flops 10000000000 | bytes 8388608 | tf_op jit(solution)/shard_map/edge/pallas_call | solution.py:423
  1.8 2.5 %collective-permute-start.1 = (f32[41,128]{1,0:T(8,128)S(1)}, f32[41,128]{1,0:T(8,128)S(1)}, u32[]{:S(2)}, u32[]{:S(2)}) collective-permute-start(f32[41,128]{1,0:T(8,128)S(1)} %edge.1), channel_id=1, source_target_pairs={{0,9},{1,8},{2,11},{3,10},{4,13},{5,12},{6,15},{7,14},{8,0},{9,1},... | collective-permute-start | bytes 62984 | tf_op jit(solution)/shard_map/ppermute | solution.py:439
  4.3 0.7 %collective-permute-start = (f32[41,128]{1,0:T(8,128)S(1)}, f32[41,128]{1,0:T(8,128)S(1)}, u32[]{:S(2)}, u32[]{:S(2)}) collective-permute-start(f32[41,128]{1,0:T(8,128)S(1)} %edge.1), channel_id=1, source_target_pairs={{0,1},{1,0},{2,3},{3,2},{4,5},{5,4},{6,7},{7,6},{8,17},{9,16},{10,... | collective-permute-start | bytes 62984 | tf_op jit(solution)/shard_map/ppermute | solution.py:439
  5.0 0.0 copy-done.4
  5.0 0.0 copy-done.3
  5.0 0.0 copy-done
  5.0 0.0 copy-done.2
  5.0 0.0 copy-done.1
  5.0 1.4 %inner_rows.1 = (f32[336,128]{1,0:T(8,128)S(1)}, f32[336,128]{1,0:T(8,128)S(1)}, f32[4,64,128]{2,1,0:T(8,128)S(1)}, f32[64,128]{1,0:T(8,128)S(1)}) custom-call(f32[10,4,64,128]{3,2,1,0:T(8,128)S(1)} %copy-done.1, f32[10,4,64,128]{3,2,1,0:T(8,128)S(1)} %copy-done, s32[64,128]{1,0:T(8,128)S(1)} %copy-done.3, s32[64,128]{1,0:T(8,128)S(1)} %copy-done.4, ...), custom_call_target="tpu_custom_call" | custom-call | tf_op jit(solution)/shard_map/inner_rows/pallas_call | solution.py:450
  6.5 0.2 %collective-permute-done.1.even_halo = f32[41,128]{1,0:T(8,128)S(1)} collective-permute-done((f32[41,128]{1,0:T(8,128)S(1)}, f32[41,128]{1,0:T(8,128)S(1)}, u32[]{:S(2)}, u32[]{:S(2)}) %collective-permute-start.1) | collective-permute-done | bytes 21024 | tf_op jit(solution)/shard_map/ppermute | solution.py:439
  6.7 0.0 collective-permute-done.odd_halo
  6.7 0.4 %last_rows.1 = (f32[336,128]{1,0:T(8,128)S(1)}, f32[336,128]{1,0:T(8,128)S(1)}, f32[4,64,128]{2,1,0:T(8,128)S(1)}, f32[64,128]{1,0:T(8,128)S(1)}) custom-call(f32[41,128]{1,0:T(8,128)S(1)} %collective-permute-done.odd_halo, f32[41,128]{1,0:T(8,128)S(1)} %collective-permute-done.1.even_halo, ...), custom_call_target="tpu_custom_call", output_to_operand_aliasing={{0}: (7, {}), {1}: (8, {}), {2}: (9, {}), {3}: (10, {})} | custom-call | tf_op jit(solution)/shard_map/last_rows/pallas_call | solution.py:459
  7.1 0.1 collective-permute-start.2
  7.1 1.4 %collective-permute-done.2.came = f32[336,128]{1,0:T(8,128)S(1)} collective-permute-done((f32[336,128]{1,0:T(8,128)S(1)}, f32[336,128]{1,0:T(8,128)S(1)}, u32[]{:S(2)}, u32[]{:S(2)}) %collective-permute-start.2) | collective-permute-done | bytes 172064 | tf_op jit(solution)/shard_map/ppermute | solution.py:473
  8.5 0.1 pair_sums.1
  8.6 2.7 %collective-permute-start.3 = (f32[104,128]{1,0:T(8,128)S(1)}, f32[104,128]{1,0:T(8,128)S(1)}, u32[]{:S(2)}, u32[]{:S(2)}) collective-permute-start(f32[104,128]{1,0:T(8,128)S(1)} %get-tuple-element.23), channel_id=1, source_target_pairs={{0,7},{1,6},{2,5},{3,4},{4,3},{5,2},{6,1},{7,0},{8,15},{9,14},{10,... | collective-permute-start | bytes 159752 | tf_op jit(solution)/shard_map/ppermute | solution.py:486
  11.3 0.5 %collective-permute-start.4 = (f32[104,128]{1,0:T(8,128)S(1)}, f32[104,128]{1,0:T(8,128)S(1)}, u32[]{:S(2)}, u32[]{:S(2)}) collective-permute-start(f32[104,128]{1,0:T(8,128)S(1)} %get-tuple-element.24), channel_id=1, source_target_pairs={{0,5},{1,4},{2,7},{3,6},{4,1},{5,0},{6,3},{7,2},{8,13},{9,12},{10,... | collective-permute-start | bytes 159752 | tf_op jit(solution)/shard_map/ppermute | solution.py:486
  11.8 0.1 collective-permute-start.5
  11.9 1.6 %collective-permute-done.3.refs_1_ = f32[104,128]{1,0:T(8,128)S(1)} collective-permute-done((f32[104,128]{1,0:T(8,128)S(1)}, f32[104,128]{1,0:T(8,128)S(1)}, u32[]{:S(2)}, u32[]{:S(2)}) %collective-permute-start.3) | collective-permute-done | bytes 53280 | tf_op jit(solution)/shard_map/ppermute | solution.py:486
  13.5 1.4 %collective-permute-done.4.refs_2_ = f32[104,128]{1,0:T(8,128)S(1)} collective-permute-done((f32[104,128]{1,0:T(8,128)S(1)}, f32[104,128]{1,0:T(8,128)S(1)}, u32[]{:S(2)}, u32[]{:S(2)}) %collective-permute-start.4) | collective-permute-done | bytes 53280 | tf_op jit(solution)/shard_map/ppermute | solution.py:486
  14.9 0.7 %collective-permute-done.5.refs_3_ = f32[104,128]{1,0:T(8,128)S(1)} collective-permute-done((f32[104,128]{1,0:T(8,128)S(1)}, f32[104,128]{1,0:T(8,128)S(1)}, u32[]{:S(2)}, u32[]{:S(2)}) %collective-permute-start.5) | collective-permute-done | bytes 53280 | tf_op jit(solution)/shard_map/ppermute | solution.py:486
  15.6 0.9 %finish.1 = (f32[4,64,128]{2,1,0:T(8,128)}, f32[4,4,8,10]{3,2,1,0:T(8,128)}) custom-call(f32[104,128]{1,0:T(8,128)S(1)} %get-tuple-element.22.refs_0_, f32[104,128]{1,0:T(8,128)S(1)} %collective-permute-done.3.refs_1_, f32[104,128]{1,0:T(8,128)S(1)} %collective-permute-done.4.refs_2_, f32[104,128]{1,0:T(8,128)S(1)} %collective-permute-done.5.refs_3_, ...), custom_call_target="tpu_custom_call" | custom-call | tf_op jit(solution)/shard_map/finish/pallas_call | solution.py:499
Async XLA Ops:
  0.6 4.4 %copy-start.4 = (s32[64,128]{1,0:T(8,128)S(1)}, s32[64,128]{1,0:T(8,128)}, u32[]{:S(2)}) copy-start(s32[64,128]{1,0:T(8,128)} %floor.5) | copy-start | bytes 98308
  0.6 4.4 %copy-start.3 = (s32[64,128]{1,0:T(8,128)S(1)}, s32[64,128]{1,0:T(8,128)}, u32[]{:S(2)}) copy-start(s32[64,128]{1,0:T(8,128)} %flag.5) | copy-start | bytes 98308
  0.7 4.4 %copy-start = (f32[10,4,64,128]{3,2,1,0:T(8,128)S(1)}, f32[10,4,64,128]{3,2,1,0:T(8,128)}, u32[]{:S(2)}) copy-start(f32[10,4,64,128]{3,2,1,0:T(8,128)} %warmth.5) | copy-start | bytes 3932164
  0.7 4.4 %copy-start.2 = (s32[64,128]{1,0:T(8,128)S(1)}, s32[64,128]{1,0:T(8,128)}, u32[]{:S(2)}) copy-start(s32[64,128]{1,0:T(8,128)} %refs_6_.1) | copy-start | bytes 98308
  0.7 4.4 %copy-start.1 = (f32[10,4,64,128]{3,2,1,0:T(8,128)S(1)}, f32[10,4,64,128]{3,2,1,0:T(8,128)}, u32[]{:S(2)}) copy-start(f32[10,4,64,128]{3,2,1,0:T(8,128)} %flow.3) | copy-start | bytes 3932164
  1.8 4.9 %collective-permute-start.1 = (f32[41,128]{1,0:T(8,128)S(1)}, f32[41,128]{1,0:T(8,128)S(1)}, u32[]{:S(2)}, u32[]{:S(2)}) collective-permute-start(f32[41,128]{1,0:T(8,128)S(1)} %edge.1), channel_id=1, source_target_pairs={{0,9},{1,8},{2,11},{3,10},{4,13},{5,12},{6,15},{7,14},{8,0},{9,1},... | collective-permute-start | bytes 62984 | tf_op jit(solution)/shard_map/ppermute | solution.py:439
  4.3 2.4 %collective-permute-start = (f32[41,128]{1,0:T(8,128)S(1)}, f32[41,128]{1,0:T(8,128)S(1)}, u32[]{:S(2)}, u32[]{:S(2)}) collective-permute-start(f32[41,128]{1,0:T(8,128)S(1)} %edge.1), channel_id=1, source_target_pairs={{0,1},{1,0},{2,3},{3,2},{4,5},{5,4},{6,7},{7,6},{8,17},{9,16},{10,... | collective-permute-start | bytes 62984 | tf_op jit(solution)/shard_map/ppermute | solution.py:439
  7.1 1.5 %collective-permute-start.2 = (f32[336,128]{1,0:T(8,128)S(1)}, f32[336,128]{1,0:T(8,128)S(1)}, u32[]{:S(2)}, u32[]{:S(2)}) collective-permute-start(f32[336,128]{1,0:T(8,128)S(1)} %get-tuple-element.21), channel_id=1, source_target_pairs={{0,1},{1,0},{2,3},{3,2},{4,5},{5,4},{6,7},{7,6},{8,9},{9,8},{10,11... | collective-permute-start | bytes 516104 | tf_op jit(solution)/shard_map/ppermute | solution.py:473
  8.6 4.9 %collective-permute-start.3 = (f32[104,128]{1,0:T(8,128)S(1)}, f32[104,128]{1,0:T(8,128)S(1)}, u32[]{:S(2)}, u32[]{:S(2)}) collective-permute-start(f32[104,128]{1,0:T(8,128)S(1)} %get-tuple-element.23), channel_id=1, source_target_pairs={{0,7},{1,6},{2,5},{3,4},{4,3},{5,2},{6,1},{7,0},{8,15},{9,14},{10,... | collective-permute-start | bytes 159752 | tf_op jit(solution)/shard_map/ppermute | solution.py:486
  11.3 3.6 %collective-permute-start.4 = (f32[104,128]{1,0:T(8,128)S(1)}, f32[104,128]{1,0:T(8,128)S(1)}, u32[]{:S(2)}, u32[]{:S(2)}) collective-permute-start(f32[104,128]{1,0:T(8,128)S(1)} %get-tuple-element.24), channel_id=1, source_target_pairs={{0,5},{1,4},{2,7},{3,6},{4,1},{5,0},{6,3},{7,2},{8,13},{9,12},{10,... | collective-permute-start | bytes 159752 | tf_op jit(solution)/shard_map/ppermute | solution.py:486
  11.8 3.8 %collective-permute-start.5 = (f32[104,128]{1,0:T(8,128)S(1)}, f32[104,128]{1,0:T(8,128)S(1)}, u32[]{:S(2)}, u32[]{:S(2)}) collective-permute-start(f32[104,128]{1,0:T(8,128)S(1)} %get-tuple-element.25), channel_id=1, source_target_pairs={{0,3},{1,2},{2,1},{3,0},{4,7},{5,6},{6,5},{7,4},{8,11},{9,10},{10,... | collective-permute-start | bytes 159752 | tf_op jit(solution)/shard_map/ppermute | solution.py:486

commit v8 on v7

--- a/solution.py
+++ b/solution.py
@@ -11,7 +11,7 @@
 BASINS = 10
 SUB = 8
 LANES = 128
-CUT = 80
+CUT = 32
 GRANT = 16 * 1024 * 1024
 
 
@@ -285,8 +285,10 @@
     room = room.at[0]
     prepare(dims, (get_v, get_w, put_mean), room)
     done = [None] * dims[4]
-    for group in level_groups(dims):
-        total = multiply(dims, group, get_v, room, shallow, basin[here, :])
+    totals = [
+        multiply(dims, group, get_v, room, shallow, basin[here, :]) for group in level_groups(dims)
+    ]
+    for group, total in zip(level_groups(dims), totals):
         extract(dims, group, total, done)
     store_block(dims, blocks - 1, done, keep, give)
 
@@ -323,13 +325,13 @@
 
 
 def finish_kernel(dims, scaling, packed, *refs):
-    mean_warmth, limit, basin, eddy, transport = refs[-5:]
+    mean_warmth, limit, basin, eddy_out, transport_out, eddy, transport, flat, sem = refs[-9:]
     snapshots, levels, rows, blocks, tiles, dests, per_dest = dims
     width = BASINS * SUB
     quantities = 2 * snapshots + 4
     own_rows = tiles * quantities
     sub, lane = iota(0), iota(1)
-    got = refs[:-5]
+    got = refs[:-9]
     if len(got[0].shape) == 3:
         got = [got[0].at[d] for d in range(got[0].shape[0])]
     mine = got[0][...]
@@ -345,14 +347,18 @@
         at = c * 2 * blocks
         bar.append(shared[at : at + blocks] / jnp.maximum(shared[at + blocks : at + 2 * blocks], 1.0))
     for k in range(levels):
-        level = pick_lanes(bar, k * width, width)
+        flat[k] = pick_lanes(bar, k * width, width)
+    copies = []
+    for k in range(levels):
         for n in range(blocks):
             where = basin[n * SUB : (n + 1) * SUB, :] * SUB + sub
-            row = jnp.broadcast_to(level[n : n + 1], (SUB, LANES))
+            row = jnp.broadcast_to(flat[k, n : n + 1, :], (SUB, LANES))
             cell = jnp.take_along_axis(row, where, axis=1, mode="promise_in_bounds")
             deep = limit[n * SUB : (n + 1) * SUB, :] > float(k)
             star = mean_warmth[k, n * SUB : (n + 1) * SUB, :] - cell
             eddy[k, n * SUB : (n + 1) * SUB, :] = jnp.where(deep, star, 0.0)
+        copies.append(pltpu.make_async_copy(eddy.at[k], eddy_out.at[k], sem.at[k]))
+        copies[-1].start()
     spread = jnp.minimum(lane, BASINS - 1) * SUB + sub
     for i in range(per_dest):
         terms = []
@@ -377,6 +383,10 @@
                 row = jnp.broadcast_to(level[term : term + 1], (SUB, LANES))
                 cell = jnp.take_along_axis(row, spread, axis=1, mode="promise_in_bounds")
                 transport[term, k, i * SUB : (i + 1) * SUB, :] = cell[:, :BASINS]
+    copies.append(pltpu.make_async_copy(transport, transport_out, sem.at[levels]))
+    copies[-1].start()
+    for copy in copies:
+        copy.wait()
 
 
 def neighbours(lat, lon, first):
@@ -496,14 +506,17 @@
             sent = jnp.repeat(sent, lon // dests, axis=0, total_repeat_length=lon)
         got = (lax.all_to_all(sent, "lon", 0, 0),)
 
+    outputs = ((levels, rows, cols), (4, levels, per_dest * SUB, BASINS))
     eddy, transport = pl.pallas_call(
         functools.partial(finish_kernel, dims, scaling, pairs and spare_lanes(dims)[0]),
-        out_shape=(
-            jax.ShapeDtypeStruct((levels, rows, cols), jnp.float32),
-            jax.ShapeDtypeStruct((4, levels, per_dest * SUB, BASINS), jnp.float32),
-        ),
+        out_shape=tuple(pltpu.HBM(shape, jnp.float32) for shape in outputs),
         in_specs=[vmem] * (len(got) + 3),
-        out_specs=(vmem, vmem),
+        out_specs=(hbm, hbm),
+        scratch_shapes=[pltpu.VMEM(shape, jnp.float32) for shape in outputs]
+        + [
+            pltpu.VMEM((levels, blocks, LANES), jnp.float32),
+            pltpu.SemaphoreType.DMA((levels + 1,)),
+        ],
         compiler_params=params,
         name="finish",
     )(*got, mean_warmth, limit, basin)

time: 16.6 us -> 16.6 us (level)
  transfers between devices with their start and end apart: 6 -> 6, of which waited for: 5 -> 5; matrix products, arithmetic and copies ran while one was open for 0% -> 0% of each run, Pallas kernels for 9% -> 8%
where the time goes in v8:
time: 16.6 us; the launch traced here: 16.5 us
  starting transfers between devices  6.57 us (40%)
  waiting for transfers between devices  5.35 us (32%)
  Pallas kernels  3.83 us (23%)
  between operations  0.72 us (4%)
    ppermute x3, waiting for transfers between devices, shards(): lax.ppermute(messages[m], 'lon', [(i, i ^ 2 * m + 1) for i in range(lon)])  3.67 us
    ppermute x3, starting transfers between devices, shards(): lax.ppermute(messages[m], 'lon', [(i, i ^ 2 * m + 1) for i in range(lon)])  3.28 us
    ppermute x2, starting transfers between devices, shards(): lax.ppermute(edge, ('lat', 'lon'), neighbours(lat, lon, first))  3.22 us
    ppermute x1, waiting for transfers between devices, shards(): came = lax.ppermute(give, 'lon', [(i, i ^ 1) for i in range(lon)])  1.39 us
    pallas_call x1, Pallas kernels, shards(): pl.pallas_call(functools.partial(inner_kernel, dims, pairs), out_shape=re...  1.37 us
    pallas_call x1, Pallas kernels, shards(): pl.pallas_call(functools.partial(edge_kernel, dims), out_shape=pltpu.VMEM...  1.1 us
    pallas_call x1, Pallas kernels, shards(): pl.pallas_call(functools.partial(finish_kernel, dims, scaling, pairs and...  0.93 us
    pallas_call x1, Pallas kernels, shards(): pl.pallas_call(functools.partial(last_kernel, dims, pairs), out_shape=res...  0.35 us
  transfers between devices with their start and end apart: 6, of which 5 were waited for; matrix products, arithmetic and copies ran while one was open for 0% of the time, Pallas kernels for 8%

profile of v8, /device:TPU:0, one launch (start us, length us, event | category | flops | bytes accessed | tf_op | source)
XLA Modules:
  0.0 16.5 jit_solution(9137300551639538826)
XLA Ops:
  0.6 0.0 copy-start.4
  0.6 0.0 copy-start.3
  0.7 0.0 copy-start
  0.7 0.0 copy-start.2
  0.7 0.0 copy-start.1
  0.7 1.1 %edge.1 = f32[41,128]{1,0:T(8,128)S(1)} custom-call(f32[10,4,64,128]{3,2,1,0:T(8,128)} %warmth.5, s32[64,128]{1,0:T(8,128)} %flag.5, s32[64,128]{1,0:T(8,128)} %floor.5), custom_call_target="tpu_custom_call" | custom-call | flops 10000000000 | bytes 8388608 | tf_op jit(solution)/shard_map/edge/pallas_call | solution.py:433
  1.8 2.5 %collective-permute-start.1 = (f32[41,128]{1,0:T(8,128)S(1)}, f32[41,128]{1,0:T(8,128)S(1)}, u32[]{:S(2)}, u32[]{:S(2)}) collective-permute-start(f32[41,128]{1,0:T(8,128)S(1)} %edge.1), channel_id=1, source_target_pairs={{0,9},{1,8},{2,11},{3,10},{4,13},{5,12},{6,15},{7,14},{8,0},{9,1},... | collective-permute-start | bytes 62984 | tf_op jit(solution)/shard_map/ppermute | solution.py:449
  4.3 0.7 %collective-permute-start = (f32[41,128]{1,0:T(8,128)S(1)}, f32[41,128]{1,0:T(8,128)S(1)}, u32[]{:S(2)}, u32[]{:S(2)}) collective-permute-start(f32[41,128]{1,0:T(8,128)S(1)} %edge.1), channel_id=1, source_target_pairs={{0,1},{1,0},{2,3},{3,2},{4,5},{5,4},{6,7},{7,6},{8,17},{9,16},{10,... | collective-permute-start | bytes 62984 | tf_op jit(solution)/shard_map/ppermute | solution.py:449
  5.0 0.0 copy-done.4
  5.0 0.0 copy-done.3
  5.0 0.0 copy-done
  5.0 0.0 copy-done.2
  5.0 0.0 copy-done.1
  5.0 1.4 %inner_rows.1 = (f32[336,128]{1,0:T(8,128)S(1)}, f32[336,128]{1,0:T(8,128)S(1)}, f32[4,64,128]{2,1,0:T(8,128)S(1)}, f32[64,128]{1,0:T(8,128)S(1)}) custom-call(f32[10,4,64,128]{3,2,1,0:T(8,128)S(1)} %copy-done.1, f32[10,4,64,128]{3,2,1,0:T(8,128)S(1)} %copy-done, s32[64,128]{1,0:T(8,128)S(1)} %copy-done.3, s32[64,128]{1,0:T(8,128)S(1)} %copy-done.4, ...), custom_call_target="tpu_custom_call" | custom-call | tf_op jit(solution)/shard_map/inner_rows/pallas_call | solution.py:460
  6.4 0.3 %collective-permute-done.1.even_halo = f32[41,128]{1,0:T(8,128)S(1)} collective-permute-done((f32[41,128]{1,0:T(8,128)S(1)}, f32[41,128]{1,0:T(8,128)S(1)}, u32[]{:S(2)}, u32[]{:S(2)}) %collective-permute-start.1) | collective-permute-done | bytes 21024 | tf_op jit(solution)/shard_map/ppermute | solution.py:449
  6.7 0.0 collective-permute-done.odd_halo
  6.7 0.4 %last_rows.1 = (f32[336,128]{1,0:T(8,128)S(1)}, f32[336,128]{1,0:T(8,128)S(1)}, f32[4,64,128]{2,1,0:T(8,128)S(1)}, f32[64,128]{1,0:T(8,128)S(1)}) custom-call(f32[41,128]{1,0:T(8,128)S(1)} %collective-permute-done.odd_halo, f32[41,128]{1,0:T(8,128)S(1)} %collective-permute-done.1.even_halo, ...), custom_call_target="tpu_custom_call", output_to_operand_aliasing={{0}: (7, {}), {1}: (8, {}), {2}: (9, {}), {3}: (10, {})} | custom-call | tf_op jit(solution)/shard_map/last_rows/pallas_call | solution.py:469
  7.1 0.1 collective-permute-start.2
  7.1 1.4 %collective-permute-done.2.came = f32[336,128]{1,0:T(8,128)S(1)} collective-permute-done((f32[336,128]{1,0:T(8,128)S(1)}, f32[336,128]{1,0:T(8,128)S(1)}, u32[]{:S(2)}, u32[]{:S(2)}) %collective-permute-start.2) | collective-permute-done | bytes 172064 | tf_op jit(solution)/shard_map/ppermute | solution.py:483
  8.5 0.1 pair_sums.1
  8.6 2.7 %collective-permute-start.3 = (f32[104,128]{1,0:T(8,128)S(1)}, f32[104,128]{1,0:T(8,128)S(1)}, u32[]{:S(2)}, u32[]{:S(2)}) collective-permute-start(f32[104,128]{1,0:T(8,128)S(1)} %get-tuple-element.23), channel_id=1, source_target_pairs={{0,7},{1,6},{2,5},{3,4},{4,3},{5,2},{6,1},{7,0},{8,15},{9,14},{10,... | collective-permute-start | bytes 159752 | tf_op jit(solution)/shard_map/ppermute | solution.py:496
  11.3 0.5 %collective-permute-start.4 = (f32[104,128]{1,0:T(8,128)S(1)}, f32[104,128]{1,0:T(8,128)S(1)}, u32[]{:S(2)}, u32[]{:S(2)}) collective-permute-start(f32[104,128]{1,0:T(8,128)S(1)} %get-tuple-element.24), channel_id=1, source_target_pairs={{0,5},{1,4},{2,7},{3,6},{4,1},{5,0},{6,3},{7,2},{8,13},{9,12},{10,... | collective-permute-start | bytes 159752 | tf_op jit(solution)/shard_map/ppermute | solution.py:496
  11.8 0.1 collective-permute-start.5
  11.9 1.6 %collective-permute-done.3.refs_1_ = f32[104,128]{1,0:T(8,128)S(1)} collective-permute-done((f32[104,128]{1,0:T(8,128)S(1)}, f32[104,128]{1,0:T(8,128)S(1)}, u32[]{:S(2)}, u32[]{:S(2)}) %collective-permute-start.3) | collective-permute-done | bytes 53280 | tf_op jit(solution)/shard_map/ppermute | solution.py:496
  13.5 1.4 %collective-permute-done.4.refs_2_ = f32[104,128]{1,0:T(8,128)S(1)} collective-permute-done((f32[104,128]{1,0:T(8,128)S(1)}, f32[104,128]{1,0:T(8,128)S(1)}, u32[]{:S(2)}, u32[]{:S(2)}) %collective-permute-start.4) | collective-permute-done | bytes 53280 | tf_op jit(solution)/shard_map/ppermute | solution.py:496
  14.9 0.7 %collective-permute-done.5.refs_3_ = f32[104,128]{1,0:T(8,128)S(1)} collective-permute-done((f32[104,128]{1,0:T(8,128)S(1)}, f32[104,128]{1,0:T(8,128)S(1)}, u32[]{:S(2)}, u32[]{:S(2)}) %collective-permute-start.5) | collective-permute-done | bytes 53280 | tf_op jit(solution)/shard_map/ppermute | solution.py:496
  15.6 0.9 %finish.1 = (f32[4,64,128]{2,1,0:T(8,128)}, f32[4,4,8,10]{3,2,1,0:T(8,128)}) custom-call(f32[104,128]{1,0:T(8,128)S(1)} %get-tuple-element.22.refs_0_, f32[104,128]{1,0:T(8,128)S(1)} %collective-permute-done.3.refs_1_, f32[104,128]{1,0:T(8,128)S(1)} %collective-permute-done.4.refs_2_, f32[104,128]{1,0:T(8,128)S(1)} %collective-permute-done.5.refs_3_, ...), custom_call_target="tpu_custom_call" | custom-call | tf_op jit(solution)/shard_map/finish/pallas_call | solution.py:510
Async XLA Ops:
  0.6 4.4 %copy-start.4 = (s32[64,128]{1,0:T(8,128)S(1)}, s32[64,128]{1,0:T(8,128)}, u32[]{:S(2)}) copy-start(s32[64,128]{1,0:T(8,128)} %floor.5) | copy-start | bytes 98308
  0.6 4.4 %copy-start.3 = (s32[64,128]{1,0:T(8,128)S(1)}, s32[64,128]{1,0:T(8,128)}, u32[]{:S(2)}) copy-start(s32[64,128]{1,0:T(8,128)} %flag.5) | copy-start | bytes 98308
  0.7 4.4 %copy-start = (f32[10,4,64,128]{3,2,1,0:T(8,128)S(1)}, f32[10,4,64,128]{3,2,1,0:T(8,128)}, u32[]{:S(2)}) copy-start(f32[10,4,64,128]{3,2,1,0:T(8,128)} %warmth.5) | copy-start | bytes 3932164
  0.7 4.4 %copy-start.2 = (s32[64,128]{1,0:T(8,128)S(1)}, s32[64,128]{1,0:T(8,128)}, u32[]{:S(2)}) copy-start(s32[64,128]{1,0:T(8,128)} %refs_6_.1) | copy-start | bytes 98308
  0.7 4.4 %copy-start.1 = (f32[10,4,64,128]{3,2,1,0:T(8,128)S(1)}, f32[10,4,64,128]{3,2,1,0:T(8,128)}, u32[]{:S(2)}) copy-start(f32[10,4,64,128]{3,2,1,0:T(8,128)} %flow.3) | copy-start | bytes 3932164
  1.8 4.9 %collective-permute-start.1 = (f32[41,128]{1,0:T(8,128)S(1)}, f32[41,128]{1,0:T(8,128)S(1)}, u32[]{:S(2)}, u32[]{:S(2)}) collective-permute-start(f32[41,128]{1,0:T(8,128)S(1)} %edge.1), channel_id=1, source_target_pairs={{0,9},{1,8},{2,11},{3,10},{4,13},{5,12},{6,15},{7,14},{8,0},{9,1},... | collective-permute-start | bytes 62984 | tf_op jit(solution)/shard_map/ppermute | solution.py:449
  4.3 2.4 %collective-permute-start = (f32[41,128]{1,0:T(8,128)S(1)}, f32[41,128]{1,0:T(8,128)S(1)}, u32[]{:S(2)}, u32[]{:S(2)}) collective-permute-start(f32[41,128]{1,0:T(8,128)S(1)} %edge.1), channel_id=1, source_target_pairs={{0,1},{1,0},{2,3},{3,2},{4,5},{5,4},{6,7},{7,6},{8,17},{9,16},{10,... | collective-permute-start | bytes 62984 | tf_op jit(solution)/shard_map/ppermute | solution.py:449
  7.1 1.5 %collective-permute-start.2 = (f32[336,128]{1,0:T(8,128)S(1)}, f32[336,128]{1,0:T(8,128)S(1)}, u32[]{:S(2)}, u32[]{:S(2)}) collective-permute-start(f32[336,128]{1,0:T(8,128)S(1)} %get-tuple-element.21), channel_id=1, source_target_pairs={{0,1},{1,0},{2,3},{3,2},{4,5},{5,4},{6,7},{7,6},{8,9},{9,8},{10,11... | collective-permute-start | bytes 516104 | tf_op jit(solution)/shard_map/ppermute | solution.py:483
  8.6 4.9 %collective-permute-start.3 = (f32[104,128]{1,0:T(8,128)S(1)}, f32[104,128]{1,0:T(8,128)S(1)}, u32[]{:S(2)}, u32[]{:S(2)}) collective-permute-start(f32[104,128]{1,0:T(8,128)S(1)} %get-tuple-element.23), channel_id=1, source_target_pairs={{0,7},{1,6},{2,5},{3,4},{4,3},{5,2},{6,1},{7,0},{8,15},{9,14},{10,... | collective-permute-start | bytes 159752 | tf_op jit(solution)/shard_map/ppermute | solution.py:496
  11.3 3.6 %collective-permute-start.4 = (f32[104,128]{1,0:T(8,128)S(1)}, f32[104,128]{1,0:T(8,128)S(1)}, u32[]{:S(2)}, u32[]{:S(2)}) collective-permute-start(f32[104,128]{1,0:T(8,128)S(1)} %get-tuple-element.24), channel_id=1, source_target_pairs={{0,5},{1,4},{2,7},{3,6},{4,1},{5,0},{6,3},{7,2},{8,13},{9,12},{10,... | collective-permute-start | bytes 159752 | tf_op jit(solution)/shard_map/ppermute | solution.py:496
  11.8 3.8 %collective-permute-start.5 = (f32[104,128]{1,0:T(8,128)S(1)}, f32[104,128]{1,0:T(8,128)S(1)}, u32[]{:S(2)}, u32[]{:S(2)}) collective-permute-start(f32[104,128]{1,0:T(8,128)S(1)} %get-tuple-element.25), channel_id=1, source_target_pairs={{0,3},{1,2},{2,1},{3,0},{4,7},{5,6},{6,5},{7,4},{8,11},{9,10},{10,... | collective-permute-start | bytes 159752 | tf_op jit(solution)/shard_map/ppermute | solution.py:496

commit v9 on v8

--- a/solution.py
+++ b/solution.py
@@ -492,9 +492,11 @@
             compiler_params=params,
             name="pair_sums",
         )(keep, came)
+        far_first = list(reversed(range(1, chips)))
+        order = far_first[1:2] + far_first[:1] + far_first[2:]
         got = messages[:1] + tuple(
             lax.ppermute(messages[m], "lon", [(i, i ^ (2 * m + 1)) for i in range(lon)])
-            for m in reversed(range(1, chips))
+            for m in order
         )
     else:
         own, shared = sums[0][: dests * own_rows], sums[0][dests * own_rows :]

time: 16.6 us -> 16.6 us (level)
  no operation moved by 1% of the time
where the time goes in v9:
time: 16.6 us; the launch traced here: 16.5 us
  starting transfers between devices  6.54 us (39%)
  waiting for transfers between devices  5.38 us (32%)
  Pallas kernels  3.83 us (23%)
  between operations  0.72 us (4%)
    ppermute x3, waiting for transfers between devices, shards(): lax.ppermute(messages[m], 'lon', [(i, i ^ 2 * m + 1) for i in range(lon)])  3.69 us
    ppermute x3, starting transfers between devices, shards(): lax.ppermute(messages[m], 'lon', [(i, i ^ 2 * m + 1) for i in range(lon)])  3.25 us
    ppermute x2, starting transfers between devices, shards(): lax.ppermute(edge, ('lat', 'lon'), neighbours(lat, lon, first))  3.22 us
    ppermute x1, waiting for transfers between devices, shards(): came = lax.ppermute(give, 'lon', [(i, i ^ 1) for i in range(lon)])  1.39 us
    pallas_call x1, Pallas kernels, shards(): pl.pallas_call(functools.partial(inner_kernel, dims, pairs), out_shape=re...  1.37 us
    pallas_call x1, Pallas kernels, shards(): pl.pallas_call(functools.partial(edge_kernel, dims), out_shape=pltpu.VMEM...  1.1 us
    pallas_call x1, Pallas kernels, shards(): pl.pallas_call(functools.partial(finish_kernel, dims, scaling, pairs and...  0.93 us
    pallas_call x1, Pallas kernels, shards(): pl.pallas_call(functools.partial(last_kernel, dims, pairs), out_shape=res...  0.35 us
  transfers between devices with their start and end apart: 6, of which 5 were waited for; matrix products, arithmetic and copies ran while one was open for 0% of the time, Pallas kernels for 8%

profile of v9, /device:TPU:0, one launch (start us, length us, event | category | flops | bytes accessed | tf_op | source)
XLA Modules:
  0.0 16.5 jit_solution(5507449861873940832)
XLA Ops:
  0.6 0.0 copy-start.4
  0.6 0.0 copy-start.3
  0.7 0.0 copy-start
  0.7 0.0 copy-start.2
  0.7 0.0 copy-start.1
  0.7 1.1 %edge.1 = f32[41,128]{1,0:T(8,128)S(1)} custom-call(f32[10,4,64,128]{3,2,1,0:T(8,128)} %warmth.5, s32[64,128]{1,0:T(8,128)} %flag.5, s32[64,128]{1,0:T(8,128)} %floor.5), custom_call_target="tpu_custom_call" | custom-call | flops 10000000000 | bytes 8388608 | tf_op jit(solution)/shard_map/edge/pallas_call | solution.py:433
  1.8 2.5 %collective-permute-start.1 = (f32[41,128]{1,0:T(8,128)S(1)}, f32[41,128]{1,0:T(8,128)S(1)}, u32[]{:S(2)}, u32[]{:S(2)}) collective-permute-start(f32[41,128]{1,0:T(8,128)S(1)} %edge.1), channel_id=1, source_target_pairs={{0,9},{1,8},{2,11},{3,10},{4,13},{5,12},{6,15},{7,14},{8,0},{9,1},... | collective-permute-start | bytes 62984 | tf_op jit(solution)/shard_map/ppermute | solution.py:449
  4.3 0.7 %collective-permute-start = (f32[41,128]{1,0:T(8,128)S(1)}, f32[41,128]{1,0:T(8,128)S(1)}, u32[]{:S(2)}, u32[]{:S(2)}) collective-permute-start(f32[41,128]{1,0:T(8,128)S(1)} %edge.1), channel_id=1, source_target_pairs={{0,1},{1,0},{2,3},{3,2},{4,5},{5,4},{6,7},{7,6},{8,17},{9,16},{10,... | collective-permute-start | bytes 62984 | tf_op jit(solution)/shard_map/ppermute | solution.py:449
  5.0 0.0 copy-done.4
  5.0 0.0 copy-done.3
  5.0 0.0 copy-done
  5.0 0.0 copy-done.2
  5.0 0.0 copy-done.1
  5.0 1.4 %inner_rows.1 = (f32[336,128]{1,0:T(8,128)S(1)}, f32[336,128]{1,0:T(8,128)S(1)}, f32[4,64,128]{2,1,0:T(8,128)S(1)}, f32[64,128]{1,0:T(8,128)S(1)}) custom-call(f32[10,4,64,128]{3,2,1,0:T(8,128)S(1)} %copy-done.1, f32[10,4,64,128]{3,2,1,0:T(8,128)S(1)} %copy-done, s32[64,128]{1,0:T(8,128)S(1)} %copy-done.3, s32[64,128]{1,0:T(8,128)S(1)} %copy-done.4, ...), custom_call_target="tpu_custom_call" | custom-call | tf_op jit(solution)/shard_map/inner_rows/pallas_call | solution.py:460
  6.4 0.3 %collective-permute-done.1.even_halo = f32[41,128]{1,0:T(8,128)S(1)} collective-permute-done((f32[41,128]{1,0:T(8,128)S(1)}, f32[41,128]{1,0:T(8,128)S(1)}, u32[]{:S(2)}, u32[]{:S(2)}) %collective-permute-start.1) | collective-permute-done | bytes 21024 | tf_op jit(solution)/shard_map/ppermute | solution.py:449
  6.7 0.0 collective-permute-done.odd_halo
  6.7 0.4 %last_rows.1 = (f32[336,128]{1,0:T(8,128)S(1)}, f32[336,128]{1,0:T(8,128)S(1)}, f32[4,64,128]{2,1,0:T(8,128)S(1)}, f32[64,128]{1,0:T(8,128)S(1)}) custom-call(f32[41,128]{1,0:T(8,128)S(1)} %collective-permute-done.odd_halo, f32[41,128]{1,0:T(8,128)S(1)} %collective-permute-done.1.even_halo, ...), custom_call_target="tpu_custom_call", output_to_operand_aliasing={{0}: (7, {}), {1}: (8, {}), {2}: (9, {}), {3}: (10, {})} | custom-call | tf_op jit(solution)/shard_map/last_rows/pallas_call | solution.py:469
  7.1 0.1 collective-permute-start.2
  7.1 1.4 %collective-permute-done.2.came = f32[336,128]{1,0:T(8,128)S(1)} collective-permute-done((f32[336,128]{1,0:T(8,128)S(1)}, f32[336,128]{1,0:T(8,128)S(1)}, u32[]{:S(2)}, u32[]{:S(2)}) %collective-permute-start.2) | collective-permute-done | bytes 172064 | tf_op jit(solution)/shard_map/ppermute | solution.py:483
  8.5 0.1 pair_sums.1
  8.6 1.7 %collective-permute-start.3 = (f32[104,128]{1,0:T(8,128)S(1)}, f32[104,128]{1,0:T(8,128)S(1)}, u32[]{:S(2)}, u32[]{:S(2)}) collective-permute-start(f32[104,128]{1,0:T(8,128)S(1)} %get-tuple-element.23), channel_id=1, source_target_pairs={{0,5},{1,4},{2,7},{3,6},{4,1},{5,0},{6,3},{7,2},{8,13},{9,12},{10,... | collective-permute-start | bytes 159752 | tf_op jit(solution)/shard_map/ppermute | solution.py:498
  10.4 1.4 %collective-permute-start.4 = (f32[104,128]{1,0:T(8,128)S(1)}, f32[104,128]{1,0:T(8,128)S(1)}, u32[]{:S(2)}, u32[]{:S(2)}) collective-permute-start(f32[104,128]{1,0:T(8,128)S(1)} %get-tuple-element.24), channel_id=1, source_target_pairs={{0,7},{1,6},{2,5},{3,4},{4,3},{5,2},{6,1},{7,0},{8,15},{9,14},{10,... | collective-permute-start | bytes 159752 | tf_op jit(solution)/shard_map/ppermute | solution.py:498
  11.8 0.1 collective-permute-start.5
  11.9 0.4 %collective-permute-done.3.refs_1_ = f32[104,128]{1,0:T(8,128)S(1)} collective-permute-done((f32[104,128]{1,0:T(8,128)S(1)}, f32[104,128]{1,0:T(8,128)S(1)}, u32[]{:S(2)}, u32[]{:S(2)}) %collective-permute-start.3) | collective-permute-done | bytes 53280 | tf_op jit(solution)/shard_map/ppermute | solution.py:498
  12.3 2.5 %collective-permute-done.4.refs_2_ = f32[104,128]{1,0:T(8,128)S(1)} collective-permute-done((f32[104,128]{1,0:T(8,128)S(1)}, f32[104,128]{1,0:T(8,128)S(1)}, u32[]{:S(2)}, u32[]{:S(2)}) %collective-permute-start.4) | collective-permute-done | bytes 53280 | tf_op jit(solution)/shard_map/ppermute | solution.py:498
  14.8 0.7 %collective-permute-done.5.refs_3_ = f32[104,128]{1,0:T(8,128)S(1)} collective-permute-done((f32[104,128]{1,0:T(8,128)S(1)}, f32[104,128]{1,0:T(8,128)S(1)}, u32[]{:S(2)}, u32[]{:S(2)}) %collective-permute-start.5) | collective-permute-done | bytes 53280 | tf_op jit(solution)/shard_map/ppermute | solution.py:498
  15.6 0.9 %finish.1 = (f32[4,64,128]{2,1,0:T(8,128)}, f32[4,4,8,10]{3,2,1,0:T(8,128)}) custom-call(f32[104,128]{1,0:T(8,128)S(1)} %get-tuple-element.22.refs_0_, f32[104,128]{1,0:T(8,128)S(1)} %collective-permute-done.3.refs_1_, f32[104,128]{1,0:T(8,128)S(1)} %collective-permute-done.4.refs_2_, f32[104,128]{1,0:T(8,128)S(1)} %collective-permute-done.5.refs_3_, ...), custom_call_target="tpu_custom_call" | custom-call | tf_op jit(solution)/shard_map/finish/pallas_call | solution.py:512
Async XLA Ops:
  0.6 4.4 %copy-start.4 = (s32[64,128]{1,0:T(8,128)S(1)}, s32[64,128]{1,0:T(8,128)}, u32[]{:S(2)}) copy-start(s32[64,128]{1,0:T(8,128)} %floor.5) | copy-start | bytes 98308
  0.6 4.4 %copy-start.3 = (s32[64,128]{1,0:T(8,128)S(1)}, s32[64,128]{1,0:T(8,128)}, u32[]{:S(2)}) copy-start(s32[64,128]{1,0:T(8,128)} %flag.5) | copy-start | bytes 98308
  0.7 4.4 %copy-start = (f32[10,4,64,128]{3,2,1,0:T(8,128)S(1)}, f32[10,4,64,128]{3,2,1,0:T(8,128)}, u32[]{:S(2)}) copy-start(f32[10,4,64,128]{3,2,1,0:T(8,128)} %warmth.5) | copy-start | bytes 3932164
  0.7 4.4 %copy-start.2 = (s32[64,128]{1,0:T(8,128)S(1)}, s32[64,128]{1,0:T(8,128)}, u32[]{:S(2)}) copy-start(s32[64,128]{1,0:T(8,128)} %refs_6_.1) | copy-start | bytes 98308
  0.7 4.4 %copy-start.1 = (f32[10,4,64,128]{3,2,1,0:T(8,128)S(1)}, f32[10,4,64,128]{3,2,1,0:T(8,128)}, u32[]{:S(2)}) copy-start(f32[10,4,64,128]{3,2,1,0:T(8,128)} %flow.3) | copy-start | bytes 3932164
  1.8 4.9 %collective-permute-start.1 = (f32[41,128]{1,0:T(8,128)S(1)}, f32[41,128]{1,0:T(8,128)S(1)}, u32[]{:S(2)}, u32[]{:S(2)}) collective-permute-start(f32[41,128]{1,0:T(8,128)S(1)} %edge.1), channel_id=1, source_target_pairs={{0,9},{1,8},{2,11},{3,10},{4,13},{5,12},{6,15},{7,14},{8,0},{9,1},... | collective-permute-start | bytes 62984 | tf_op jit(solution)/shard_map/ppermute | solution.py:449
  4.3 2.4 %collective-permute-start = (f32[41,128]{1,0:T(8,128)S(1)}, f32[41,128]{1,0:T(8,128)S(1)}, u32[]{:S(2)}, u32[]{:S(2)}) collective-permute-start(f32[41,128]{1,0:T(8,128)S(1)} %edge.1), channel_id=1, source_target_pairs={{0,1},{1,0},{2,3},{3,2},{4,5},{5,4},{6,7},{7,6},{8,17},{9,16},{10,... | collective-permute-start | bytes 62984 | tf_op jit(solution)/shard_map/ppermute | solution.py:449
  7.1 1.5 %collective-permute-start.2 = (f32[336,128]{1,0:T(8,128)S(1)}, f32[336,128]{1,0:T(8,128)S(1)}, u32[]{:S(2)}, u32[]{:S(2)}) collective-permute-start(f32[336,128]{1,0:T(8,128)S(1)} %get-tuple-element.21), channel_id=1, source_target_pairs={{0,1},{1,0},{2,3},{3,2},{4,5},{5,4},{6,7},{7,6},{8,9},{9,8},{10,11... | collective-permute-start | bytes 516104 | tf_op jit(solution)/shard_map/ppermute | solution.py:483
  8.6 3.7 %collective-permute-start.3 = (f32[104,128]{1,0:T(8,128)S(1)}, f32[104,128]{1,0:T(8,128)S(1)}, u32[]{:S(2)}, u32[]{:S(2)}) collective-permute-start(f32[104,128]{1,0:T(8,128)S(1)} %get-tuple-element.23), channel_id=1, source_target_pairs={{0,5},{1,4},{2,7},{3,6},{4,1},{5,0},{6,3},{7,2},{8,13},{9,12},{10,... | collective-permute-start | bytes 159752 | tf_op jit(solution)/shard_map/ppermute | solution.py:498
  10.4 4.5 %collective-permute-start.4 = (f32[104,128]{1,0:T(8,128)S(1)}, f32[104,128]{1,0:T(8,128)S(1)}, u32[]{:S(2)}, u32[]{:S(2)}) collective-permute-start(f32[104,128]{1,0:T(8,128)S(1)} %get-tuple-element.24), channel_id=1, source_target_pairs={{0,7},{1,6},{2,5},{3,4},{4,3},{5,2},{6,1},{7,0},{8,15},{9,14},{10,... | collective-permute-start | bytes 159752 | tf_op jit(solution)/shard_map/ppermute | solution.py:498
  11.8 3.8 %collective-permute-start.5 = (f32[104,128]{1,0:T(8,128)S(1)}, f32[104,128]{1,0:T(8,128)S(1)}, u32[]{:S(2)}, u32[]{:S(2)}) collective-permute-start(f32[104,128]{1,0:T(8,128)S(1)} %get-tuple-element.25), channel_id=1, source_target_pairs={{0,3},{1,2},{2,1},{3,0},{4,7},{5,6},{6,5},{7,4},{8,11},{9,10},{10,... | collective-permute-start | bytes 159752 | tf_op jit(solution)/shard_map/ppermute | solution.py:498

commit v10 on v9

--- a/solution.py
+++ b/solution.py
@@ -400,7 +400,7 @@
             elif other < i:
                 target = other * lon + j
             else:
-                target = other * lon + across
+                target = other * lon + (across if i > 0 else j)
             route.append((i * lon + j, target))
     return route
 

time: 16.6 us -> 16.6 us (level)
  no operation moved by 1% of the time
where the time goes in v10:
time: 16.6 us; the launch traced here: 16.5 us
  starting transfers between devices  6.54 us (39%)
  waiting for transfers between devices  5.36 us (32%)
  Pallas kernels  3.83 us (23%)
  between operations  0.73 us (4%)
    ppermute x3, waiting for transfers between devices, shards(): lax.ppermute(messages[m], 'lon', [(i, i ^ 2 * m + 1) for i in range(lon)])  3.69 us
    ppermute x3, starting transfers between devices, shards(): lax.ppermute(messages[m], 'lon', [(i, i ^ 2 * m + 1) for i in range(lon)])  3.25 us
    ppermute x2, starting transfers between devices, shards(): lax.ppermute(edge, ('lat', 'lon'), neighbours(lat, lon, first))  3.09 us
    pallas_call x1, Pallas kernels, shards(): pl.pallas_call(functools.partial(inner_kernel, dims, pairs), out_shape=re...  1.37 us
    ppermute x1, waiting for transfers between devices, shards(): came = lax.ppermute(give, 'lon', [(i, i ^ 1) for i in range(lon)])  1.27 us
    pallas_call x1, Pallas kernels, shards(): pl.pallas_call(functools.partial(edge_kernel, dims), out_shape=pltpu.VMEM...  1.1 us
    pallas_call x1, Pallas kernels, shards(): pl.pallas_call(functools.partial(finish_kernel, dims, scaling, pairs and...  0.93 us
    ppermute x2, waiting for transfers between devices, shards(): lax.ppermute(edge, ('lat', 'lon'), neighbours(lat, lon, first))  0.39 us
  transfers between devices with their start and end apart: 6, of which 5 were waited for; matrix products, arithmetic and copies ran while one was open for 0% of the time, Pallas kernels for 8%

profile of v10, /device:TPU:0, one launch (start us, length us, event | category | flops | bytes accessed | tf_op | source)
XLA Modules:
  0.0 16.5 jit_solution(238159031099081000)
XLA Ops:
  0.6 0.0 copy-start.4
  0.6 0.0 copy-start.3
  0.7 0.0 copy-start
  0.7 0.0 copy-start.2
  0.7 0.0 copy-start.1
  0.7 1.1 %edge.1 = f32[41,128]{1,0:T(8,128)S(1)} custom-call(f32[10,4,64,128]{3,2,1,0:T(8,128)} %warmth.5, s32[64,128]{1,0:T(8,128)} %flag.5, s32[64,128]{1,0:T(8,128)} %floor.5), custom_call_target="tpu_custom_call" | custom-call | flops 10000000000 | bytes 8388608 | tf_op jit(solution)/shard_map/edge/pallas_call | solution.py:433
  1.8 3.1 %collective-permute-start.1 = (f32[41,128]{1,0:T(8,128)S(1)}, f32[41,128]{1,0:T(8,128)S(1)}, u32[]{:S(2)}, u32[]{:S(2)}) collective-permute-start(f32[41,128]{1,0:T(8,128)S(1)} %edge.1), channel_id=1, source_target_pairs={{0,8},{1,9},{2,10},{3,11},{4,12},{5,13},{6,14},{7,15},{8,0},{9,1},... | collective-permute-start | bytes 62984 | tf_op jit(solution)/shard_map/ppermute | solution.py:449
  4.9 0.0 collective-permute-start
  4.9 0.0 copy-done.4
  4.9 0.0 copy-done.3
  4.9 0.0 copy-done
  4.9 0.0 copy-done.2
  4.9 0.0 copy-done.1
  4.9 1.4 %inner_rows.1 = (f32[336,128]{1,0:T(8,128)S(1)}, f32[336,128]{1,0:T(8,128)S(1)}, f32[4,64,128]{2,1,0:T(8,128)S(1)}, f32[64,128]{1,0:T(8,128)S(1)}) custom-call(f32[10,4,64,128]{3,2,1,0:T(8,128)S(1)} %copy-done.1, f32[10,4,64,128]{3,2,1,0:T(8,128)S(1)} %copy-done, s32[64,128]{1,0:T(8,128)S(1)} %copy-done.3, s32[64,128]{1,0:T(8,128)S(1)} %copy-done.4, ...), custom_call_target="tpu_custom_call" | custom-call | tf_op jit(solution)/shard_map/inner_rows/pallas_call | solution.py:460
  6.3 0.4 %collective-permute-done.1.even_halo = f32[41,128]{1,0:T(8,128)S(1)} collective-permute-done((f32[41,128]{1,0:T(8,128)S(1)}, f32[41,128]{1,0:T(8,128)S(1)}, u32[]{:S(2)}, u32[]{:S(2)}) %collective-permute-start.1) | collective-permute-done | bytes 21024 | tf_op jit(solution)/shard_map/ppermute | solution.py:449
  6.7 0.0 collective-permute-done.odd_halo
  6.7 0.4 %last_rows.1 = (f32[336,128]{1,0:T(8,128)S(1)}, f32[336,128]{1,0:T(8,128)S(1)}, f32[4,64,128]{2,1,0:T(8,128)S(1)}, f32[64,128]{1,0:T(8,128)S(1)}) custom-call(f32[41,128]{1,0:T(8,128)S(1)} %collective-permute-done.odd_halo, f32[41,128]{1,0:T(8,128)S(1)} %collective-permute-done.1.even_halo, ...), custom_call_target="tpu_custom_call", output_to_operand_aliasing={{0}: (7, {}), {1}: (8, {}), {2}: (9, {}), {3}: (10, {})} | custom-call | tf_op jit(solution)/shard_map/last_rows/pallas_call | solution.py:469
  7.1 0.2 %collective-permute-start.2 = (f32[336,128]{1,0:T(8,128)S(1)}, f32[336,128]{1,0:T(8,128)S(1)}, u32[]{:S(2)}, u32[]{:S(2)}) collective-permute-start(f32[336,128]{1,0:T(8,128)S(1)} %get-tuple-element.21), channel_id=1, source_target_pairs={{0,1},{1,0},{2,3},{3,2},{4,5},{5,4},{6,7},{7,6},{8,9},{9,8},{10,11... | collective-permute-start | bytes 516104 | tf_op jit(solution)/shard_map/ppermute | solution.py:483
  7.2 1.3 %collective-permute-done.2.came = f32[336,128]{1,0:T(8,128)S(1)} collective-permute-done((f32[336,128]{1,0:T(8,128)S(1)}, f32[336,128]{1,0:T(8,128)S(1)}, u32[]{:S(2)}, u32[]{:S(2)}) %collective-permute-start.2) | collective-permute-done | bytes 172064 | tf_op jit(solution)/shard_map/ppermute | solution.py:483
  8.5 0.1 pair_sums.1
  8.6 1.7 %collective-permute-start.3 = (f32[104,128]{1,0:T(8,128)S(1)}, f32[104,128]{1,0:T(8,128)S(1)}, u32[]{:S(2)}, u32[]{:S(2)}) collective-permute-start(f32[104,128]{1,0:T(8,128)S(1)} %get-tuple-element.23), channel_id=1, source_target_pairs={{0,5},{1,4},{2,7},{3,6},{4,1},{5,0},{6,3},{7,2},{8,13},{9,12},{10,... | collective-permute-start | bytes 159752 | tf_op jit(solution)/shard_map/ppermute | solution.py:498
  10.3 1.4 %collective-permute-start.4 = (f32[104,128]{1,0:T(8,128)S(1)}, f32[104,128]{1,0:T(8,128)S(1)}, u32[]{:S(2)}, u32[]{:S(2)}) collective-permute-start(f32[104,128]{1,0:T(8,128)S(1)} %get-tuple-element.24), channel_id=1, source_target_pairs={{0,7},{1,6},{2,5},{3,4},{4,3},{5,2},{6,1},{7,0},{8,15},{9,14},{10,... | collective-permute-start | bytes 159752 | tf_op jit(solution)/shard_map/ppermute | solution.py:498
  11.7 0.1 collective-permute-start.5
  11.9 0.4 %collective-permute-done.3.refs_1_ = f32[104,128]{1,0:T(8,128)S(1)} collective-permute-done((f32[104,128]{1,0:T(8,128)S(1)}, f32[104,128]{1,0:T(8,128)S(1)}, u32[]{:S(2)}, u32[]{:S(2)}) %collective-permute-start.3) | collective-permute-done | bytes 53280 | tf_op jit(solution)/shard_map/ppermute | solution.py:498
  12.3 2.5 %collective-permute-done.4.refs_2_ = f32[104,128]{1,0:T(8,128)S(1)} collective-permute-done((f32[104,128]{1,0:T(8,128)S(1)}, f32[104,128]{1,0:T(8,128)S(1)}, u32[]{:S(2)}, u32[]{:S(2)}) %collective-permute-start.4) | collective-permute-done | bytes 53280 | tf_op jit(solution)/shard_map/ppermute | solution.py:498
  14.8 0.7 %collective-permute-done.5.refs_3_ = f32[104,128]{1,0:T(8,128)S(1)} collective-permute-done((f32[104,128]{1,0:T(8,128)S(1)}, f32[104,128]{1,0:T(8,128)S(1)}, u32[]{:S(2)}, u32[]{:S(2)}) %collective-permute-start.5) | collective-permute-done | bytes 53280 | tf_op jit(solution)/shard_map/ppermute | solution.py:498
  15.5 0.9 %finish.1 = (f32[4,64,128]{2,1,0:T(8,128)}, f32[4,4,8,10]{3,2,1,0:T(8,128)}) custom-call(f32[104,128]{1,0:T(8,128)S(1)} %get-tuple-element.22.refs_0_, f32[104,128]{1,0:T(8,128)S(1)} %collective-permute-done.3.refs_1_, f32[104,128]{1,0:T(8,128)S(1)} %collective-permute-done.4.refs_2_, f32[104,128]{1,0:T(8,128)S(1)} %collective-permute-done.5.refs_3_, ...), custom_call_target="tpu_custom_call" | custom-call | tf_op jit(solution)/shard_map/finish/pallas_call | solution.py:512
Async XLA Ops:
  0.6 4.3 %copy-start.4 = (s32[64,128]{1,0:T(8,128)S(1)}, s32[64,128]{1,0:T(8,128)}, u32[]{:S(2)}) copy-start(s32[64,128]{1,0:T(8,128)} %floor.5) | copy-start | bytes 98308
  0.6 4.2 %copy-start.3 = (s32[64,128]{1,0:T(8,128)S(1)}, s32[64,128]{1,0:T(8,128)}, u32[]{:S(2)}) copy-start(s32[64,128]{1,0:T(8,128)} %flag.5) | copy-start | bytes 98308
  0.7 4.2 %copy-start = (f32[10,4,64,128]{3,2,1,0:T(8,128)S(1)}, f32[10,4,64,128]{3,2,1,0:T(8,128)}, u32[]{:S(2)}) copy-start(f32[10,4,64,128]{3,2,1,0:T(8,128)} %warmth.5) | copy-start | bytes 3932164
  0.7 4.2 %copy-start.2 = (s32[64,128]{1,0:T(8,128)S(1)}, s32[64,128]{1,0:T(8,128)}, u32[]{:S(2)}) copy-start(s32[64,128]{1,0:T(8,128)} %refs_6_.1) | copy-start | bytes 98308
  0.7 4.2 %copy-start.1 = (f32[10,4,64,128]{3,2,1,0:T(8,128)S(1)}, f32[10,4,64,128]{3,2,1,0:T(8,128)}, u32[]{:S(2)}) copy-start(f32[10,4,64,128]{3,2,1,0:T(8,128)} %flow.3) | copy-start | bytes 3932164
  1.8 4.9 %collective-permute-start.1 = (f32[41,128]{1,0:T(8,128)S(1)}, f32[41,128]{1,0:T(8,128)S(1)}, u32[]{:S(2)}, u32[]{:S(2)}) collective-permute-start(f32[41,128]{1,0:T(8,128)S(1)} %edge.1), channel_id=1, source_target_pairs={{0,8},{1,9},{2,10},{3,11},{4,12},{5,13},{6,14},{7,15},{8,0},{9,1},... | collective-permute-start | bytes 62984 | tf_op jit(solution)/shard_map/ppermute | solution.py:449
  4.9 1.8 %collective-permute-start = (f32[41,128]{1,0:T(8,128)S(1)}, f32[41,128]{1,0:T(8,128)S(1)}, u32[]{:S(2)}, u32[]{:S(2)}) collective-permute-start(f32[41,128]{1,0:T(8,128)S(1)} %edge.1), channel_id=1, source_target_pairs={{0,1},{1,0},{2,3},{3,2},{4,5},{5,4},{6,7},{7,6},{8,17},{9,16},{10,... | collective-permute-start | bytes 62984 | tf_op jit(solution)/shard_map/ppermute | solution.py:449
  7.1 1.5 %collective-permute-start.2 = (f32[336,128]{1,0:T(8,128)S(1)}, f32[336,128]{1,0:T(8,128)S(1)}, u32[]{:S(2)}, u32[]{:S(2)}) collective-permute-start(f32[336,128]{1,0:T(8,128)S(1)} %get-tuple-element.21), channel_id=1, source_target_pairs={{0,1},{1,0},{2,3},{3,2},{4,5},{5,4},{6,7},{7,6},{8,9},{9,8},{10,11... | collective-permute-start | bytes 516104 | tf_op jit(solution)/shard_map/ppermute | solution.py:483
  8.6 3.7 %collective-permute-start.3 = (f32[104,128]{1,0:T(8,128)S(1)}, f32[104,128]{1,0:T(8,128)S(1)}, u32[]{:S(2)}, u32[]{:S(2)}) collective-permute-start(f32[104,128]{1,0:T(8,128)S(1)} %get-tuple-element.23), channel_id=1, source_target_pairs={{0,5},{1,4},{2,7},{3,6},{4,1},{5,0},{6,3},{7,2},{8,13},{9,12},{10,... | collective-permute-start | bytes 159752 | tf_op jit(solution)/shard_map/ppermute | solution.py:498
  10.3 4.5 %collective-permute-start.4 = (f32[104,128]{1,0:T(8,128)S(1)}, f32[104,128]{1,0:T(8,128)S(1)}, u32[]{:S(2)}, u32[]{:S(2)}) collective-permute-start(f32[104,128]{1,0:T(8,128)S(1)} %get-tuple-element.24), channel_id=1, source_target_pairs={{0,7},{1,6},{2,5},{3,4},{4,3},{5,2},{6,1},{7,0},{8,15},{9,14},{10,... | collective-permute-start | bytes 159752 | tf_op jit(solution)/shard_map/ppermute | solution.py:498
  11.7 3.8 %collective-permute-start.5 = (f32[104,128]{1,0:T(8,128)S(1)}, f32[104,128]{1,0:T(8,128)S(1)}, u32[]{:S(2)}, u32[]{:S(2)}) collective-permute-start(f32[104,128]{1,0:T(8,128)S(1)} %get-tuple-element.25), channel_id=1, source_target_pairs={{0,3},{1,2},{2,1},{3,0},{4,7},{5,6},{6,5},{7,4},{8,11},{9,10},{10,... | collective-permute-start | bytes 159752 | tf_op jit(solution)/shard_map/ppermute | solution.py:498
